TPU v7x, 32 devices: a whole 2x2x4 slice. The times are simulated.
32 devices in a mesh: gx: 4 (over x, core), gy: 2 (over y), gz: 4 (over z).
Axes of the slice: x: 2, y: 2, z: 4, core: 2. Of those that a mesh axis runs over, the one named last changes fastest.
Arguments:
- start_field: float32 [256, 128, 1024], P('gx', 'gy', 'gz'), may hold values from -6 to 6
- right_side: float32 [256, 128, 1024], P('gx', 'gy', 'gz'), may hold values from -6 to 6
Outputs:
- corrected: float32 [256, 128, 1024], P('gx', 'gy', 'gz')
All inputs are finite; a program needn't handle non-finite values.
Results may differ from a plain program's by a relative error of at most 0.00002.
Values sent between devices are 32-bit elements; how exact they have to be, the bound alone decides.
No kernel may reach another device: no remote copies, remote signals or barrier semaphores. Data moves between devices by JAX's collectives and lax.ppermute only.
A program may use at most 128 MiB of HBM per device.

v0:
```python
import functools

import jax
import jax.numpy as jnp
from jax import lax
from jax.experimental import pallas as pl
from jax.experimental.pallas import tpu as pltpu
from jax.sharding import PartitionSpec as P

LANES = 128
F = 3
G = 2
SLOT = F + G
PER = LANES // SLOT
CL = 4
CH = 3
CPER = LANES // CL

VMEM = pl.BlockSpec(memory_space=pltpu.VMEM)
ANY = pl.BlockSpec(memory_space=pl.ANY)


def f32(*shape):
    return jax.ShapeDtypeStruct(shape, jnp.float32)


def call(body, name, ins, outs, scratch=(), alias=None, limit=None, out_specs=None):
    return pl.pallas_call(
        body,
        name=name,
        in_specs=[VMEM] * len(ins),
        out_specs=[VMEM] * len(outs) if out_specs is None else out_specs,
        out_shape=outs,
        scratch_shapes=list(scratch),
        input_output_aliases=alias or {},
        compiler_params=pltpu.CompilerParams(vmem_limit_bytes=limit),
    )(*ins)


def iota(shape, dim):
    return lax.broadcasted_iota(jnp.int32, shape, dim)


def ends(axis):
    i = lax.axis_index(axis)
    return i == 0, i == lax.axis_size(axis) - 1


def exchange(msgs, axis):
    n = lax.axis_size(axis)
    if n == 2:
        return [lax.ppermute(msgs[0], axis, [(0, 1), (1, 0)])]
    down = lax.ppermute(msgs[0], axis, [(i + 1, i) for i in range(n - 1)])
    up = lax.ppermute(msgs[1], axis, [(i, i + 1) for i in range(n - 1)])
    return [down, up]


def emit(outs, index, axis, low, high):
    if len(outs) == 1:
        outs[0][index] = jnp.where(ends(axis)[0], high(), low())
    else:
        outs[0][index] = low()
        outs[1][index] = high()


def arrived(refs, index, axis):
    if len(refs) == 1:
        value = refs[0][index]
        first = ends(axis)[0]
        zero = jnp.zeros_like(value)
        return jnp.where(first, value, zero), jnp.where(first, zero, value)
    return refs[0][index], refs[1][index]


def count(axis):
    return 1 if lax.axis_size(axis) == 2 else 2


def build_body(start, right, se, re):
    nx, ny, nz = start.shape

    def plane(p, _):
        for t in range(nz // LANES):
            se[t, p, 0:ny, :] = start[p, :, t * LANES:(t + 1) * LANES]
            re[t, p, 0:ny, :] = right[p, :, t * LANES:(t + 1) * LANES]
        return 0

    lax.fori_loop(0, nx, plane, 0, unroll=2)


def xhalo_body(nx, ny, nz, nin, *refs):
    halo = refs[:nin]
    se, re, outs = refs[nin + 2], refs[nin + 3], refs[nin + 4:]
    xe, ye = nx + 8, ny + 8
    nt = nz // LANES
    for t in range(nt):
        cut = slice(t * LANES, (t + 1) * LANES)
        for k in range(SLOT):
            high, low = arrived(halo, (k, slice(None), cut), "gx")
            dst, size, j = (se, F, k) if k < F else (re, G, k - F)
            dst[t, nx + j, 0:ny, :] = high
            dst[t, xe - size + j, 0:ny, :] = low
    se2 = se.reshape(nt + 1, xe * ye, LANES)
    re2 = re.reshape(nt + 1, xe * ye, LANES)
    for t in range(nt):
        for k in range(SLOT):
            src, size, j = (se2, F, k) if k < F else (re2, G, k - F)
            emit(
                outs, (k * nt + t,), "gy",
                lambda: src[t, pl.ds(j, xe, stride=ye), :],
                lambda: src[t, pl.ds(ny - size + j, xe, stride=ye), :],
            )


def yhalo_body(nx, ny, nz, nin, *refs):
    halo = refs[:nin]
    se, re, outs = refs[nin + 2], refs[nin + 3], refs[nin + 4:]
    xe, ye = nx + 8, ny + 8
    nt = nz // LANES
    se2 = se.reshape(nt + 1, xe * ye, LANES)
    re2 = re.reshape(nt + 1, xe * ye, LANES)
    for t in range(nt):
        for k in range(SLOT):
            high, low = arrived(halo, (k * nt + t,), "gy")
            dst, size, j = (se2, F, k) if k < F else (re2, G, k - F)
            dst[t, pl.ds(ny + j, xe, stride=ye), :] = high
            dst[t, pl.ds(ye - size + j, xe, stride=ye), :] = low
    lane = iota((ye, LANES), 1)

    def tile(group, _):
        low = jnp.zeros((ye, LANES), jnp.float32)
        high = jnp.zeros((ye, LANES), jnp.float32)
        for j in range(PER):
            p = jnp.minimum(group * PER + j, xe - 1)
            at = j * SLOT
            in_s = (lane >= at) & (lane < at + F)
            in_r = (lane >= at + F) & (lane < at + SLOT)
            low = jnp.where(in_s, pltpu.roll(se[0, p], at, 1), low)
            low = jnp.where(in_r, pltpu.roll(re[0, p], at + F, 1), low)
            high = jnp.where(in_s, pltpu.roll(se[nt - 1, p], (at + F) % LANES, 1), high)
            high = jnp.where(in_r, pltpu.roll(re[nt - 1, p], (at + SLOT) % LANES, 1), high)
        emit(outs, (group,), "gz", lambda: low, lambda: high)
        return 0

    lax.fori_loop(0, -(-xe // PER), tile, 0)


def neighbours(ref, q, before, after, tiles):
    total = ref.shape[0]
    rows = ref.shape[2]
    lane = iota((rows, LANES), 1)
    centre = [ref[t, q] for t in range(total)]
    left = [pltpu.roll(c, 1, 1) for c in centre]
    right = [pltpu.roll(c, LANES - 1, 1) for c in centre]
    found = []
    for t in range(tiles):
        c = centre[t]
        near = jnp.where(lane == 0, left[t - 1], left[t])
        near = near + jnp.where(lane == LANES - 1, right[(t + 1) % total], right[t])
        near = near + (pltpu.roll(c, 1, 0) + pltpu.roll(c, rows - 1, 0))
        near = near + (ref[t, before] + ref[t, after])
        found.append((c, near))
    return found


def wrap(q, size):
    return jnp.where(q < 0, q + size, jnp.where(q >= size, q - size, q))


def inside(shape, dim, cells, low, high, axis):
    first, last = ends(axis)
    at = iota(shape, dim)
    size = shape[dim]
    up = jnp.where(last, 0.0, 1.0)
    down = jnp.where(first, 0.0, 1.0)
    return jnp.where(at < cells, 1.0, jnp.where(at < cells + high, up, jnp.where(at >= size - low, down, 0.0)))


def split_dot(value, weight):
    high = value.astype(jnp.bfloat16)
    rest = value - high.astype(jnp.float32)
    mid = rest.astype(jnp.bfloat16)
    small = (rest - mid.astype(jnp.float32)).astype(jnp.bfloat16)
    dot = functools.partial(jnp.dot, preferred_element_type=jnp.float32)
    return dot(high, weight) + dot(mid, weight) + dot(small, weight)


def smooth_body(nx, ny, nz, nin, *refs):
    halo = refs[:nin]
    se, re, s2, coarse = refs[nin + 2:nin + 6]
    outs = refs[nin + 6:-4]
    s1, rx, rz, mask = refs[-4:]
    xe, ye = nx + 8, ny + 8
    nt = nz // LANES
    lane = iota((ye, LANES), 1)

    def unpack(group, _):
        high, low = arrived(halo, (group,), "gz")
        for j in range(PER):
            p = jnp.minimum(group * PER + j, xe - 1)
            at = j * SLOT

            @pl.when(group * PER + j < xe)
            def _():
                se[nt, p] = jnp.where(
                    lane < 64, pltpu.roll(high, (-at) % LANES, 1), pltpu.roll(low, (-F - at) % LANES, 1)
                )
                re[nt, p] = jnp.where(
                    lane < 64, pltpu.roll(high, (-at - F) % LANES, 1), pltpu.roll(low, (-G - at - F) % LANES, 1)
                )
        return 0

    lax.fori_loop(0, -(-xe // PER), unpack, 0)

    valid = inside((ye, LANES), 0, ny, F, F, "gy")
    for t in range(nt):
        mask[t] = valid * (1.0 / 7.0)
    mask[nt] = valid * inside((ye, LANES), 1, 0, F, F, "gz") * (1.0 / 7.0)

    first, last = ends("gx")
    up = jnp.where(last, 0.0, 1.0)
    down = jnp.where(first, 0.0, 1.0)

    def sweep(src, dst, reach):
        def plane(q, factor):
            found = neighbours(src, q, wrap(q - 1, xe), wrap(q + 1, xe), nt + 1)
            for t, (c, near) in enumerate(found):
                m = mask[t] if factor is None else mask[t] * factor
                dst[t, q] = m * (near + (c + re[t, q]))

        def inner(q, _):
            plane(q, None)
            return 0

        lax.fori_loop(0, nx, inner, 0)

        def outer(k, _):
            plane(jnp.where(k < reach, nx + k, xe - 2 * reach + k), jnp.where(k < reach, up, down))
            return 0

        lax.fori_loop(0, 2 * reach, outer, 0)

    sweep(se, s1, 2)
    sweep(s1, s2, 1)

    def residual(q):
        found = neighbours(s2, q, wrap(q - 1, xe), wrap(q + 1, xe), nt)
        return [(re[t, q] + (near - 6.0 * c))[0:ny] for t, (c, near) in enumerate(found)]

    for t in range(nt):
        rx[0:ny, t * LANES:(t + 1) * LANES] = jnp.zeros((ny, LANES), jnp.float32)

    def pair(i, _):
        even = residual(2 * i)
        at = pl.multiple_of(i * ny, 8)
        for t in range(nt):
            cut = slice(t * LANES, (t + 1) * LANES)
            rx[pl.ds(at, ny), cut] = rx[pl.ds(at, ny), cut] + 0.25 * even[t]
        odd = residual(2 * i + 1)
        for t in range(nt):
            cut = slice(t * LANES, (t + 1) * LANES)
            rx[pl.ds(at + ny, ny), cut] = 0.25 * even[t] + 0.5 * odd[t]
        return 0

    lax.fori_loop(0, nx // 2, pair, 0)

    cz = nz // 2
    ct = cz // LANES
    wide = (ct + 1) * LANES
    z = iota((nz, wide), 0)
    k = iota((nz, wide), 1)
    k = jnp.where(k >= cz, k - wide, k)
    off = z - 2 * k
    weight = jnp.where((off == 0) | (off == 2), 0.25, jnp.where(off == 1, 0.5, 0.0))
    weight = jnp.where(k < -1, 0.0, weight).astype(jnp.bfloat16)

    def zpart(i, _):
        at = pl.multiple_of(i * ny, 8)
        got = split_dot(rx[pl.ds(at, ny), :], weight)
        for t in range(ct + 1):
            rz[t, pl.ds(at, ny), :] = got[:, t * LANES:(t + 1) * LANES]
        return 0

    cx, cy = nx // 2, ny // 2
    lax.fori_loop(0, cx + 1, zpart, 0, unroll=3)

    row = iota((cy, LANES), 0)
    row8 = iota((8, LANES), 0)

    def ypart(i, _):
        q = jnp.where(i == 0, cx + 7, i - 1)
        for t in range(ct + 1):
            even = rz[t, pl.ds(i * ny, cy, stride=2), :]
            odd = rz[t, pl.ds(i * ny + 1, cy, stride=2), :]
            after = rz[t, pl.ds(i * ny + 2, cy, stride=2), :]
            after = jnp.where(row == cy - 1, 0.0, after)
            coarse[t, q, 0:cy, :] = 0.25 * even + 0.5 * odd + 0.25 * after
            coarse[t, q, cy:cy + 8, :] = jnp.where(row8 == 7, 0.25 * even[0:1], 0.0)
        return 0

    rz[:, (cx + 1) * ny:(cx + 1) * ny + 8, :] = jnp.zeros((ct + 1, 8, LANES), jnp.float32)
    lax.fori_loop(0, cx + 1, ypart, 0)
    for q in range(cx, cx + 7):
        for t in range(ct + 1):
            coarse[t, q] = jnp.zeros((cy + 8, LANES), jnp.float32)

    def layer(t, q):
        return coarse[t, q]

    faces(outs, "gx", lambda t, j: coarse[t, (cx + 7 + j) % (cx + 8)], lambda t, j: coarse[t, cx - CL + j], ct)


def faces(outs, axis, low, high, ct):
    extra_low = extra_high = None
    for j in range(CL):
        for t in range(ct):
            emit(outs, (j * ct + t,), axis, lambda: low(t, j), lambda: high(t, j))
        a = pltpu.roll(low(ct, j), (j + 1) % LANES, 1)
        b = pltpu.roll(high(ct, j), (j + 1) % LANES, 1)
        lane = iota(a.shape, 1)
        extra_low = a if j == 0 else jnp.where(lane == j, a, extra_low)
        extra_high = b if j == 0 else jnp.where(lane == j, b, extra_high)
    emit(outs, (CL * ct,), axis, lambda: extra_low, lambda: extra_high)


def place_faces(refs, axis, ct, size, read, write):
    for t in range(ct + 1):
        for j in range(CL):
            if t < ct:
                high, low = arrived(refs, (j * ct + t,), axis)
            else:
                high, low = arrived(refs, (CL * ct,), axis)
                lane = iota(high.shape, 1)
                turn = (LANES - 1 - j) % LANES
                high = jnp.where(lane == LANES - 1, pltpu.roll(high, turn, 1), 0.0)
                low = jnp.where(lane == LANES - 1, pltpu.roll(low, turn, 1), 0.0)
            if j == 0:
                write(t, size - 1, read(t, size - 1) + high)
            else:
                write(t, size + j - 1, high)
            if j == CL - 1:
                write(t, size + 7, read(t, size + 7) + low)
            else:
                write(t, size + 4 + j, low)


def coarse_x_body(cx, cy, cz, nin, *refs):
    halo = refs[:nin]
    coarse, outs = refs[nin + 1], refs[nin + 2:]
    ct = cz // LANES
    xe, ye = cx + 8, cy + 8

    def write(t, q, value):
        coarse[t, q] = value

    place_faces(halo, "gx", ct, cx, lambda t, q: coarse[t, q], write)
    flat = coarse.reshape(ct + 1, xe * ye, LANES)
    faces(
        outs, "gy",
        lambda t, j: flat[t, pl.ds((cy + 7 + j) % ye, xe, stride=ye), :],
        lambda t, j: flat[t, pl.ds(cy - CL + j, xe, stride=ye), :],
        ct,
    )


def coarse_y_body(cx, cy, cz, nin, *refs):
    halo = refs[:nin]
    coarse, outs = refs[nin + 1], refs[nin + 2:]
    ct = cz // LANES
    xe, ye = cx + 8, cy + 8
    flat = coarse.reshape(ct + 1, xe * ye, LANES)

    def write(t, q, value):
        flat[t, pl.ds(q, xe, stride=ye), :] = value

    place_faces(halo, "gy", ct, cy, lambda t, q: flat[t, pl.ds(q, xe, stride=ye), :], write)
    lane = iota((ye, LANES), 1)

    def tile(group, _):
        low = jnp.zeros((ye, LANES), jnp.float32)
        high = jnp.zeros((ye, LANES), jnp.float32)
        for j in range(CPER):
            p = jnp.minimum(group * CPER + j, xe - 1)
            at = j * CL
            head = jnp.where(lane < CL - 1, coarse[0, p], coarse[ct, p])
            head = pltpu.roll(head, (at + 1) % LANES, 1)
            here = (lane >= at) & (lane < at + CL)
            low = jnp.where(here, head, low)
            high = jnp.where(here, pltpu.roll(coarse[ct - 1, p], (at + CL) % LANES, 1), high)
        emit(outs, (group,), "gz", lambda: low, lambda: high)
        return 0

    lax.fori_loop(0, -(-xe // CPER), tile, 0)


def finish_body(cx, cy, cz, nin, *refs):
    halo = refs[:nin]
    smooth, _, coarse, out = refs[nin:nin + 4]
    ca, cb, mask, fine, stage, sems = refs[nin + 4:]
    ct = cz // LANES
    xe, ye = cx + 8, cy + 8
    nx, ny, nz = 2 * cx, 2 * cy, 2 * cz
    nt = nz // LANES
    lane = iota((ye, LANES), 1)
    first, last = ends("gx")
    up = jnp.where(last, 0.0, 1.0)
    down = jnp.where(first, 0.0, 1.0)

    valid = inside((ye, LANES), 0, cy, CL, CH, "gy")
    for t in range(ct):
        mask[t] = valid * (1.0 / 7.0)
    mask[ct] = valid * inside((ye, LANES), 1, 0, CL, CH, "gz") * (1.0 / 7.0)

    def unpack(group, _):
        high, low = arrived(halo, (group,), "gz")
        for j in range(CPER):
            p = group * CPER + j
            at = j * CL

            @pl.when(p < xe)
            def _():
                q = jnp.minimum(p, xe - 1)
                fromhigh = pltpu.roll(high, (-at - 1) % LANES, 1)
                fromlow = pltpu.roll(low, (-CL - at) % LANES, 1)
                tail = coarse[ct - 1, q]
                tail = tail + jnp.where(lane == LANES - 1, fromhigh, 0.0)
                wing = jnp.where(lane < CH, fromhigh, jnp.where(lane >= LANES - CL, fromlow, 0.0))
                wing = wing + jnp.where(lane == LANES - 1, coarse[ct, q], 0.0)
                xm = jnp.where(p < cx, 1.0, jnp.where(p < cx + CL, up, down))
                coarse[ct - 1, q] = 4.0 * tail
                coarse[ct, q] = 4.0 * wing
                for t in range(ct - 1):
                    coarse[t, q] = 4.0 * coarse[t, q]
                for t in range(ct + 1):
                    ca[t, q] = (mask[t] * xm) * coarse[t, q]
        return 0

    lax.fori_loop(0, -(-xe // CPER), unpack, 0)

    def sweep(src, dst, low, high):
        def step(k, _):
            p = k - low
            q = wrap(p, xe)
            xm = jnp.where(p < 0, down, jnp.where(p >= cx, up, 1.0))
            found = neighbours(src, q, wrap(p - 1, xe), wrap(p + 1, xe), ct + 1)
            for t, (c, near) in enumerate(found):
                dst[t, q] = (mask[t] * xm) * (near + (c + coarse[t, q]))
            return 0

        lax.fori_loop(0, cx + low + high, step, 0)

    sweep(ca, cb, 3, 2)
    sweep(cb, ca, 2, 1)
    sweep(ca, cb, 1, 0)

    wide = (ct + 1) * LANES
    k = iota((wide, nz), 0)
    z = iota((wide, nz), 1)
    k = jnp.where(k >= cz, k - wide, k)
    off = z - 2 * k
    weight = jnp.where(off == 1, 1.0, jnp.where((off == 0) | (off == 2), 0.5, 0.0))
    weight = jnp.where(k < -1, 0.0, weight).astype(jnp.bfloat16)

    def prolong(i, _):
        q = jnp.where(i == 0, xe - 1, i - 1)
        value = jnp.concatenate([cb[t, q] for t in range(ct + 1)], axis=1)
        got = split_dot(value, weight)
        even = 0.5 * (got + pltpu.roll(got, 1, 0))
        for t in range(nt):
            cut = slice(t * LANES, (t + 1) * LANES)
            fine[t, pl.ds(i * ny, cy, stride=2), :] = even[0:cy, cut]
            fine[t, pl.ds(i * ny + 1, cy, stride=2), :] = got[0:cy, cut]
        return 0

    lax.fori_loop(0, cx + 1, prolong, 0, unroll=3)

    chunks = sems.shape[0]
    per = cx // chunks

    def send(c):
        at = c * 2 * per
        return pltpu.make_async_copy(stage.at[pl.ds(at, 2 * per)], out.at[pl.ds(at, 2 * per)], sems.at[c])

    for c in range(chunks):
        def add(i, _):
            at = pl.multiple_of(i * ny, 8)
            for t in range(nt):
                cut = slice(t * LANES, (t + 1) * LANES)
                here = fine[t, pl.ds(at + ny, ny), :]
                before = fine[t, pl.ds(at, ny), :]
                stage[2 * i, :, cut] = smooth[t, 2 * i, 0:ny, :] + 0.5 * (before + here)
                stage[2 * i + 1, :, cut] = smooth[t, 2 * i + 1, 0:ny, :] + here
            return 0

        lax.fori_loop(c * per, (c + 1) * per, add, 0)
        send(c).start()
    for c in range(chunks):
        send(c).wait()


def on_device(start, right):
    nx, ny, nz = start.shape
    nt = nz // LANES
    xe, ye = nx + 8, ny + 8
    cx, cy, cz = nx // 2, ny // 2, nz // 2
    ct = cz // LANES
    cxe, cye = cx + 8, cy + 8
    big = f32(nt + 1, xe, ye, LANES)
    mb = 1 << 20

    to_prev = jnp.concatenate([start[:F], right[:G]], axis=0)
    to_next = jnp.concatenate([start[nx - F:], right[nx - G:]], axis=0)
    if count("gx") == 1:
        to_prev = jnp.where(ends("gx")[0], to_next, to_prev)
    halo = exchange([to_prev, to_next], "gx")
    se, re = call(build_body, "build", [start, right], [big, big], limit=8 * mb)

    n = len(halo)
    se, re, *msgs = call(
        functools.partial(xhalo_body, nx, ny, nz, n), "xhalo", [*halo, se, re],
        [big, big] + [f32(SLOT * nt, xe, LANES)] * count("gy"), alias={n: 0, n + 1: 1}, limit=8 * mb,
    )
    halo = exchange(msgs, "gy")
    n = len(halo)
    se, re, *msgs = call(
        functools.partial(yhalo_body, nx, ny, nz, n), "yhalo", [*halo, se, re],
        [big, big] + [f32(-(-xe // PER), ye, LANES)] * count("gz"), alias={n: 0, n + 1: 1}, limit=8 * mb,
    )
    halo = exchange(msgs, "gz")
    n = len(halo)
    small = f32(ct + 1, cxe, cye, LANES)
    se, re, s2, coarse, *msgs = call(
        functools.partial(smooth_body, nx, ny, nz, n), "smooth", [*halo, se, re],
        [big, big, big, small] + [f32(CL * ct + 1, cye, LANES)] * count("gx"),
        scratch=[
            pltpu.VMEM((nt + 1, xe, ye, LANES), jnp.float32),
            pltpu.VMEM(((cx + 1) * ny, nz), jnp.float32),
            pltpu.VMEM((ct + 1, (cx + 1) * ny + 8, LANES), jnp.float32),
            pltpu.VMEM((nt + 1, ye, LANES), jnp.float32),
        ],
        alias={n: 0, n + 1: 1}, limit=24 * mb,
    )
    halo = exchange(msgs, "gx")
    n = len(halo)
    coarse, *msgs = call(
        functools.partial(coarse_x_body, cx, cy, cz, n), "coarse_x", [*halo, coarse],
        [small] + [f32(CL * ct + 1, cxe, LANES)] * count("gy"), alias={n: 0}, limit=8 * mb,
    )
    halo = exchange(msgs, "gy")
    n = len(halo)
    coarse, *msgs = call(
        functools.partial(coarse_y_body, cx, cy, cz, n), "coarse_y", [*halo, coarse],
        [small] + [f32(-(-cxe // CPER), cye, LANES)] * count("gz"), alias={n: 0}, limit=8 * mb,
    )
    halo = exchange(msgs, "gz")
    n = len(halo)
    _, out = call(
        functools.partial(finish_body, cx, cy, cz, n), "finish", [*halo, s2, coarse],
        [small, f32(nx, ny, nz)],
        scratch=[
            pltpu.VMEM((ct + 1, cxe, cye, LANES), jnp.float32),
            pltpu.VMEM((ct + 1, cxe, cye, LANES), jnp.float32),
            pltpu.VMEM((ct + 1, cye, LANES), jnp.float32),
            pltpu.VMEM((nt, (cx + 1) * ny, LANES), jnp.float32),
            pltpu.VMEM((nx, ny, nz), jnp.float32),
            pltpu.SemaphoreType.DMA((8,)),
        ],
        alias={n + 1: 0}, limit=24 * mb, out_specs=[VMEM, ANY],
    )
    return out


def solution(mesh):
    spec = P("gx", "gy", "gz")
    return jax.shard_map(on_device, mesh=mesh, in_specs=(spec, spec), out_specs=spec, check_vma=False)
```

profile of v0, /device:TPU:16, one launch (start us, length us, event | category | flops | bytes accessed | tf_op | source)
XLA Modules:
  0.0 112.4 jit_solution(1527914557275185628)
XLA Ops:
  0.0 1.0 fusion.1
  1.0 1.1 fusion
  2.1 1.3 %collective-permute-start = (f32[5,64,256]{2,1,0:T(8,128)S(1)}, f32[5,64,256]{2,1,0:T(8,128)S(1)}, u32[]{:S(2)}, u32[]{:S(2)}) collective-permute-start(f32[5,64,256]{2,1,0:T(8,128)S(1)} %pad_maximum_fusion), channel_id=1, source_target_pairs={{8,0},{16,8},{24,16},{9,1},{17,9},{25,17},{10,2},{18,10},{26,18},{... | collective-permute-start | bytes 983048 | tf_op jit(solution)/shard_map/ppermute | solution.py:53
  3.4 3.1 %collective-permute-start.1 = (f32[5,64,256]{2,1,0:T(8,128)S(1)}, f32[5,64,256]{2,1,0:T(8,128)S(1)}, u32[]{:S(2)}, u32[]{:S(2)}) collective-permute-start(f32[5,64,256]{2,1,0:T(8,128)S(1)} %pad_maximum_fusion.1), channel_id=1, source_target_pairs={{0,8},{8,16},{16,24},{1,9},{9,17},{17,25},{2,10},{10,18},{18,26},{... | collective-permute-start | bytes 983048 | tf_op jit(solution)/shard_map/ppermute | solution.py:54
  6.5 0.0 copy-start
  6.5 2.2 %copy-done = f32[64,64,256]{2,1,0:T(8,128)S(1)} copy-done((f32[64,64,256]{2,1,0:T(8,128)S(1)}, f32[64,64,256]{2,1,0:T(8,128)}, u32[]{:S(2)}) %copy-start) | copy-done | bytes 4194328
  8.7 0.0 copy-start.1
  8.7 2.2 %copy-done.1 = f32[64,64,256]{2,1,0:T(8,128)S(1)} copy-done((f32[64,64,256]{2,1,0:T(8,128)S(1)}, f32[64,64,256]{2,1,0:T(8,128)}, u32[]{:S(2)}) %copy-start.1) | copy-done | bytes 4194328
  10.8 0.6 build.1
  11.4 0.0 collective-permute-done.refs_0_
  11.4 0.0 collective-permute-done.1.refs_1_
  11.5 0.2 xhalo.1
  11.6 1.6 %collective-permute-start.2 = (f32[10,72,128]{2,1,0:T(8,128)S(1)}, f32[10,72,128]{2,1,0:T(8,128)S(1)}, u32[]{:S(2)}, u32[]{:S(2)}) collective-permute-start(f32[10,72,128]{2,1,0:T(8,128)S(1)} %get-tuple-element.26), channel_id=1, source_target_pairs={{0,4},{4,0},{1,5},{5,1},{2,6},{6,2},{3,7},{7,3},{8,12},{12,8},{9,1... | collective-permute-start | bytes 1105928 | tf_op jit(solution)/shard_map/ppermute | solution.py:52
  13.2 9.8 %collective-permute-done.2.refs_0_ = f32[10,72,128]{2,1,0:T(8,128)S(1)} collective-permute-done((f32[10,72,128]{2,1,0:T(8,128)S(1)}, f32[10,72,128]{2,1,0:T(8,128)S(1)}, u32[]{:S(2)}, u32[]{:S(2)}) %collective-permute-start.2) | collective-permute-done | bytes 368672 | tf_op jit(solution)/shard_map/ppermute | solution.py:52
  23.0 3.4 %yhalo.1 = (f32[3,72,72,128]{3,2,1,0:T(8,128)S(1)}, f32[3,72,72,128]{3,2,1,0:T(8,128)S(1)}, f32[3,72,128]{2,1,0:T(8,128)S(1)}, f32[3,72,128]{2,1,0:T(8,128)S(1)}) custom-call(f32[10,72,128]{2,1,0:T(8,128)S(1)} %collective-permute-done.2.refs_0_, f32[3,72,72,128]{3,2,1,0:T(8,128)S(1)} %get-tuple-element.27.refs_1_, ...), custom_call_target="tpu_custom_call", output_to_operand_aliasing={{0}: (1, {}), {1}: (2, {})} | custom-call | tf_op jit(solution)/shard_map/yhalo/pallas_call | solution.py:28
  26.4 2.4 %collective-permute-start.3 = (f32[3,72,128]{2,1,0:T(8,128)S(1)}, f32[3,72,128]{2,1,0:T(8,128)S(1)}, u32[]{:S(2)}, u32[]{:S(2)}) collective-permute-start(f32[3,72,128]{2,1,0:T(8,128)S(1)} %get-tuple-element.29), channel_id=1, source_target_pairs={{1,0},{2,1},{3,2},{5,4},{6,5},{7,6},{9,8},{10,9},{11,10},{13,12},{... | collective-permute-start | bytes 331784 | tf_op jit(solution)/shard_map/ppermute | solution.py:53
  28.8 3.5 %collective-permute-start.4 = (f32[3,72,128]{2,1,0:T(8,128)S(1)}, f32[3,72,128]{2,1,0:T(8,128)S(1)}, u32[]{:S(2)}, u32[]{:S(2)}) collective-permute-start(f32[3,72,128]{2,1,0:T(8,128)S(1)} %get-tuple-element.30), channel_id=1, source_target_pairs={{0,1},{1,2},{2,3},{4,5},{5,6},{6,7},{8,9},{9,10},{10,11},{12,13},{... | collective-permute-start | bytes 331784 | tf_op jit(solution)/shard_map/ppermute | solution.py:54
  32.3 1.1 collective-permute-done.3.refs_0_
  33.4 2.1 %collective-permute-done.4.refs_1_ = f32[3,72,128]{2,1,0:T(8,128)S(1)} collective-permute-done((f32[3,72,128]{2,1,0:T(8,128)S(1)}, f32[3,72,128]{2,1,0:T(8,128)S(1)}, u32[]{:S(2)}, u32[]{:S(2)}) %collective-permute-start.4) | collective-permute-done | bytes 110624 | tf_op jit(solution)/shard_map/ppermute | solution.py:54
  35.5 37.4 %smooth.1 = (f32[3,72,72,128]{3,2,1,0:T(8,128)S(1)}, f32[3,72,72,128]{3,2,1,0:T(8,128)S(1)}, f32[3,72,72,128]{3,2,1,0:T(8,128)S(1)}, f32[2,40,40,128]{3,2,1,0:T(...) custom-call(f32[3,72,128]{2,1,0:T(8,128)S(1)} %collective-permute-do, ...), custom_call_target="tpu_custom_call", output_to_operand_aliasing={{0}: (2, {}), {1}: (3, {})} | custom-call | tf_op jit(solution)/shard_map/smooth/pallas_call | solution.py:28
  72.9 1.3 %collective-permute-start.5 = (f32[5,40,128]{2,1,0:T(8,128)S(1)}, f32[5,40,128]{2,1,0:T(8,128)S(1)}, u32[]{:S(2)}, u32[]{:S(2)}) collective-permute-start(f32[5,40,128]{2,1,0:T(8,128)S(1)} %get-tuple-element.33), channel_id=1, source_target_pairs={{8,0},{16,8},{24,16},{9,1},{17,9},{25,17},{10,2},{18,10},{26,18},{... | collective-permute-start | bytes 307208 | tf_op jit(solution)/shard_map/ppermute | solution.py:53
  74.2 3.0 %collective-permute-start.6 = (f32[5,40,128]{2,1,0:T(8,128)S(1)}, f32[5,40,128]{2,1,0:T(8,128)S(1)}, u32[]{:S(2)}, u32[]{:S(2)}) collective-permute-start(f32[5,40,128]{2,1,0:T(8,128)S(1)} %get-tuple-element.34), channel_id=1, source_target_pairs={{0,8},{8,16},{16,24},{1,9},{9,17},{17,25},{2,10},{10,18},{18,26},{... | collective-permute-start | bytes 307208 | tf_op jit(solution)/shard_map/ppermute | solution.py:54
  77.2 0.0 collective-permute-done.5.refs_0_
  77.2 0.9 collective-permute-done.6.refs_1_
  78.1 0.2 coarse_x.1
  78.3 1.6 %collective-permute-start.7 = (f32[5,40,128]{2,1,0:T(8,128)S(1)}, f32[5,40,128]{2,1,0:T(8,128)S(1)}, u32[]{:S(2)}, u32[]{:S(2)}) collective-permute-start(f32[5,40,128]{2,1,0:T(8,128)S(1)} %get-tuple-element.36), channel_id=1, source_target_pairs={{0,4},{4,0},{1,5},{5,1},{2,6},{6,2},{3,7},{7,3},{8,12},{12,8},{9,1... | collective-permute-start | bytes 307208 | tf_op jit(solution)/shard_map/ppermute | solution.py:52
  79.9 4.2 %collective-permute-done.7.refs_0_ = f32[5,40,128]{2,1,0:T(8,128)S(1)} collective-permute-done((f32[5,40,128]{2,1,0:T(8,128)S(1)}, f32[5,40,128]{2,1,0:T(8,128)S(1)}, u32[]{:S(2)}, u32[]{:S(2)}) %collective-permute-start.7) | collective-permute-done | bytes 102432 | tf_op jit(solution)/shard_map/ppermute | solution.py:52
  84.1 1.0 coarse_y.1
  85.1 2.0 %collective-permute-start.8 = (f32[2,40,128]{2,1,0:T(8,128)S(1)}, f32[2,40,128]{2,1,0:T(8,128)S(1)}, u32[]{:S(2)}, u32[]{:S(2)}) collective-permute-start(f32[2,40,128]{2,1,0:T(8,128)S(1)} %get-tuple-element.38), channel_id=1, source_target_pairs={{1,0},{2,1},{3,2},{5,4},{6,5},{7,6},{9,8},{10,9},{11,10},{13,12},{... | collective-permute-start | bytes 122888 | tf_op jit(solution)/shard_map/ppermute | solution.py:53
  87.1 3.9 %collective-permute-start.9 = (f32[2,40,128]{2,1,0:T(8,128)S(1)}, f32[2,40,128]{2,1,0:T(8,128)S(1)}, u32[]{:S(2)}, u32[]{:S(2)}) collective-permute-start(f32[2,40,128]{2,1,0:T(8,128)S(1)} %get-tuple-element.39), channel_id=1, source_target_pairs={{0,1},{1,2},{2,3},{4,5},{5,6},{6,7},{8,9},{9,10},{10,11},{12,13},{... | collective-permute-start | bytes 122888 | tf_op jit(solution)/shard_map/ppermute | solution.py:54
  91.0 0.0 collective-permute-done.8.refs_0_
  91.0 2.0 %collective-permute-done.9.refs_1_ = f32[2,40,128]{2,1,0:T(8,128)S(1)} collective-permute-done((f32[2,40,128]{2,1,0:T(8,128)S(1)}, f32[2,40,128]{2,1,0:T(8,128)S(1)}, u32[]{:S(2)}, u32[]{:S(2)}) %collective-permute-start.9) | collective-permute-done | bytes 40992 | tf_op jit(solution)/shard_map/ppermute | solution.py:54
  93.0 19.5 %finish.1 = (f32[2,40,40,128]{3,2,1,0:T(8,128)S(1)}, f32[64,64,256]{2,1,0:T(8,128)}) custom-call(f32[2,40,128]{2,1,0:T(8,128)S(1)} %collective-permute-done.8.refs_0_, f32[2,40,128]{2,1,0:T(8,128)S(1)} %collective-permute-done.9.refs_1_, f32[3,72,72,128]{3,2,1,0:T(8,128)S(1)} %get-tuple-element.40.refs_2_, ...), custom_call_target="tpu_custom_call", output_to_operand_aliasing={{0}: (3, {})} | custom-call | tf_op jit(solution)/shard_map/finish/pallas_call | solution.py:28
  (2 shorter events, 0.0 us)
Async XLA Ops:
  2.1 9.4 %collective-permute-start = (f32[5,64,256]{2,1,0:T(8,128)S(1)}, f32[5,64,256]{2,1,0:T(8,128)S(1)}, u32[]{:S(2)}, u32[]{:S(2)}) collective-permute-start(f32[5,64,256]{2,1,0:T(8,128)S(1)} %pad_maximum_fusion), channel_id=1, source_target_pairs={{8,0},{16,8},{24,16},{9,1},{17,9},{25,17},{10,2},{18,10},{26,18},{... | collective-permute-start | bytes 983048 | tf_op jit(solution)/shard_map/ppermute | solution.py:53
  3.4 8.0 %collective-permute-start.1 = (f32[5,64,256]{2,1,0:T(8,128)S(1)}, f32[5,64,256]{2,1,0:T(8,128)S(1)}, u32[]{:S(2)}, u32[]{:S(2)}) collective-permute-start(f32[5,64,256]{2,1,0:T(8,128)S(1)} %pad_maximum_fusion.1), channel_id=1, source_target_pairs={{0,8},{8,16},{16,24},{1,9},{9,17},{17,25},{2,10},{10,18},{18,26},{... | collective-permute-start | bytes 983048 | tf_op jit(solution)/shard_map/ppermute | solution.py:54
  6.5 2.2 %copy-start = (f32[64,64,256]{2,1,0:T(8,128)S(1)}, f32[64,64,256]{2,1,0:T(8,128)}, u32[]{:S(2)}) copy-start(f32[64,64,256]{2,1,0:T(8,128)} %start.1) | copy-start | bytes 12582916
  8.7 2.2 %copy-start.1 = (f32[64,64,256]{2,1,0:T(8,128)S(1)}, f32[64,64,256]{2,1,0:T(8,128)}, u32[]{:S(2)}) copy-start(f32[64,64,256]{2,1,0:T(8,128)} %right.1) | copy-start | bytes 12582916
  11.6 11.4 %collective-permute-start.2 = (f32[10,72,128]{2,1,0:T(8,128)S(1)}, f32[10,72,128]{2,1,0:T(8,128)S(1)}, u32[]{:S(2)}, u32[]{:S(2)}) collective-permute-start(f32[10,72,128]{2,1,0:T(8,128)S(1)} %get-tuple-element.26), channel_id=1, source_target_pairs={{0,4},{4,0},{1,5},{5,1},{2,6},{6,2},{3,7},{7,3},{8,12},{12,8},{9,1... | collective-permute-start | bytes 1105928 | tf_op jit(solution)/shard_map/ppermute | solution.py:52
  26.4 7.0 %collective-permute-start.3 = (f32[3,72,128]{2,1,0:T(8,128)S(1)}, f32[3,72,128]{2,1,0:T(8,128)S(1)}, u32[]{:S(2)}, u32[]{:S(2)}) collective-permute-start(f32[3,72,128]{2,1,0:T(8,128)S(1)} %get-tuple-element.29), channel_id=1, source_target_pairs={{1,0},{2,1},{3,2},{5,4},{6,5},{7,6},{9,8},{10,9},{11,10},{13,12},{... | collective-permute-start | bytes 331784 | tf_op jit(solution)/shard_map/ppermute | solution.py:53
  28.8 6.7 %collective-permute-start.4 = (f32[3,72,128]{2,1,0:T(8,128)S(1)}, f32[3,72,128]{2,1,0:T(8,128)S(1)}, u32[]{:S(2)}, u32[]{:S(2)}) collective-permute-start(f32[3,72,128]{2,1,0:T(8,128)S(1)} %get-tuple-element.30), channel_id=1, source_target_pairs={{0,1},{1,2},{2,3},{4,5},{5,6},{6,7},{8,9},{9,10},{10,11},{12,13},{... | collective-permute-start | bytes 331784 | tf_op jit(solution)/shard_map/ppermute | solution.py:54
  72.9 4.3 %collective-permute-start.5 = (f32[5,40,128]{2,1,0:T(8,128)S(1)}, f32[5,40,128]{2,1,0:T(8,128)S(1)}, u32[]{:S(2)}, u32[]{:S(2)}) collective-permute-start(f32[5,40,128]{2,1,0:T(8,128)S(1)} %get-tuple-element.33), channel_id=1, source_target_pairs={{8,0},{16,8},{24,16},{9,1},{17,9},{25,17},{10,2},{18,10},{26,18},{... | collective-permute-start | bytes 307208 | tf_op jit(solution)/shard_map/ppermute | solution.py:53
  74.2 4.0 %collective-permute-start.6 = (f32[5,40,128]{2,1,0:T(8,128)S(1)}, f32[5,40,128]{2,1,0:T(8,128)S(1)}, u32[]{:S(2)}, u32[]{:S(2)}) collective-permute-start(f32[5,40,128]{2,1,0:T(8,128)S(1)} %get-tuple-element.34), channel_id=1, source_target_pairs={{0,8},{8,16},{16,24},{1,9},{9,17},{17,25},{2,10},{10,18},{18,26},{... | collective-permute-start | bytes 307208 | tf_op jit(solution)/shard_map/ppermute | solution.py:54
  78.3 5.8 %collective-permute-start.7 = (f32[5,40,128]{2,1,0:T(8,128)S(1)}, f32[5,40,128]{2,1,0:T(8,128)S(1)}, u32[]{:S(2)}, u32[]{:S(2)}) collective-permute-start(f32[5,40,128]{2,1,0:T(8,128)S(1)} %get-tuple-element.36), channel_id=1, source_target_pairs={{0,4},{4,0},{1,5},{5,1},{2,6},{6,2},{3,7},{7,3},{8,12},{12,8},{9,1... | collective-permute-start | bytes 307208 | tf_op jit(solution)/shard_map/ppermute | solution.py:52
  85.1 5.9 %collective-permute-start.8 = (f32[2,40,128]{2,1,0:T(8,128)S(1)}, f32[2,40,128]{2,1,0:T(8,128)S(1)}, u32[]{:S(2)}, u32[]{:S(2)}) collective-permute-start(f32[2,40,128]{2,1,0:T(8,128)S(1)} %get-tuple-element.38), channel_id=1, source_target_pairs={{1,0},{2,1},{3,2},{5,4},{6,5},{7,6},{9,8},{10,9},{11,10},{13,12},{... | collective-permute-start | bytes 122888 | tf_op jit(solution)/shard_map/ppermute | solution.py:53
  87.1 5.9 %collective-permute-start.9 = (f32[2,40,128]{2,1,0:T(8,128)S(1)}, f32[2,40,128]{2,1,0:T(8,128)S(1)}, u32[]{:S(2)}, u32[]{:S(2)}) collective-permute-start(f32[2,40,128]{2,1,0:T(8,128)S(1)} %get-tuple-element.39), channel_id=1, source_target_pairs={{0,1},{1,2},{2,3},{4,5},{5,6},{6,7},{8,9},{9,10},{10,11},{12,13},{... | collective-permute-start | bytes 122888 | tf_op jit(solution)/shard_map/ppermute | solution.py:54
where the time goes:
time: 114 us; the launch traced here: 112 us
  Pallas kernels  62.1 us (54%)
  starting transfers between devices  23.5 us (21%)
  waiting for transfers between devices  20.2 us (18%)
  local copies, waits for them, and re-layouts  6.41 us (6%)
    pallas_call x7, Pallas kernels, call(): pl.pallas_call(body, name=name, in_specs=[VMEM] * len(ins), out_specs=[VM...  62.1 us
    ppermute x2, waiting for transfers between devices, exchange(): return [lax.ppermute(msgs[0], axis, [(0, 1), (1, 0)])]  14 us
    ppermute x4, starting transfers between devices, exchange(): up = lax.ppermute(msgs[1], axis, [(i, i + 1) for i in range(n - 1)])  13.4 us
    ppermute x4, starting transfers between devices, exchange(): down = lax.ppermute(msgs[0], axis, [(i + 1, i) for i in range(n - 1)])  6.91 us
    ppermute x4, waiting for transfers between devices, exchange(): up = lax.ppermute(msgs[1], axis, [(i, i + 1) for i in range(n - 1)])  4.98 us
    unnamed x4, local copies, waits for them, and re-layouts  4.37 us
    ppermute x2, starting transfers between devices, exchange(): return [lax.ppermute(msgs[0], axis, [(0, 1), (1, 0)])]  3.17 us
  transfers between devices with their start and end apart: 10, of which 6 were waited for; matrix products, arithmetic and copies ran while one was open for 0% of the time, Pallas kernels for 1%

commit v1 on v0

v1 whole, which is shorter than its diff:
```python
import functools

import jax
import jax.numpy as jnp
from jax import lax
from jax.experimental import pallas as pl
from jax.experimental.pallas import tpu as pltpu
from jax.sharding import PartitionSpec as P

LANES = 128
O = 4
F = 3
G = 2
SLOT = F + G
PER = LANES // SLOT
CL = 4
CH = 3
CPER = LANES // CL

VMEM = pl.BlockSpec(memory_space=pltpu.VMEM)
ANY = pl.BlockSpec(memory_space=pl.ANY)


def f32(*shape):
    return jax.ShapeDtypeStruct(shape, jnp.float32)


def call(body, name, ins, outs, scratch=(), alias=None, limit=None, out_specs=None):
    return pl.pallas_call(
        body,
        name=name,
        in_specs=[VMEM] * len(ins),
        out_specs=[VMEM] * len(outs) if out_specs is None else out_specs,
        out_shape=outs,
        scratch_shapes=list(scratch),
        input_output_aliases=alias or {},
        compiler_params=pltpu.CompilerParams(vmem_limit_bytes=limit),
    )(*ins)


def iota(shape, dim):
    return lax.broadcasted_iota(jnp.int32, shape, dim)


def ends(axis):
    i = lax.axis_index(axis)
    return i == 0, i == lax.axis_size(axis) - 1


def exchange(msgs, axis):
    n = lax.axis_size(axis)
    if n == 2:
        return [lax.ppermute(msgs[0], axis, [(0, 1), (1, 0)])]
    down = lax.ppermute(msgs[0], axis, [(i + 1, i) for i in range(n - 1)])
    up = lax.ppermute(msgs[1], axis, [(i, i + 1) for i in range(n - 1)])
    return [down, up]


def emit(outs, index, axis, low, high):
    if len(outs) == 1:
        outs[0][index] = jnp.where(ends(axis)[0], high(), low())
    else:
        outs[0][index] = low()
        outs[1][index] = high()


def arrived(refs, index, axis):
    if len(refs) == 1:
        value = refs[0][index]
        first = ends(axis)[0]
        zero = jnp.zeros_like(value)
        return jnp.where(first, value, zero), jnp.where(first, zero, value)
    return refs[0][index], refs[1][index]


def count(axis):
    return 1 if lax.axis_size(axis) == 2 else 2


def turn(value, lanes):
    return pltpu.roll(value, lanes % LANES, 1)


def build_body(start, right, se, re):
    nx, ny, nz = start.shape
    ye = ny + 2 * O

    def plane(p, _):
        for t in range(nz // LANES):
            at = (p + O) * ye + O
            se[t, pl.ds(at, ny), :] = start[p, :, t * LANES:(t + 1) * LANES]
            re[t, pl.ds(at, ny), :] = right[p, :, t * LANES:(t + 1) * LANES]
        return 0

    lax.fori_loop(0, nx, plane, 0, unroll=4)


def xhalo_body(nx, ny, nz, nin, *refs):
    halo = refs[:nin]
    se, re, outs = refs[nin + 2], refs[nin + 3], refs[nin + 4:]
    xe, ye = nx + 2 * O, ny + 2 * O
    nt = nz // LANES
    for t in range(nt):
        cut = slice(t * LANES, (t + 1) * LANES)
        for k in range(SLOT):
            high, low = arrived(halo, (k, slice(None), cut), "gx")
            dst, size, j = (se, F, k) if k < F else (re, G, k - F)
            dst[t, pl.ds((O + nx + j) * ye + O, ny), :] = high
            dst[t, pl.ds((O - size + j) * ye + O, ny), :] = low
    for t in range(nt):
        for k in range(SLOT):
            src, size, j = (se, F, k) if k < F else (re, G, k - F)
            emit(
                outs, (k * nt + t,), "gy",
                lambda: src[t, pl.ds(O + j, xe, stride=ye), :],
                lambda: src[t, pl.ds(O + ny - size + j, xe, stride=ye), :],
            )


def yhalo_body(nx, ny, nz, nin, *refs):
    halo = refs[:nin]
    se, re, outs = refs[nin + 2], refs[nin + 3], refs[nin + 4:]
    xe, ye = nx + 2 * O, ny + 2 * O
    nt = nz // LANES
    for t in range(nt):
        for k in range(SLOT):
            high, low = arrived(halo, (k * nt + t,), "gy")
            dst, size, j = (se, F, k) if k < F else (re, G, k - F)
            dst[t, pl.ds(O + ny + j, xe, stride=ye), :] = high
            dst[t, pl.ds(O - size + j, xe, stride=ye), :] = low
    lane = iota((8, LANES), 1)

    def rows(r, _):
        base = pl.multiple_of(r * 8, 8)
        for group in range(-(-xe // PER)):
            low = jnp.zeros((8, LANES), jnp.float32)
            high = low
            for j in range(min(PER, xe - group * PER)):
                at = j * SLOT
                here = pl.ds((group * PER + j) * ye + base, 8)
                in_s = (lane >= at) & (lane < at + F)
                in_r = (lane >= at + F) & (lane < at + SLOT)
                low = jnp.where(in_s, turn(se[0, here, :], at), low)
                low = jnp.where(in_r, turn(re[0, here, :], at + F), low)
                high = jnp.where(in_s, turn(se[nt - 1, here, :], at + F), high)
                high = jnp.where(in_r, turn(re[nt - 1, here, :], at + SLOT), high)
            emit(outs, (group, pl.ds(base, 8)), "gz", lambda: low, lambda: high)
        return 0

    lax.fori_loop(0, ye // 8, rows, 0)


def inside(shape, dim, offset, cells, axis):
    first, last = ends(axis)
    at = iota(shape, dim) - offset
    up = jnp.where(last, 0.0, 1.0)
    down = jnp.where(first, 0.0, 1.0)
    return jnp.where(at < 0, down, jnp.where(at < cells, 1.0, up))


def fill_mask(mask, ny):
    total, ye, _ = mask.shape
    valid = inside((ye, LANES), 0, O, ny, "gy") * (1.0 / 7.0)
    for t in range(total - 1):
        mask[t] = valid
    first, last = ends("gz")
    lane = iota((ye, LANES), 1)
    mask[total - 1] = valid * jnp.where(
        lane < CH, jnp.where(last, 0.0, 1.0), jnp.where(lane >= LANES - CL, jnp.where(first, 0.0, 1.0), 0.0)
    )


def stencil(ref, ye, base, planes, tiles, use):
    total = ref.shape[0]
    lane = iota((8, LANES), 1)

    def at(p, t, shift=0):
        return ref[t, pl.ds((p + O) * ye + base + shift, 8), :]

    before = [at(planes[0] - 1, t) for t in range(tiles)]
    centre = [at(planes[0], t) for t in range(total)]
    for p in planes:
        after = [at(p + 1, t) for t in range(total)]
        left = [turn(c, 1) for c in centre]
        right = [turn(c, -1) for c in centre]
        for t in range(tiles):
            near = jnp.where(lane == 0, left[t - 1], left[t])
            near = near + jnp.where(lane == LANES - 1, right[(t + 1) % total], right[t])
            near = near + (at(p, t, -1) + at(p, t, 1))
            near = near + (before[t] + after[t])
            use(p, t, centre[t], near)
        before, centre = centre, after


def sweep(src, dst, right, mask, nx, low, high):
    total, ye, _ = mask.shape
    first, last = ends("gx")
    up = jnp.where(last, 0.0, 1.0)
    down = jnp.where(first, 0.0, 1.0)

    def rows(r, _):
        base = pl.multiple_of(r * 8, 8)
        m = [mask[t, pl.ds(base, 8), :] for t in range(total)]

        def use(p, t, centre, near):
            here = pl.ds((p + O) * ye + base, 8)
            factor = m[t] * down if p < 0 else m[t] * up if p >= nx else m[t]
            dst[t, here, :] = factor * (near + (centre + right[t, here, :]))

        stencil(src, ye, base, range(-low, nx + high), total, use)
        return 0

    lax.fori_loop(0, ye // 8, rows, 0)


def split_dot(value, weight):
    high = value.astype(jnp.bfloat16)
    rest = value - high.astype(jnp.float32)
    mid = rest.astype(jnp.bfloat16)
    small = (rest - mid.astype(jnp.float32)).astype(jnp.bfloat16)
    dot = functools.partial(jnp.dot, preferred_element_type=jnp.float32)
    return dot(high, weight) + dot(mid, weight) + dot(small, weight)


def lane_dot(src, src_at, dst, dst_at, rows, weight):
    step = max(s for s in range(8, 273, 8) if rows % s == 0)
    for at in range(0, rows, step):
        value = jnp.concatenate([src[t, pl.ds(src_at + at, step), :] for t in range(weight.shape[0] // LANES)], axis=1)
        got = split_dot(value, weight)
        for t in range(weight.shape[1] // LANES):
            dst[t, pl.ds(dst_at + at, step), :] = got[:, t * LANES:(t + 1) * LANES]


def transfer_weights(fine, coarse, halo, fine_dim, inner, outer):
    shape = (fine, coarse + halo) if fine_dim == 0 else (coarse + halo, fine)
    z = iota(shape, fine_dim)
    k = iota(shape, 1 - fine_dim)
    k = jnp.where(k >= coarse, k - (coarse + halo), k)
    off = z - 2 * k
    weight = jnp.where(off == 1, inner, jnp.where((off == 0) | (off == 2), outer, 0.0))
    return jnp.where(k < -1, 0.0, weight).astype(jnp.bfloat16)


def smooth_body(nx, ny, nz, nin, *refs):
    halo = refs[:nin]
    se, re, s2, coarse = refs[nin + 2:nin + 6]
    outs = refs[nin + 6:-4]
    s1, rx, ry, mask = refs[-4:]
    xe, ye = nx + 2 * O, ny + 2 * O
    nt = nz // LANES
    lane = iota((8, LANES), 1)

    def unpack(r, _):
        base = pl.multiple_of(r * 8, 8)
        for group in range(-(-xe // PER)):
            high, low = arrived(halo, (group, pl.ds(base, 8)), "gz")
            for j in range(min(PER, xe - group * PER)):
                at = j * SLOT
                here = pl.ds((group * PER + j) * ye + base, 8)
                se[nt, here, :] = jnp.where(lane < 64, turn(high, -at), turn(low, -F - at))
                re[nt, here, :] = jnp.where(lane < 64, turn(high, -at - F), turn(low, -G - at - F))
        return 0

    lax.fori_loop(0, ye // 8, unpack, 0)
    fill_mask(mask, ny)
    sweep(se, s1, re, mask, nx, 2, 2)
    sweep(s1, s2, re, mask, nx, 1, 1)

    def restrict_x(r, _):
        base = r * 8 + O
        at = pl.multiple_of(r * 8, 8)
        quarter, half = {}, {}

        def use(p, t, centre, near):
            value = (near + re[t, pl.ds((p + O) * ye + base, 8), :]) - 6.0 * centre
            if p % 2:
                half[t] = 0.5 * value
                if p == nx - 1:
                    rx[t, pl.ds((nx // 2) * ny + at, 8), :] = quarter[t] + half[t]
                return
            value = 0.25 * value
            part = value if p == 0 else (quarter[t] + half[t]) + value
            rx[t, pl.ds((p // 2) * ny + at, 8), :] = part
            quarter[t] = value

        stencil(s2, ye, base, range(nx), nt, use)
        return 0

    lax.fori_loop(0, ny // 8, restrict_x, 0)

    cx, cy, cz = nx // 2, ny // 2, nz // 2
    ct = cz // LANES
    cye = cy + 2 * O
    row = iota((8, LANES), 0)
    zero = jnp.zeros((8, LANES), jnp.float32)
    for t in range(nt):
        rx[t, pl.ds((cx + 1) * ny, 8), :] = zero

    def restrict_y(i, _):
        for t in range(nt):
            for k in range(cy // 8):
                at = i * ny + 16 * k
                even = 0.25 * rx[t, pl.ds(at, 8, stride=2), :]
                odd = 0.5 * rx[t, pl.ds(at + 1, 8, stride=2), :]
                after = 0.25 * rx[t, pl.ds(at + 2, 8, stride=2), :]
                if k == cy // 8 - 1:
                    after = jnp.where(row == 7, 0.0, after)
                if k == 0:
                    ry[t, pl.ds(i * cye, 8), :] = jnp.where(row == O - 1, even[0:1], 0.0)
                    ry[t, pl.ds(i * cye + cy, 8), :] = zero
                ry[t, pl.ds(i * cye + O + 8 * k, 8), :] = (even + odd) + after
        return 0

    lax.fori_loop(0, cx + 1, restrict_y, 0, unroll=3 if cx % 3 == 2 else 1)
    weight = transfer_weights(nz, cz, LANES, 0, 0.5, 0.25)
    lane_dot(ry, 0, coarse, (O - 1) * cye, (cx + 1) * cye, weight)
    for t in range(ct + 1):
        coarse[t, pl.ds((cx + 2 * O - 1) * cye, cye), :] = jnp.zeros((cye, LANES), jnp.float32)
    faces(
        outs, "gx",
        lambda t, j: coarse[t, pl.ds((O - 1 + j) * cye, cye), :],
        lambda t, j: coarse[t, pl.ds((cx + j) * cye, cye), :],
        ct,
    )


def faces(outs, axis, low, high, ct):
    extra_low = extra_high = None
    for j in range(CL):
        for t in range(ct):
            emit(outs, (j * ct + t,), axis, lambda: low(t, j), lambda: high(t, j))
        a = turn(low(ct, j), j + 1)
        b = turn(high(ct, j), j + 1)
        lane = iota(a.shape, 1)
        extra_low = a if j == 0 else jnp.where(lane == j, a, extra_low)
        extra_high = b if j == 0 else jnp.where(lane == j, b, extra_high)
    emit(outs, (CL * ct,), axis, lambda: extra_low, lambda: extra_high)


def place_faces(refs, axis, ct, size, read, write):
    for t in range(ct + 1):
        for j in range(CL):
            if t < ct:
                high, low = arrived(refs, (j * ct + t,), axis)
            else:
                high, low = arrived(refs, (CL * ct,), axis)
                lane = iota(high.shape, 1)
                high = jnp.where(lane == LANES - 1, turn(high, -1 - j), 0.0)
                low = jnp.where(lane == LANES - 1, turn(low, -1 - j), 0.0)
            q = size - 1 + j
            write(t, q, read(t, q) + high if j == 0 else high)
            q = j - CL
            write(t, q, read(t, q) + low if j == CL - 1 else low)


def coarse_x_body(cx, cy, cz, nin, *refs):
    halo = refs[:nin]
    coarse, outs = refs[nin + 1], refs[nin + 2:]
    ct = cz // LANES
    xe, ye = cx + 2 * O, cy + 2 * O

    def read(t, q):
        return coarse[t, pl.ds((q + O) * ye, ye), :]

    def write(t, q, value):
        coarse[t, pl.ds((q + O) * ye, ye), :] = value

    place_faces(halo, "gx", ct, cx, read, write)
    faces(
        outs, "gy",
        lambda t, j: coarse[t, pl.ds(O - 1 + j, xe, stride=ye), :],
        lambda t, j: coarse[t, pl.ds(cy + j, xe, stride=ye), :],
        ct,
    )


def coarse_y_body(cx, cy, cz, nin, *refs):
    halo = refs[:nin]
    coarse, outs = refs[nin + 1], refs[nin + 2:]
    ct = cz // LANES
    xe, ye = cx + 2 * O, cy + 2 * O

    def read(t, q):
        return coarse[t, pl.ds(q + O, xe, stride=ye), :]

    def write(t, q, value):
        coarse[t, pl.ds(q + O, xe, stride=ye), :] = value

    place_faces(halo, "gy", ct, cy, read, write)
    lane = iota((8, LANES), 1)

    def rows(r, _):
        base = pl.multiple_of(r * 8, 8)
        for group in range(-(-xe // CPER)):
            low = jnp.zeros((8, LANES), jnp.float32)
            high = low
            for j in range(min(CPER, xe - group * CPER)):
                at = j * CL
                rows8 = pl.ds((group * CPER + j) * ye + base, 8)
                head = jnp.where(lane < CL - 1, coarse[0, rows8, :], coarse[ct, rows8, :])
                here = (lane >= at) & (lane < at + CL)
                low = jnp.where(here, turn(head, at + 1), low)
                high = jnp.where(here, turn(coarse[ct - 1, rows8, :], at + CL), high)
            emit(outs, (group, pl.ds(base, 8)), "gz", lambda: low, lambda: high)
        return 0

    lax.fori_loop(0, ye // 8, rows, 0)


def finish_body(cx, cy, cz, nin, *refs):
    halo = refs[:nin]
    smooth, _, coarse, out = refs[nin:nin + 4]
    ca, cb, mask, fine, stage, sems = refs[nin + 4:]
    ct = cz // LANES
    xe, ye = cx + 2 * O, cy + 2 * O
    nx, ny, nz = 2 * cx, 2 * cy, 2 * cz
    nt = nz // LANES
    lane = iota((8, LANES), 1)
    first, last = ends("gx")
    up = jnp.where(last, 0.0, 1.0)
    down = jnp.where(first, 0.0, 1.0)
    fill_mask(mask, cy)

    def unpack(r, _):
        base = pl.multiple_of(r * 8, 8)
        m = [mask[t, pl.ds(base, 8), :] for t in range(ct + 1)]
        for group in range(-(-xe // CPER)):
            high, low = arrived(halo, (group, pl.ds(base, 8)), "gz")
            for j in range(min(CPER, xe - group * CPER)):
                q = group * CPER + j
                here = pl.ds(q * ye + base, 8)
                fromhigh = turn(high, -j * CL - 1)
                fromlow = turn(low, -j * CL - CL)
                edge = lane == LANES - 1
                value = [coarse[t, here, :] for t in range(ct + 1)]
                value[ct - 1] = value[ct - 1] + jnp.where(edge, fromhigh, 0.0)
                wing = jnp.where(lane < CH, fromhigh, jnp.where(lane >= LANES - CL, fromlow, 0.0))
                value[ct] = wing + jnp.where(edge, value[ct], 0.0)
                for t in range(ct + 1):
                    factor = m[t] * down if q < O else m[t] * up if q >= O + cx else m[t]
                    scaled = 4.0 * value[t]
                    coarse[t, here, :] = scaled
                    ca[t, here, :] = factor * scaled
        return 0

    lax.fori_loop(0, ye // 8, unpack, 0)
    sweep(ca, cb, coarse, mask, cx, 3, 2)
    sweep(cb, ca, coarse, mask, cx, 2, 1)
    sweep(ca, cb, coarse, mask, cx, 1, 0)
    lane_dot(cb, (O - 1) * ye, fine, 0, (cx + 1) * ye, transfer_weights(nz, cz, LANES, 1, 1.0, 0.5))

    chunks = sems.shape[0]
    per = cx // chunks
    fye = ny + 2 * O
    flat = stage.reshape(nt, nx * ny, LANES)

    def send(c, t):
        at = c * 2 * per
        cut = pl.ds(t * LANES, LANES)
        return pltpu.make_async_copy(
            stage.at[t, pl.ds(at, 2 * per)], out.at[pl.ds(at, 2 * per), :, cut], sems.at[c, t]
        )

    def add(i, _):
        for t in range(nt):
            for k in range(cy // 8):
                at = (i + 1) * ye + O + 8 * k
                here = fine[t, pl.ds(at, 8), :]
                mid = 0.5 * (here + fine[t, pl.ds(at - 1, 8), :])
                before = fine[t, pl.ds(at - ye, 8), :]
                before_mid = 0.5 * (before + fine[t, pl.ds(at - ye - 1, 8), :])
                parts = (0.5 * (before_mid + mid), 0.5 * (before + here), mid, here)
                for n, part in enumerate(parts):
                    src = (2 * i + n // 2 + O) * fye + O + 16 * k + n % 2
                    dst = (2 * i + n // 2) * ny + 16 * k + n % 2
                    flat[t, pl.ds(dst, 8, stride=2), :] = smooth[t, pl.ds(src, 8, stride=2), :] + part
        return 0

    for c in range(chunks):
        lax.fori_loop(c * per, (c + 1) * per, add, 0)
        for t in range(nt):
            send(c, t).start()
    for c in range(chunks):
        for t in range(nt):
            send(c, t).wait()


def on_device(start, right):
    nx, ny, nz = start.shape
    nt = nz // LANES
    xe, ye = nx + 2 * O, ny + 2 * O
    cx, cy, cz = nx // 2, ny // 2, nz // 2
    ct = cz // LANES
    cxe, cye = cx + 2 * O, cy + 2 * O
    big = f32(nt + 1, xe * ye, LANES)
    mb = 1 << 20

    to_prev = jnp.concatenate([start[:F], right[:G]], axis=0)
    to_next = jnp.concatenate([start[nx - F:], right[nx - G:]], axis=0)
    if count("gx") == 1:
        to_prev = jnp.where(ends("gx")[0], to_next, to_prev)
    halo = exchange([to_prev, to_next], "gx")
    se, re = call(build_body, "build", [start, right], [big, big], limit=8 * mb)

    n = len(halo)
    se, re, *msgs = call(
        functools.partial(xhalo_body, nx, ny, nz, n), "xhalo", [*halo, se, re],
        [big, big] + [f32(SLOT * nt, xe, LANES)] * count("gy"), alias={n: 0, n + 1: 1}, limit=8 * mb,
    )
    halo = exchange(msgs, "gy")
    n = len(halo)
    se, re, *msgs = call(
        functools.partial(yhalo_body, nx, ny, nz, n), "yhalo", [*halo, se, re],
        [big, big] + [f32(-(-xe // PER), ye, LANES)] * count("gz"), alias={n: 0, n + 1: 1}, limit=8 * mb,
    )
    halo = exchange(msgs, "gz")
    n = len(halo)
    small = f32(ct + 1, cxe * cye, LANES)
    se, re, s2, coarse, *msgs = call(
        functools.partial(smooth_body, nx, ny, nz, n), "smooth", [*halo, se, re],
        [big, big, big, small] + [f32(CL * ct + 1, cye, LANES)] * count("gx"),
        scratch=[
            pltpu.VMEM((nt + 1, xe * ye, LANES), jnp.float32),
            pltpu.VMEM((nt, (cx + 1) * ny + 8, LANES), jnp.float32),
            pltpu.VMEM((nt, (cx + 1) * cye, LANES), jnp.float32),
            pltpu.VMEM((nt + 1, ye, LANES), jnp.float32),
        ],
        alias={n: 0, n + 1: 1}, limit=24 * mb,
    )
    halo = exchange(msgs, "gx")
    n = len(halo)
    coarse, *msgs = call(
        functools.partial(coarse_x_body, cx, cy, cz, n), "coarse_x", [*halo, coarse],
        [small] + [f32(CL * ct + 1, cxe, LANES)] * count("gy"), alias={n: 0}, limit=8 * mb,
    )
    halo = exchange(msgs, "gy")
    n = len(halo)
    coarse, *msgs = call(
        functools.partial(coarse_y_body, cx, cy, cz, n), "coarse_y", [*halo, coarse],
        [small] + [f32(-(-cxe // CPER), cye, LANES)] * count("gz"), alias={n: 0}, limit=8 * mb,
    )
    halo = exchange(msgs, "gz")
    n = len(halo)
    _, out = call(
        functools.partial(finish_body, cx, cy, cz, n), "finish", [*halo, s2, coarse],
        [small, f32(nx, ny, nz)],
        scratch=[
            pltpu.VMEM((ct + 1, cxe * cye, LANES), jnp.float32),
            pltpu.VMEM((ct + 1, cxe * cye, LANES), jnp.float32),
            pltpu.VMEM((ct + 1, cye, LANES), jnp.float32),
            pltpu.VMEM((nt, (cx + 1) * cye, LANES), jnp.float32),
            pltpu.VMEM((nt, nx, ny, LANES), jnp.float32),
            pltpu.SemaphoreType.DMA((8, nt)),
        ],
        alias={n + 1: 0}, limit=24 * mb, out_specs=[VMEM, ANY],
    )
    return out


def solution(mesh):
    spec = P("gx", "gy", "gz")
    return jax.shard_map(on_device, mesh=mesh, in_specs=(spec, spec), out_specs=spec, check_vma=False)
```

time: 114 us -> 81.9 us (0.72)
  Pallas kernels: 62.1 us -> 30 us
    pallas_call x7, Pallas kernels: 62.1 us -> 30 us  [call(): pl.pallas_call(body, name=name, in_specs=[VMEM] * len(ins), out_specs=[VM...]
where the time goes in v1:
time: 81.9 us; the launch traced here: 80.3 us
  Pallas kernels  30 us (37%)
  starting transfers between devices  23.5 us (29%)
  waiting for transfers between devices  20.2 us (25%)
  local copies, waits for them, and re-layouts  6.41 us (8%)
    pallas_call x7, Pallas kernels, call(): pl.pallas_call(body, name=name, in_specs=[VMEM] * len(ins), out_specs=[VM...  30 us
    ppermute x2, waiting for transfers between devices, exchange(): return [lax.ppermute(msgs[0], axis, [(0, 1), (1, 0)])]  14 us
    ppermute x4, starting transfers between devices, exchange(): up = lax.ppermute(msgs[1], axis, [(i, i + 1) for i in range(n - 1)])  13.4 us
    ppermute x4, starting transfers between devices, exchange(): down = lax.ppermute(msgs[0], axis, [(i + 1, i) for i in range(n - 1)])  6.91 us
    ppermute x4, waiting for transfers between devices, exchange(): up = lax.ppermute(msgs[1], axis, [(i, i + 1) for i in range(n - 1)])  4.98 us
    unnamed x4, local copies, waits for them, and re-layouts  4.37 us
    ppermute x2, starting transfers between devices, exchange(): return [lax.ppermute(msgs[0], axis, [(0, 1), (1, 0)])]  3.17 us
    slice x2, local copies, waits for them, and re-layouts, on_device(): to_next = jnp.concatenate([start[nx - F:], right[nx - G:]], axis=0)  2.04 us
  transfers between devices with their start and end apart: 10, of which 6 were waited for; matrix products, arithmetic and copies ran while one was open for 0% of the time, Pallas kernels for 1%

profile of v1, /device:TPU:16, one launch (start us, length us, event | category | flops | bytes accessed | tf_op | source)
XLA Modules:
  0.0 80.3 jit_solution(4378376966664921441)
XLA Ops:
  0.0 1.0 %fusion.1 = (f32[2,64,256]{2,1,0:T(8,128)S(1)}, f32[2,64,256]{2,1,0:T(8,128)S(1)}) fusion(f32[64,64,256]{2,1,0:T(8,128)} %right.1), kind=kLoop, calls=%fused_computation.3 | loop fusion | bytes 524288 | tf_op jit(solution)/shard_map/slice | solution.py:499
  1.0 1.1 %fusion = (f32[3,64,256]{2,1,0:T(8,128)S(1)}, f32[3,64,256]{2,1,0:T(8,128)S(1)}) fusion(f32[64,64,256]{2,1,0:T(8,128)} %start.1), kind=kLoop, calls=%fused_computation.2 | loop fusion | bytes 786432 | tf_op jit(solution)/shard_map/slice | solution.py:499
  2.1 1.3 %collective-permute-start = (f32[5,64,256]{2,1,0:T(8,128)S(1)}, f32[5,64,256]{2,1,0:T(8,128)S(1)}, u32[]{:S(2)}, u32[]{:S(2)}) collective-permute-start(f32[5,64,256]{2,1,0:T(8,128)S(1)} %pad_maximum_fusion), channel_id=1, source_target_pairs={{8,0},{16,8},{24,16},{9,1},{17,9},{25,17},{10,2},{18,10},{26,18},{... | collective-permute-start | bytes 983048 | tf_op jit(solution)/shard_map/ppermute | solution.py:54
  3.4 3.1 %collective-permute-start.1 = (f32[5,64,256]{2,1,0:T(8,128)S(1)}, f32[5,64,256]{2,1,0:T(8,128)S(1)}, u32[]{:S(2)}, u32[]{:S(2)}) collective-permute-start(f32[5,64,256]{2,1,0:T(8,128)S(1)} %pad_maximum_fusion.1), channel_id=1, source_target_pairs={{0,8},{8,16},{16,24},{1,9},{9,17},{17,25},{2,10},{10,18},{18,26},{... | collective-permute-start | bytes 983048 | tf_op jit(solution)/shard_map/ppermute | solution.py:55
  6.5 0.0 copy-start
  6.5 2.2 %copy-done = f32[64,64,256]{2,1,0:T(8,128)S(1)} copy-done((f32[64,64,256]{2,1,0:T(8,128)S(1)}, f32[64,64,256]{2,1,0:T(8,128)}, u32[]{:S(2)}) %copy-start) | copy-done | bytes 4194328
  8.7 0.0 copy-start.1
  8.7 2.2 %copy-done.1 = f32[64,64,256]{2,1,0:T(8,128)S(1)} copy-done((f32[64,64,256]{2,1,0:T(8,128)S(1)}, f32[64,64,256]{2,1,0:T(8,128)}, u32[]{:S(2)}) %copy-start.1) | copy-done | bytes 4194328
  10.8 0.6 build.1
  11.4 0.0 collective-permute-done.refs_0_
  11.4 0.0 collective-permute-done.1.refs_1_
  11.4 0.2 xhalo.1
  11.6 1.6 %collective-permute-start.2 = (f32[10,72,128]{2,1,0:T(8,128)S(1)}, f32[10,72,128]{2,1,0:T(8,128)S(1)}, u32[]{:S(2)}, u32[]{:S(2)}) collective-permute-start(f32[10,72,128]{2,1,0:T(8,128)S(1)} %get-tuple-element.26), channel_id=1, source_target_pairs={{0,4},{4,0},{1,5},{5,1},{2,6},{6,2},{3,7},{7,3},{8,12},{12,8},{9,1... | collective-permute-start | bytes 1105928 | tf_op jit(solution)/shard_map/ppermute | solution.py:53
  13.2 9.8 %collective-permute-done.2.refs_0_ = f32[10,72,128]{2,1,0:T(8,128)S(1)} collective-permute-done((f32[10,72,128]{2,1,0:T(8,128)S(1)}, f32[10,72,128]{2,1,0:T(8,128)S(1)}, u32[]{:S(2)}, u32[]{:S(2)}) %collective-permute-start.2) | collective-permute-done | bytes 368672 | tf_op jit(solution)/shard_map/ppermute | solution.py:53
  23.0 3.6 %yhalo.1 = (f32[3,5184,128]{2,1,0:T(8,128)S(1)}, f32[3,5184,128]{2,1,0:T(8,128)S(1)}, f32[3,72,128]{2,1,0:T(8,128)S(1)}, f32[3,72,128]{2,1,0:T(8,128)S(1)}) custom-call(f32[10,72,128]{2,1,0:T(8,128)S(1)} %collective-permute-done.2.refs_0_, f32[3,5184,128]{2,1,0:T(8,128)S(1)} %get-tuple-element.27.refs_1_, ...), custom_call_target="tpu_custom_call", output_to_operand_aliasing={{0}: (1, {}), {1}: (2, {})} | custom-call | tf_op jit(solution)/shard_map/yhalo/pallas_call | solution.py:29
  26.6 2.4 %collective-permute-start.3 = (f32[3,72,128]{2,1,0:T(8,128)S(1)}, f32[3,72,128]{2,1,0:T(8,128)S(1)}, u32[]{:S(2)}, u32[]{:S(2)}) collective-permute-start(f32[3,72,128]{2,1,0:T(8,128)S(1)} %get-tuple-element.29), channel_id=1, source_target_pairs={{1,0},{2,1},{3,2},{5,4},{6,5},{7,6},{9,8},{10,9},{11,10},{13,12},{... | collective-permute-start | bytes 331784 | tf_op jit(solution)/shard_map/ppermute | solution.py:54
  29.0 3.5 %collective-permute-start.4 = (f32[3,72,128]{2,1,0:T(8,128)S(1)}, f32[3,72,128]{2,1,0:T(8,128)S(1)}, u32[]{:S(2)}, u32[]{:S(2)}) collective-permute-start(f32[3,72,128]{2,1,0:T(8,128)S(1)} %get-tuple-element.30), channel_id=1, source_target_pairs={{0,1},{1,2},{2,3},{4,5},{5,6},{6,7},{8,9},{9,10},{10,11},{12,13},{... | collective-permute-start | bytes 331784 | tf_op jit(solution)/shard_map/ppermute | solution.py:55
  32.4 1.1 %collective-permute-done.3.refs_0_ = f32[3,72,128]{2,1,0:T(8,128)S(1)} collective-permute-done((f32[3,72,128]{2,1,0:T(8,128)S(1)}, f32[3,72,128]{2,1,0:T(8,128)S(1)}, u32[]{:S(2)}, u32[]{:S(2)}) %collective-permute-start.3) | collective-permute-done | bytes 110624 | tf_op jit(solution)/shard_map/ppermute | solution.py:54
  33.6 2.1 %collective-permute-done.4.refs_1_ = f32[3,72,128]{2,1,0:T(8,128)S(1)} collective-permute-done((f32[3,72,128]{2,1,0:T(8,128)S(1)}, f32[3,72,128]{2,1,0:T(8,128)S(1)}, u32[]{:S(2)}, u32[]{:S(2)}) %collective-permute-start.4) | collective-permute-done | bytes 110624 | tf_op jit(solution)/shard_map/ppermute | solution.py:55
  35.6 17.3 %smooth.1 = (f32[3,5184,128]{2,1,0:T(8,128)S(1)}, f32[3,5184,128]{2,1,0:T(8,128)S(1)}, f32[3,5184,128]{2,1,0:T(8,128)S(1)}, f32[2,1600,128]{2,1,0:T(8,128)S(1)},...) custom-call(f32[3,72,128]{2,1,0:T(8,128)S(1)} %collective-permute-done.3.refs_, ...), custom_call_target="tpu_custom_call", output_to_operand_aliasing={{0}: (2, {}), {1}: (3, {})} | custom-call | tf_op jit(solution)/shard_map/smooth/pallas_call | solution.py:29
  52.9 1.3 %collective-permute-start.5 = (f32[5,40,128]{2,1,0:T(8,128)S(1)}, f32[5,40,128]{2,1,0:T(8,128)S(1)}, u32[]{:S(2)}, u32[]{:S(2)}) collective-permute-start(f32[5,40,128]{2,1,0:T(8,128)S(1)} %get-tuple-element.33), channel_id=1, source_target_pairs={{8,0},{16,8},{24,16},{9,1},{17,9},{25,17},{10,2},{18,10},{26,18},{... | collective-permute-start | bytes 307208 | tf_op jit(solution)/shard_map/ppermute | solution.py:54
  54.2 3.0 %collective-permute-start.6 = (f32[5,40,128]{2,1,0:T(8,128)S(1)}, f32[5,40,128]{2,1,0:T(8,128)S(1)}, u32[]{:S(2)}, u32[]{:S(2)}) collective-permute-start(f32[5,40,128]{2,1,0:T(8,128)S(1)} %get-tuple-element.34), channel_id=1, source_target_pairs={{0,8},{8,16},{16,24},{1,9},{9,17},{17,25},{2,10},{10,18},{18,26},{... | collective-permute-start | bytes 307208 | tf_op jit(solution)/shard_map/ppermute | solution.py:55
  57.3 0.0 collective-permute-done.5.refs_0_
  57.3 0.9 %collective-permute-done.6.refs_1_ = f32[5,40,128]{2,1,0:T(8,128)S(1)} collective-permute-done((f32[5,40,128]{2,1,0:T(8,128)S(1)}, f32[5,40,128]{2,1,0:T(8,128)S(1)}, u32[]{:S(2)}, u32[]{:S(2)}) %collective-permute-start.6) | collective-permute-done | bytes 102432 | tf_op jit(solution)/shard_map/ppermute | solution.py:55
  58.2 0.2 coarse_x.1
  58.4 1.6 %collective-permute-start.7 = (f32[5,40,128]{2,1,0:T(8,128)S(1)}, f32[5,40,128]{2,1,0:T(8,128)S(1)}, u32[]{:S(2)}, u32[]{:S(2)}) collective-permute-start(f32[5,40,128]{2,1,0:T(8,128)S(1)} %get-tuple-element.36), channel_id=1, source_target_pairs={{0,4},{4,0},{1,5},{5,1},{2,6},{6,2},{3,7},{7,3},{8,12},{12,8},{9,1... | collective-permute-start | bytes 307208 | tf_op jit(solution)/shard_map/ppermute | solution.py:53
  60.0 4.2 %collective-permute-done.7.refs_0_ = f32[5,40,128]{2,1,0:T(8,128)S(1)} collective-permute-done((f32[5,40,128]{2,1,0:T(8,128)S(1)}, f32[5,40,128]{2,1,0:T(8,128)S(1)}, u32[]{:S(2)}, u32[]{:S(2)}) %collective-permute-start.7) | collective-permute-done | bytes 102432 | tf_op jit(solution)/shard_map/ppermute | solution.py:53
  64.2 0.9 %coarse_y.1 = (f32[2,1600,128]{2,1,0:T(8,128)S(1)}, f32[2,40,128]{2,1,0:T(8,128)S(1)}, f32[2,40,128]{2,1,0:T(8,128)S(1)}) custom-call(f32[5,40,128]{2,1,0:T(8,128)S(1)} %collective-permute-done.7.refs_0_, f32[2,1600,128]{2,1,0:T(8,128)S(1)} %get-tuple-element.37.refs_1_), custom_call_target="tpu_custom_call", output_to_operand_aliasing={{0}: (1, {})} | custom-call | tf_op jit(solution)/shard_map/coarse_y/pallas_call | solution.py:29
  65.1 2.0 %collective-permute-start.8 = (f32[2,40,128]{2,1,0:T(8,128)S(1)}, f32[2,40,128]{2,1,0:T(8,128)S(1)}, u32[]{:S(2)}, u32[]{:S(2)}) collective-permute-start(f32[2,40,128]{2,1,0:T(8,128)S(1)} %get-tuple-element.38), channel_id=1, source_target_pairs={{1,0},{2,1},{3,2},{5,4},{6,5},{7,6},{9,8},{10,9},{11,10},{13,12},{... | collective-permute-start | bytes 122888 | tf_op jit(solution)/shard_map/ppermute | solution.py:54
  67.1 3.9 %collective-permute-start.9 = (f32[2,40,128]{2,1,0:T(8,128)S(1)}, f32[2,40,128]{2,1,0:T(8,128)S(1)}, u32[]{:S(2)}, u32[]{:S(2)}) collective-permute-start(f32[2,40,128]{2,1,0:T(8,128)S(1)} %get-tuple-element.39), channel_id=1, source_target_pairs={{0,1},{1,2},{2,3},{4,5},{5,6},{6,7},{8,9},{9,10},{10,11},{12,13},{... | collective-permute-start | bytes 122888 | tf_op jit(solution)/shard_map/ppermute | solution.py:55
  71.0 0.0 collective-permute-done.8.refs_0_
  71.0 2.0 %collective-permute-done.9.refs_1_ = f32[2,40,128]{2,1,0:T(8,128)S(1)} collective-permute-done((f32[2,40,128]{2,1,0:T(8,128)S(1)}, f32[2,40,128]{2,1,0:T(8,128)S(1)}, u32[]{:S(2)}, u32[]{:S(2)}) %collective-permute-start.9) | collective-permute-done | bytes 40992 | tf_op jit(solution)/shard_map/ppermute | solution.py:55
  73.0 7.3 %finish.1 = (f32[2,1600,128]{2,1,0:T(8,128)S(1)}, f32[64,64,256]{2,1,0:T(8,128)}) custom-call(f32[2,40,128]{2,1,0:T(8,128)S(1)} %collective-permute-done.8.refs_0_, f32[2,40,128]{2,1,0:T(8,128)S(1)} %collective-permute-done.9.refs_1_, f32[3,5184,128]{2,1,0:T(8,128)S(1)} %get-tuple-element.40.refs_2_, ...), custom_call_target="tpu_custom_call", output_to_operand_aliasing={{0}: (3, {})} | custom-call | tf_op jit(solution)/shard_map/finish/pallas_call | solution.py:29
  (2 shorter events, 0.0 us)
Async XLA Ops:
  2.1 9.3 %collective-permute-start = (f32[5,64,256]{2,1,0:T(8,128)S(1)}, f32[5,64,256]{2,1,0:T(8,128)S(1)}, u32[]{:S(2)}, u32[]{:S(2)}) collective-permute-start(f32[5,64,256]{2,1,0:T(8,128)S(1)} %pad_maximum_fusion), channel_id=1, source_target_pairs={{8,0},{16,8},{24,16},{9,1},{17,9},{25,17},{10,2},{18,10},{26,18},{... | collective-permute-start | bytes 983048 | tf_op jit(solution)/shard_map/ppermute | solution.py:54
  3.4 8.0 %collective-permute-start.1 = (f32[5,64,256]{2,1,0:T(8,128)S(1)}, f32[5,64,256]{2,1,0:T(8,128)S(1)}, u32[]{:S(2)}, u32[]{:S(2)}) collective-permute-start(f32[5,64,256]{2,1,0:T(8,128)S(1)} %pad_maximum_fusion.1), channel_id=1, source_target_pairs={{0,8},{8,16},{16,24},{1,9},{9,17},{17,25},{2,10},{10,18},{18,26},{... | collective-permute-start | bytes 983048 | tf_op jit(solution)/shard_map/ppermute | solution.py:55
  6.5 2.2 %copy-start = (f32[64,64,256]{2,1,0:T(8,128)S(1)}, f32[64,64,256]{2,1,0:T(8,128)}, u32[]{:S(2)}) copy-start(f32[64,64,256]{2,1,0:T(8,128)} %start.1) | copy-start | bytes 12582916
  8.7 2.2 %copy-start.1 = (f32[64,64,256]{2,1,0:T(8,128)S(1)}, f32[64,64,256]{2,1,0:T(8,128)}, u32[]{:S(2)}) copy-start(f32[64,64,256]{2,1,0:T(8,128)} %right.1) | copy-start | bytes 12582916
  11.6 11.4 %collective-permute-start.2 = (f32[10,72,128]{2,1,0:T(8,128)S(1)}, f32[10,72,128]{2,1,0:T(8,128)S(1)}, u32[]{:S(2)}, u32[]{:S(2)}) collective-permute-start(f32[10,72,128]{2,1,0:T(8,128)S(1)} %get-tuple-element.26), channel_id=1, source_target_pairs={{0,4},{4,0},{1,5},{5,1},{2,6},{6,2},{3,7},{7,3},{8,12},{12,8},{9,1... | collective-permute-start | bytes 1105928 | tf_op jit(solution)/shard_map/ppermute | solution.py:53
  26.6 7.0 %collective-permute-start.3 = (f32[3,72,128]{2,1,0:T(8,128)S(1)}, f32[3,72,128]{2,1,0:T(8,128)S(1)}, u32[]{:S(2)}, u32[]{:S(2)}) collective-permute-start(f32[3,72,128]{2,1,0:T(8,128)S(1)} %get-tuple-element.29), channel_id=1, source_target_pairs={{1,0},{2,1},{3,2},{5,4},{6,5},{7,6},{9,8},{10,9},{11,10},{13,12},{... | collective-permute-start | bytes 331784 | tf_op jit(solution)/shard_map/ppermute | solution.py:54
  29.0 6.7 %collective-permute-start.4 = (f32[3,72,128]{2,1,0:T(8,128)S(1)}, f32[3,72,128]{2,1,0:T(8,128)S(1)}, u32[]{:S(2)}, u32[]{:S(2)}) collective-permute-start(f32[3,72,128]{2,1,0:T(8,128)S(1)} %get-tuple-element.30), channel_id=1, source_target_pairs={{0,1},{1,2},{2,3},{4,5},{5,6},{6,7},{8,9},{9,10},{10,11},{12,13},{... | collective-permute-start | bytes 331784 | tf_op jit(solution)/shard_map/ppermute | solution.py:55
  52.9 4.3 %collective-permute-start.5 = (f32[5,40,128]{2,1,0:T(8,128)S(1)}, f32[5,40,128]{2,1,0:T(8,128)S(1)}, u32[]{:S(2)}, u32[]{:S(2)}) collective-permute-start(f32[5,40,128]{2,1,0:T(8,128)S(1)} %get-tuple-element.33), channel_id=1, source_target_pairs={{8,0},{16,8},{24,16},{9,1},{17,9},{25,17},{10,2},{18,10},{26,18},{... | collective-permute-start | bytes 307208 | tf_op jit(solution)/shard_map/ppermute | solution.py:54
  54.2 4.0 %collective-permute-start.6 = (f32[5,40,128]{2,1,0:T(8,128)S(1)}, f32[5,40,128]{2,1,0:T(8,128)S(1)}, u32[]{:S(2)}, u32[]{:S(2)}) collective-permute-start(f32[5,40,128]{2,1,0:T(8,128)S(1)} %get-tuple-element.34), channel_id=1, source_target_pairs={{0,8},{8,16},{16,24},{1,9},{9,17},{17,25},{2,10},{10,18},{18,26},{... | collective-permute-start | bytes 307208 | tf_op jit(solution)/shard_map/ppermute | solution.py:55
  58.4 5.8 %collective-permute-start.7 = (f32[5,40,128]{2,1,0:T(8,128)S(1)}, f32[5,40,128]{2,1,0:T(8,128)S(1)}, u32[]{:S(2)}, u32[]{:S(2)}) collective-permute-start(f32[5,40,128]{2,1,0:T(8,128)S(1)} %get-tuple-element.36), channel_id=1, source_target_pairs={{0,4},{4,0},{1,5},{5,1},{2,6},{6,2},{3,7},{7,3},{8,12},{12,8},{9,1... | collective-permute-start | bytes 307208 | tf_op jit(solution)/shard_map/ppermute | solution.py:53
  65.1 5.9 %collective-permute-start.8 = (f32[2,40,128]{2,1,0:T(8,128)S(1)}, f32[2,40,128]{2,1,0:T(8,128)S(1)}, u32[]{:S(2)}, u32[]{:S(2)}) collective-permute-start(f32[2,40,128]{2,1,0:T(8,128)S(1)} %get-tuple-element.38), channel_id=1, source_target_pairs={{1,0},{2,1},{3,2},{5,4},{6,5},{7,6},{9,8},{10,9},{11,10},{13,12},{... | collective-permute-start | bytes 122888 | tf_op jit(solution)/shard_map/ppermute | solution.py:54
  67.1 5.9 %collective-permute-start.9 = (f32[2,40,128]{2,1,0:T(8,128)S(1)}, f32[2,40,128]{2,1,0:T(8,128)S(1)}, u32[]{:S(2)}, u32[]{:S(2)}) collective-permute-start(f32[2,40,128]{2,1,0:T(8,128)S(1)} %get-tuple-element.39), channel_id=1, source_target_pairs={{0,1},{1,2},{2,3},{4,5},{5,6},{6,7},{8,9},{9,10},{10,11},{12,13},{... | collective-permute-start | bytes 122888 | tf_op jit(solution)/shard_map/ppermute | solution.py:55

commit v2 on v1

--- a/solution.py
+++ b/solution.py
@@ -25,7 +25,7 @@
     return jax.ShapeDtypeStruct(shape, jnp.float32)
 
 
-def call(body, name, ins, outs, scratch=(), alias=None, limit=None, out_specs=None):
+def call(body, name, ins, outs, scratch=(), alias=None, limit=None, out_specs=None, cost=1e8):
     return pl.pallas_call(
         body,
         name=name,
@@ -34,6 +34,7 @@
         out_shape=outs,
         scratch_shapes=list(scratch),
         input_output_aliases=alias or {},
+        cost_estimate=pl.CostEstimate(flops=int(cost), bytes_accessed=0, transcendentals=0),
         compiler_params=pltpu.CompilerParams(vmem_limit_bytes=limit),
     )(*ins)
 
@@ -47,43 +48,84 @@
     return i == 0, i == lax.axis_size(axis) - 1
 
 
+def paired(axis):
+    return axis != "gx"
+
+
 def exchange(msgs, axis):
     n = lax.axis_size(axis)
-    if n == 2:
-        return [lax.ppermute(msgs[0], axis, [(0, 1), (1, 0)])]
-    down = lax.ppermute(msgs[0], axis, [(i + 1, i) for i in range(n - 1)])
-    up = lax.ppermute(msgs[1], axis, [(i, i + 1) for i in range(n - 1)])
-    return [down, up]
+    if not paired(axis):
+        down = lax.ppermute(msgs[0], axis, [(i, (i - 1) % n) for i in range(n)])
+        up = lax.ppermute(msgs[1], axis, [(i, (i + 1) % n) for i in range(n)])
+        return [down, up]
+    found = [None] * len(msgs)
+    for phase in reversed(range(len(msgs))):
+        routes = []
+        for i in range(phase, n - 1, 2):
+            routes += [(i, i + 1), (i + 1, i)]
+        found[phase] = lax.ppermute(msgs[phase], axis, routes)
+    return found
 
 
 def emit(outs, index, axis, low, high):
-    if len(outs) == 1:
-        outs[0][index] = jnp.where(ends(axis)[0], high(), low())
+    if paired(axis):
+        even = lax.axis_index(axis) % 2 == 0
+        low, high = low(), high()
+        outs[0][index] = jnp.where(even, high, low)
+        if len(outs) > 1:
+            outs[1][index] = jnp.where(even, low, high)
     else:
         outs[0][index] = low()
         outs[1][index] = high()
 
 
 def arrived(refs, index, axis):
-    if len(refs) == 1:
-        value = refs[0][index]
-        first = ends(axis)[0]
-        zero = jnp.zeros_like(value)
-        return jnp.where(first, value, zero), jnp.where(first, zero, value)
-    return refs[0][index], refs[1][index]
+    a = refs[0][index]
+    b = refs[1][index] if len(refs) > 1 else jnp.zeros_like(a)
+    if paired(axis):
+        even = lax.axis_index(axis) % 2 == 0
+        return jnp.where(even, a, b), jnp.where(even, b, a)
+    first, last = ends(axis)
+    return jnp.where(last, 0.0, a), jnp.where(first, 0.0, b)
+
+
+def written(outs, index, axis):
+    a = outs[0][index]
+    b = outs[1][index] if len(outs) > 1 else jnp.zeros_like(a)
+    if paired(axis):
+        even = lax.axis_index(axis) % 2 == 0
+        return jnp.where(even, a, b), jnp.where(even, b, a)
+    return b, a
 
 
 def count(axis):
-    return 1 if lax.axis_size(axis) == 2 else 2
+    return 1 if paired(axis) and lax.axis_size(axis) == 2 else 2
 
 
 def turn(value, lanes):
     return pltpu.roll(value, lanes % LANES, 1)
 
 
-def build_body(start, right, se, re):
+def pack(outs, se, re, row, at_row, group, planes, ye, partial):
+    lane = iota((8, LANES), 1)
+    nt = se.shape[0] - 1
+    low, high = partial
+    for q in planes:
+        at = (q - group * PER) * SLOT
+        here = pl.ds(q * ye + row, 8)
+        one = turn(jnp.where(lane < 64, se[0, here, :], re[nt - 1, here, :]), at + G)
+        two = turn(jnp.where(lane < 64, re[0, here, :], se[nt - 1, here, :]), at)
+        low = jnp.where((lane >= at + G) & (lane < at + SLOT), one, low)
+        low = jnp.where((lane >= at) & (lane < at + G), two, low)
+        back = (lane - (at - F)) % LANES
+        high = jnp.where(back < F, two, high)
+        high = jnp.where((back >= F) & (back < SLOT), one, high)
+    emit(outs, (group, pl.ds(at_row, 8)), "gz", lambda: low, lambda: high)
+
+
+def build_body(start, right, se, re, *outs):
     nx, ny, nz = start.shape
-    ye = ny + 2 * O
+    xe, ye = nx + 2 * O, ny + 2 * O
 
     def plane(p, _):
         for t in range(nz // LANES):
@@ -94,10 +136,21 @@
 
     lax.fori_loop(0, nx, plane, 0, unroll=4)
 
+    def rows(r, _):
+        at = pl.multiple_of(r * 8, 8)
+        zero = jnp.zeros((8, LANES), jnp.float32)
+        for group in range(-(-xe // PER)):
+            planes = range(max(O, group * PER), min(O + nx, (group + 1) * PER))
+            pack(outs, se, re, at + O, at, group, planes, ye, (zero, zero))
+        return 0
+
+    lax.fori_loop(0, ny // 8, rows, 0)
+
 
 def xhalo_body(nx, ny, nz, nin, *refs):
     halo = refs[:nin]
-    se, re, outs = refs[nin + 2], refs[nin + 3], refs[nin + 4:]
+    outs = refs[nin + 2 + count("gz"):]
+    se, re, outs = outs[0], outs[1], outs[2:]
     xe, ye = nx + 2 * O, ny + 2 * O
     nt = nz // LANES
     for t in range(nt):
@@ -107,47 +160,72 @@
             dst, size, j = (se, F, k) if k < F else (re, G, k - F)
             dst[t, pl.ds((O + nx + j) * ye + O, ny), :] = high
             dst[t, pl.ds((O - size + j) * ye + O, ny), :] = low
-    for t in range(nt):
-        for k in range(SLOT):
-            src, size, j = (se, F, k) if k < F else (re, G, k - F)
-            emit(
-                outs, (k * nt + t,), "gy",
-                lambda: src[t, pl.ds(O + j, xe, stride=ye), :],
-                lambda: src[t, pl.ds(O + ny - size + j, xe, stride=ye), :],
-            )
-
-
-def yhalo_body(nx, ny, nz, nin, *refs):
+
+    def rows(r, _):
+        at = pl.multiple_of(r * 8, 8)
+        for group in range(-(-xe // PER)):
+            span = range(group * PER, min(xe, (group + 1) * PER))
+            planes = [q for q in span if O - F <= q < O or O + nx <= q < O + nx + F]
+            if planes:
+                high, low = written(outs, (group, pl.ds(at, 8)), "gz")
+                pack(outs, se, re, at + O, at, group, planes, ye, (low, high))
+        return 0
+
+    lax.fori_loop(0, ny // 8, rows, 0)
+
+
+def zhalo_body(nx, ny, nz, nin, *refs):
     halo = refs[:nin]
     se, re, outs = refs[nin + 2], refs[nin + 3], refs[nin + 4:]
     xe, ye = nx + 2 * O, ny + 2 * O
     nt = nz // LANES
-    for t in range(nt):
-        for k in range(SLOT):
-            high, low = arrived(halo, (k * nt + t,), "gy")
-            dst, size, j = (se, F, k) if k < F else (re, G, k - F)
+    lane = iota((8, LANES), 1)
+
+    def unpack(r, _):
+        at_row = pl.multiple_of(r * 8, 8)
+        for group in range(-(-xe // PER)):
+            high, low = arrived(halo, (group, pl.ds(at_row, 8)), "gz")
+            pick = lane % SLOT < G
+            one = jnp.where(pick, high, low)
+            two = jnp.where(pick, low, high)
+            one = jnp.where(lane >= LANES - F, low, one)
+            for j in range(min(PER, xe - group * PER)):
+                a = turn(one, -j * SLOT)
+                b = turn(two, -j * SLOT - G)
+                here = pl.ds((group * PER + j) * ye + at_row + O, 8)
+                se[nt, here, :] = jnp.where(lane < 64, b, a)
+                re[nt, here, :] = jnp.where(lane < 64, a, b)
+        return 0
+
+    lax.fori_loop(0, ny // 8, unpack, 0)
+    lane = iota((xe, LANES), 1)
+    extra_low = extra_high = jnp.zeros((xe, LANES), jnp.float32)
+    for k in range(SLOT):
+        src, size, j = (se, F, k) if k < F else (re, G, k - F)
+        for t in range(nt + 1):
+            low = src[t, pl.ds(O + j, xe, stride=ye), :]
+            high = src[t, pl.ds(O + ny - size + j, xe, stride=ye), :]
+            if t < nt:
+                emit(outs, (k * nt + t,), "gy", lambda: low, lambda: high)
+            else:
+                here = (lane >= 8 * k) & (lane < 8 * k + 2 * F)
+                extra_low = jnp.where(here, turn(low, 8 * k + F), extra_low)
+                extra_high = jnp.where(here, turn(high, 8 * k + F), extra_high)
+    emit(outs, (SLOT * nt,), "gy", lambda: extra_low, lambda: extra_high)
+
+
+def place_y(halo, se, re, nx, ny):
+    xe, ye = nx + 2 * O, ny + 2 * O
+    nt = se.shape[0] - 1
+    for k in range(SLOT):
+        dst, size, j = (se, F, k) if k < F else (re, G, k - F)
+        for t in range(nt + 1):
+            if t < nt:
+                high, low = arrived(halo, (k * nt + t,), "gy")
+            else:
+                high, low = (turn(v, -8 * k - F) for v in arrived(halo, (SLOT * nt,), "gy"))
             dst[t, pl.ds(O + ny + j, xe, stride=ye), :] = high
             dst[t, pl.ds(O - size + j, xe, stride=ye), :] = low
-    lane = iota((8, LANES), 1)
-
-    def rows(r, _):
-        base = pl.multiple_of(r * 8, 8)
-        for group in range(-(-xe // PER)):
-            low = jnp.zeros((8, LANES), jnp.float32)
-            high = low
-            for j in range(min(PER, xe - group * PER)):
-                at = j * SLOT
-                here = pl.ds((group * PER + j) * ye + base, 8)
-                in_s = (lane >= at) & (lane < at + F)
-                in_r = (lane >= at + F) & (lane < at + SLOT)
-                low = jnp.where(in_s, turn(se[0, here, :], at), low)
-                low = jnp.where(in_r, turn(re[0, here, :], at + F), low)
-                high = jnp.where(in_s, turn(se[nt - 1, here, :], at + F), high)
-                high = jnp.where(in_r, turn(re[nt - 1, here, :], at + SLOT), high)
-            emit(outs, (group, pl.ds(base, 8)), "gz", lambda: low, lambda: high)
-        return 0
-
-    lax.fori_loop(0, ye // 8, rows, 0)
 
 
 def inside(shape, dim, offset, cells, axis):
@@ -181,25 +259,25 @@
     centre = [at(planes[0], t) for t in range(total)]
     for p in planes:
         after = [at(p + 1, t) for t in range(total)]
-        left = [turn(c, 1) for c in centre]
-        right = [turn(c, -1) for c in centre]
         for t in range(tiles):
-            near = jnp.where(lane == 0, left[t - 1], left[t])
-            near = near + jnp.where(lane == LANES - 1, right[(t + 1) % total], right[t])
+            wrapped = jnp.where(lane == LANES - 1, centre[t - 1], centre[t])
+            near = turn(wrapped, 1)
+            wrapped = jnp.where(lane == 0, centre[(t + 1) % total], centre[t])
+            near = near + turn(wrapped, -1)
             near = near + (at(p, t, -1) + at(p, t, 1))
             near = near + (before[t] + after[t])
             use(p, t, centre[t], near)
         before, centre = centre, after
 
 
-def sweep(src, dst, right, mask, nx, low, high):
+def sweep(src, dst, right, mask, nx, low, high, tiles):
     total, ye, _ = mask.shape
     first, last = ends("gx")
     up = jnp.where(last, 0.0, 1.0)
     down = jnp.where(first, 0.0, 1.0)
 
     def rows(r, _):
-        base = pl.multiple_of(r * 8, 8)
+        base = tiles[1](r)
         m = [mask[t, pl.ds(base, 8), :] for t in range(total)]
 
         def use(p, t, centre, near):
@@ -210,65 +288,15 @@
         stencil(src, ye, base, range(-low, nx + high), total, use)
         return 0
 
-    lax.fori_loop(0, ye // 8, rows, 0)
-
-
-def split_dot(value, weight):
-    high = value.astype(jnp.bfloat16)
-    rest = value - high.astype(jnp.float32)
-    mid = rest.astype(jnp.bfloat16)
-    small = (rest - mid.astype(jnp.float32)).astype(jnp.bfloat16)
-    dot = functools.partial(jnp.dot, preferred_element_type=jnp.float32)
-    return dot(high, weight) + dot(mid, weight) + dot(small, weight)
-
-
-def lane_dot(src, src_at, dst, dst_at, rows, weight):
-    step = max(s for s in range(8, 273, 8) if rows % s == 0)
-    for at in range(0, rows, step):
-        value = jnp.concatenate([src[t, pl.ds(src_at + at, step), :] for t in range(weight.shape[0] // LANES)], axis=1)
-        got = split_dot(value, weight)
-        for t in range(weight.shape[1] // LANES):
-            dst[t, pl.ds(dst_at + at, step), :] = got[:, t * LANES:(t + 1) * LANES]
-
-
-def transfer_weights(fine, coarse, halo, fine_dim, inner, outer):
-    shape = (fine, coarse + halo) if fine_dim == 0 else (coarse + halo, fine)
-    z = iota(shape, fine_dim)
-    k = iota(shape, 1 - fine_dim)
-    k = jnp.where(k >= coarse, k - (coarse + halo), k)
-    off = z - 2 * k
-    weight = jnp.where(off == 1, inner, jnp.where((off == 0) | (off == 2), outer, 0.0))
-    return jnp.where(k < -1, 0.0, weight).astype(jnp.bfloat16)
-
-
-def smooth_body(nx, ny, nz, nin, *refs):
-    halo = refs[:nin]
-    se, re, s2, coarse = refs[nin + 2:nin + 6]
-    outs = refs[nin + 6:-4]
-    s1, rx, ry, mask = refs[-4:]
-    xe, ye = nx + 2 * O, ny + 2 * O
-    nt = nz // LANES
-    lane = iota((8, LANES), 1)
-
-    def unpack(r, _):
-        base = pl.multiple_of(r * 8, 8)
-        for group in range(-(-xe // PER)):
-            high, low = arrived(halo, (group, pl.ds(base, 8)), "gz")
-            for j in range(min(PER, xe - group * PER)):
-                at = j * SLOT
-                here = pl.ds((group * PER + j) * ye + base, 8)
-                se[nt, here, :] = jnp.where(lane < 64, turn(high, -at), turn(low, -F - at))
-                re[nt, here, :] = jnp.where(lane < 64, turn(high, -at - F), turn(low, -G - at - F))
-        return 0
-
-    lax.fori_loop(0, ye // 8, unpack, 0)
-    fill_mask(mask, ny)
-    sweep(se, s1, re, mask, nx, 2, 2)
-    sweep(s1, s2, re, mask, nx, 1, 1)
-
-    def restrict_x(r, _):
-        base = r * 8 + O
-        at = pl.multiple_of(r * 8, 8)
+    lax.fori_loop(0, tiles[0], rows, 0)
+
+
+def residual_x(s2, re, rx, nx, ny, tiles):
+    ye = ny + 2 * O
+
+    def rows(r, _):
+        base = tiles[1](r)
+        at = base - O
         quarter, half = {}, {}
 
         def use(p, t, centre, near):
@@ -283,10 +311,63 @@
             rx[t, pl.ds((p // 2) * ny + at, 8), :] = part
             quarter[t] = value
 
-        stencil(s2, ye, base, range(nx), nt, use)
-        return 0
-
-    lax.fori_loop(0, ny // 8, restrict_x, 0)
+        stencil(s2, ye, base, range(nx), rx.shape[0], use)
+        return 0
+
+    lax.fori_loop(0, tiles[0], rows, 0)
+
+
+def every(ye):
+    return ye // 8, lambda r: pl.multiple_of(r * 8, 8)
+
+
+def split_dot(value, weight):
+    high = value.astype(jnp.bfloat16)
+    rest = value - high.astype(jnp.float32)
+    mid = rest.astype(jnp.bfloat16)
+    small = (rest - mid.astype(jnp.float32)).astype(jnp.bfloat16)
+    dot = functools.partial(jnp.dot, preferred_element_type=jnp.float32)
+    return dot(high, weight) + dot(mid, weight) + dot(small, weight)
+
+
+def lane_dot(src, src_at, dst, dst_at, rows, weight):
+    step = max(s for s in range(8, 273, 8) if rows % s == 0)
+    for at in range(0, rows, step):
+        value = jnp.concatenate([src[t, pl.ds(src_at + at, step), :] for t in range(weight.shape[0] // LANES)], axis=1)
+        got = split_dot(value, weight)
+        for t in range(weight.shape[1] // LANES):
+            dst[t, pl.ds(dst_at + at, step), :] = got[:, t * LANES:(t + 1) * LANES]
+
+
+def transfer_weights(fine, coarse, halo, fine_dim, inner, outer):
+    shape = (fine, coarse + halo) if fine_dim == 0 else (coarse + halo, fine)
+    z = iota(shape, fine_dim)
+    k = iota(shape, 1 - fine_dim)
+    k = jnp.where(k >= coarse, k - (coarse + halo), k)
+    off = z - 2 * k
+    weight = jnp.where(off == 1, inner, jnp.where((off == 0) | (off == 2), outer, 0.0))
+    return jnp.where(k < -1, 0.0, weight).astype(jnp.bfloat16)
+
+
+def inner_body(nx, ny, nz, se, re, s1, s2, rx, mask):
+    fill_mask(mask, ny)
+    many = ny // 8 - 1
+    sweep(se, s1, re, mask, nx, 2, 2, (many, lambda r: pl.multiple_of(r * 8 + 8, 8)))
+    sweep(s1, s2, re, mask, nx, 1, 1, (many, lambda r: jnp.minimum(r * 8 + 9, ny - 9)))
+    residual_x(s2, re, rx, nx, ny, (many, lambda r: O + jnp.minimum(r * 8 + 6, ny - 14)))
+
+
+def outer_body(nx, ny, nz, nin, *refs):
+    halo = refs[:nin]
+    se, re, s1, s2, rx, coarse = refs[nin + 5:nin + 11]
+    outs = refs[nin + 11:-2]
+    ry, mask = refs[-2:]
+    nt = nz // LANES
+    place_y(halo, se, re, nx, ny)
+    fill_mask(mask, ny)
+    sweep(se, s1, re, mask, nx, 2, 2, (2, lambda r: pl.multiple_of(r * ny, 8)))
+    sweep(s1, s2, re, mask, nx, 1, 1, (2, lambda r: r * (ny - 2) + 1))
+    residual_x(s2, re, rx, nx, ny, (2, lambda r: O + r * (ny - 8)))
 
     cx, cy, cz = nx // 2, ny // 2, nz // 2
     ct = cz // LANES
@@ -444,9 +525,9 @@
         return 0
 
     lax.fori_loop(0, ye // 8, unpack, 0)
-    sweep(ca, cb, coarse, mask, cx, 3, 2)
-    sweep(cb, ca, coarse, mask, cx, 2, 1)
-    sweep(ca, cb, coarse, mask, cx, 1, 0)
+    sweep(ca, cb, coarse, mask, cx, 3, 2, every(ye))
+    sweep(cb, ca, coarse, mask, cx, 2, 1, every(ye))
+    sweep(ca, cb, coarse, mask, cx, 1, 0, every(ye))
     lane_dot(cb, (O - 1) * ye, fine, 0, (cx + 1) * ye, transfer_weights(nz, cz, LANES, 1, 1.0, 0.5))
 
     chunks = sems.shape[0]
@@ -497,35 +578,36 @@
 
     to_prev = jnp.concatenate([start[:F], right[:G]], axis=0)
     to_next = jnp.concatenate([start[nx - F:], right[nx - G:]], axis=0)
-    if count("gx") == 1:
-        to_prev = jnp.where(ends("gx")[0], to_next, to_prev)
     halo = exchange([to_prev, to_next], "gx")
-    se, re = call(build_body, "build", [start, right], [big, big], limit=8 * mb)
-
+    face = [f32(-(-xe // PER), ny, LANES)] * count("gz")
+    se, re, *msgs = call(build_body, "build", [start, right], [big, big] + face, limit=8 * mb)
+
+    n = len(halo)
+    alias = {n + i: i for i in range(2 + len(msgs))}
+    se, re, *msgs = call(
+        functools.partial(xhalo_body, nx, ny, nz, n), "xhalo", [*halo, se, re, *msgs],
+        [big, big] + face, alias=alias, limit=8 * mb,
+    )
+    halo = exchange(msgs, "gz")
     n = len(halo)
     se, re, *msgs = call(
-        functools.partial(xhalo_body, nx, ny, nz, n), "xhalo", [*halo, se, re],
-        [big, big] + [f32(SLOT * nt, xe, LANES)] * count("gy"), alias={n: 0, n + 1: 1}, limit=8 * mb,
+        functools.partial(zhalo_body, nx, ny, nz, n), "zhalo", [*halo, se, re],
+        [big, big] + [f32(SLOT * nt + 1, xe, LANES)] * count("gy"), alias={n: 0, n + 1: 1}, limit=8 * mb,
     )
     halo = exchange(msgs, "gy")
-    n = len(halo)
-    se, re, *msgs = call(
-        functools.partial(yhalo_body, nx, ny, nz, n), "yhalo", [*halo, se, re],
-        [big, big] + [f32(-(-xe // PER), ye, LANES)] * count("gz"), alias={n: 0, n + 1: 1}, limit=8 * mb,
-    )
-    halo = exchange(msgs, "gz")
+    part = f32(nt, (cx + 1) * ny + 8, LANES)
+    masks = pltpu.VMEM((nt + 1, ye, LANES), jnp.float32)
+    s1, s2, rx = call(
+        functools.partial(inner_body, nx, ny, nz), "inner", [se, re], [big, big, part], scratch=[masks],
+        limit=8 * mb, cost=9e9,
+    )
     n = len(halo)
     small = f32(ct + 1, cxe * cye, LANES)
-    se, re, s2, coarse, *msgs = call(
-        functools.partial(smooth_body, nx, ny, nz, n), "smooth", [*halo, se, re],
-        [big, big, big, small] + [f32(CL * ct + 1, cye, LANES)] * count("gx"),
-        scratch=[
-            pltpu.VMEM((nt + 1, xe * ye, LANES), jnp.float32),
-            pltpu.VMEM((nt, (cx + 1) * ny + 8, LANES), jnp.float32),
-            pltpu.VMEM((nt, (cx + 1) * cye, LANES), jnp.float32),
-            pltpu.VMEM((nt + 1, ye, LANES), jnp.float32),
-        ],
-        alias={n: 0, n + 1: 1}, limit=24 * mb,
+    se, re, s1, s2, rx, coarse, *msgs = call(
+        functools.partial(outer_body, nx, ny, nz, n), "outer", [*halo, se, re, s1, s2, rx],
+        [big, big, big, big, part, small] + [f32(CL * ct + 1, cye, LANES)] * count("gx"),
+        scratch=[pltpu.VMEM((nt, (cx + 1) * cye, LANES), jnp.float32), masks],
+        alias={n + i: i for i in range(5)}, limit=8 * mb,
     )
     halo = exchange(msgs, "gx")
     n = len(halo)
@@ -552,7 +634,7 @@
             pltpu.VMEM((nt, nx, ny, LANES), jnp.float32),
             pltpu.SemaphoreType.DMA((8, nt)),
         ],
-        alias={n + 1: 0}, limit=24 * mb, out_specs=[VMEM, ANY],
+        alias={n + 1: 0}, limit=12 * mb, out_specs=[VMEM, ANY],
     )
     return out
 

time: 81.9 us -> 63.3 us (0.77); the launches traced: 80.3 us -> 63.1 us
  starting transfers between devices: 23.5 us -> 9.34 us
  Pallas kernels: 30 us -> 27.5 us
    ppermute x10, starting transfers between devices: 23.5 us -> 9.34 us  [the longest x6 7.75 us: exchange(): found[phase] = lax.ppermute(msgs[phase], axis, routes)]
    pallas_call x7 -> x8, Pallas kernels: 30 us -> 27.5 us  [call(): pl.pallas_call(body, name=name, in_specs=[VMEM] * len(ins), out_specs=[VM...]
  transfers between devices with their start and end apart: 10 -> 10, of which waited for: 6 -> 9; matrix products, arithmetic and copies ran while one was open for 0% -> 0% of each run, Pallas kernels for 1% -> 19%
where the time goes in v2:
time: 63.3 us; the launch traced here: 63.1 us
  Pallas kernels  27.5 us (43%)
  waiting for transfers between devices  19.7 us (31%)
  starting transfers between devices  9.34 us (15%)
  local copies, waits for them, and re-layouts  6.41 us (10%)
    pallas_call x8, Pallas kernels, call(): pl.pallas_call(body, name=name, in_specs=[VMEM] * len(ins), out_specs=[VM...  27.5 us
    ppermute x6, waiting for transfers between devices, exchange(): found[phase] = lax.ppermute(msgs[phase], axis, routes)  12.8 us
    ppermute x6, starting transfers between devices, exchange(): found[phase] = lax.ppermute(msgs[phase], axis, routes)  7.75 us
    unnamed x4, local copies, waits for them, and re-layouts  4.37 us
    ppermute x2, waiting for transfers between devices, exchange(): up = lax.ppermute(msgs[1], axis, [(i, (i + 1) % n) for i in range(n)])  3.97 us
    ppermute x2, waiting for transfers between devices, exchange(): down = lax.ppermute(msgs[0], axis, [(i, (i - 1) % n) for i in range(n)])  2.88 us
    slice x2, local copies, waits for them, and re-layouts, on_device(): to_next = jnp.concatenate([start[nx - F:], right[nx - G:]], axis=0)  2.04 us
  transfers between devices with their start and end apart: 10, of which 9 were waited for; matrix products, arithmetic and copies ran while one was open for 0% of the time, Pallas kernels for 19%

profile of v2, /device:TPU:16, one launch (start us, length us, event | category | flops | bytes accessed | tf_op | source)
XLA Modules:
  0.0 63.1 jit_solution(760135370782362524)
XLA Ops:
  0.0 1.0 %fusion.1 = (f32[2,64,256]{2,1,0:T(8,128)S(1)}, f32[2,64,256]{2,1,0:T(8,128)S(1)}) fusion(f32[64,64,256]{2,1,0:T(8,128)} %right.1), kind=kLoop, calls=%fused_computation.3 | loop fusion | bytes 524288 | tf_op jit(solution)/shard_map/slice | solution.py:580
  1.0 1.1 %fusion = (f32[3,64,256]{2,1,0:T(8,128)S(1)}, f32[3,64,256]{2,1,0:T(8,128)S(1)}) fusion(f32[64,64,256]{2,1,0:T(8,128)} %start.1), kind=kLoop, calls=%fused_computation.2 | loop fusion | bytes 786432 | tf_op jit(solution)/shard_map/slice | solution.py:580
  2.1 1.0 %collective-permute-start = (f32[5,64,256]{2,1,0:T(8,128)S(1)}, f32[5,64,256]{2,1,0:T(8,128)S(1)}, u32[]{:S(2)}, u32[]{:S(2)}) collective-permute-start(f32[5,64,256]{2,1,0:T(8,128)S(1)} %pad_maximum_fusion), channel_id=1, source_target_pairs={{0,24},{8,0},{16,8},{24,16},{1,25},{9,1},{17,9},{25,17},{2,26},{10... | collective-permute-start | bytes 983048 | tf_op jit(solution)/shard_map/ppermute | solution.py:58
  3.1 0.1 collective-permute-start.1
  3.2 0.0 copy-start
  3.2 2.2 %copy-done = f32[64,64,256]{2,1,0:T(8,128)S(1)} copy-done((f32[64,64,256]{2,1,0:T(8,128)S(1)}, f32[64,64,256]{2,1,0:T(8,128)}, u32[]{:S(2)}) %copy-start) | copy-done | bytes 4194328
  5.3 0.0 copy-start.1
  5.3 2.2 %copy-done.1 = f32[64,64,256]{2,1,0:T(8,128)S(1)} copy-done((f32[64,64,256]{2,1,0:T(8,128)S(1)}, f32[64,64,256]{2,1,0:T(8,128)}, u32[]{:S(2)}) %copy-start.1) | copy-done | bytes 4194328
  7.5 2.5 %build.1 = (f32[3,5184,128]{2,1,0:T(8,128)S(1)}, f32[3,5184,128]{2,1,0:T(8,128)S(1)}, f32[3,64,128]{2,1,0:T(8,128)S(1)}, f32[3,64,128]{2,1,0:T(8,128)S(1)}) custom-call(f32[64,64,256]{2,1,0:T(8,128)S(1)} %copy-done, f32[64,64,256]{2,1,0:T(8,128)S(1)} %copy-done.1), custom_call_target="tpu_custom_call" | custom-call | flops 100000000 | tf_op jit(solution)/shard_map/build/pallas_call | solution.py:29
  10.0 1.1 %collective-permute-done.refs_0_ = f32[5,64,256]{2,1,0:T(8,128)S(1)} collective-permute-done((f32[5,64,256]{2,1,0:T(8,128)S(1)}, f32[5,64,256]{2,1,0:T(8,128)S(1)}, u32[]{:S(2)}, u32[]{:S(2)}) %collective-permute-start) | collective-permute-done | bytes 327712 | tf_op jit(solution)/shard_map/ppermute | solution.py:58
  11.1 1.1 %collective-permute-done.1.refs_1_ = f32[5,64,256]{2,1,0:T(8,128)S(1)} collective-permute-done((f32[5,64,256]{2,1,0:T(8,128)S(1)}, f32[5,64,256]{2,1,0:T(8,128)S(1)}, u32[]{:S(2)}, u32[]{:S(2)}) %collective-permute-start.1) | collective-permute-done | bytes 327712 | tf_op jit(solution)/shard_map/ppermute | solution.py:59
  12.2 0.8 %xhalo.1 = (f32[3,5184,128]{2,1,0:T(8,128)S(1)}, f32[3,5184,128]{2,1,0:T(8,128)S(1)}, f32[3,64,128]{2,1,0:T(8,128)S(1)}, f32[3,64,128]{2,1,0:T(8,128)S(1)}) custom-call(f32[5,64,256]{2,1,0:T(8,128)S(1)} %collective-permute-done.refs_0_, ...), custom_call_target="tpu_custom_call", output_to_operand_aliasing={{0}: (2, {}), {1}: (3, {}), {2}: (4, {}), {3}: (5, {})} | custom-call | flops 100000000 | tf_op jit(solution)/shard_map/xhalo/pallas_call | solution.py:29
  13.0 1.6 %collective-permute-start.2 = (f32[3,64,128]{2,1,0:T(8,128)S(1)}, f32[3,64,128]{2,1,0:T(8,128)S(1)}, u32[]{:S(2)}, u32[]{:S(2)}) collective-permute-start(f32[3,64,128]{2,1,0:T(8,128)S(1)} %get-tuple-element.33), channel_id=1, source_target_pairs={{0,1},{1,0},{2,3},{3,2},{4,5},{5,4},{6,7},{7,6},{8,9},{9,8},{10,11... | collective-permute-start | bytes 294920 | tf_op jit(solution)/shard_map/ppermute | solution.py:66
  14.6 1.9 %collective-permute-start.3 = (f32[3,64,128]{2,1,0:T(8,128)S(1)}, f32[3,64,128]{2,1,0:T(8,128)S(1)}, u32[]{:S(2)}, u32[]{:S(2)}) collective-permute-start(f32[3,64,128]{2,1,0:T(8,128)S(1)} %get-tuple-element.34), channel_id=1, source_target_pairs={{1,2},{2,1},{5,6},{6,5},{9,10},{10,9},{13,14},{14,13},{17,18},{18,... | collective-permute-start | bytes 294920 | tf_op jit(solution)/shard_map/ppermute | solution.py:66
  16.5 1.1 %collective-permute-done.2.refs_0_ = f32[3,64,128]{2,1,0:T(8,128)S(1)} collective-permute-done((f32[3,64,128]{2,1,0:T(8,128)S(1)}, f32[3,64,128]{2,1,0:T(8,128)S(1)}, u32[]{:S(2)}, u32[]{:S(2)}) %collective-permute-start.2) | collective-permute-done | bytes 98336 | tf_op jit(solution)/shard_map/ppermute | solution.py:66
  17.6 3.5 %collective-permute-done.3.refs_1_ = f32[3,64,128]{2,1,0:T(8,128)S(1)} collective-permute-done((f32[3,64,128]{2,1,0:T(8,128)S(1)}, f32[3,64,128]{2,1,0:T(8,128)S(1)}, u32[]{:S(2)}, u32[]{:S(2)}) %collective-permute-start.3) | collective-permute-done | bytes 98336 | tf_op jit(solution)/shard_map/ppermute | solution.py:66
  21.1 2.1 %zhalo.1 = (f32[3,5184,128]{2,1,0:T(8,128)S(1)}, f32[3,5184,128]{2,1,0:T(8,128)S(1)}, f32[11,72,128]{2,1,0:T(8,128)S(1)}) custom-call(f32[3,64,128]{2,1,0:T(8,128)S(1)} %collective-permute-done.2.refs_0_, f32[3,64,128]{2,1,0:T(8,128)S(1)} %collective-permute-done.3.refs_1_, ...), custom_call_target="tpu_custom_call", output_to_operand_aliasing={{0}: (2, {}), {1}: (3, {})} | custom-call | flops 100000000 | tf_op jit(solution)/shard_map/zhalo/pallas_call | solution.py:29
  23.2 1.6 %collective-permute-start.4 = (f32[11,72,128]{2,1,0:T(8,128)S(1)}, f32[11,72,128]{2,1,0:T(8,128)S(1)}, u32[]{:S(2)}, u32[]{:S(2)}) collective-permute-start(f32[11,72,128]{2,1,0:T(8,128)S(1)} %get-tuple-element.37), channel_id=1, source_target_pairs={{0,4},{4,0},{1,5},{5,1},{2,6},{6,2},{3,7},{7,3},{8,12},{12,8},{9,1... | collective-permute-start | bytes 1216520 | tf_op jit(solution)/shard_map/ppermute | solution.py:66
  24.8 9.5 %inner.1 = (f32[3,5184,128]{2,1,0:T(8,128)S(1)}, f32[3,5184,128]{2,1,0:T(8,128)S(1)}, f32[2,2120,128]{2,1,0:T(8,128)S(1)}) custom-call(f32[3,5184,128]{2,1,0:T(8,128)S(1)} %get-tuple-element.38.se.refs_1_, f32[3,5184,128]{2,1,0:T(8,128)S(1)} %get-tuple-element.39.re.refs_2_), custom_call_target="tpu_custom_call" | custom-call | flops 8999999488 | tf_op jit(solution)/shard_map/inner/pallas_call | solution.py:29
  34.3 0.0 collective-permute-done.4.refs_0_
  34.3 4.2 %outer.1 = (f32[3,5184,128]{2,1,0:T(8,128)S(1)}, f32[3,5184,128]{2,1,0:T(8,128)S(1)}, f32[3,5184,128]{2,1,0:T(8,128)S(1)}, f32[3,5184,128]{2,1,0:T(8,128)S(1)}, ...) custom-call(f32[11,72,128]{2,1,0:T(8,128)S(1)} %collective-permute-d, ...), custom_call_target="tpu_custom_call", output_to_operand_aliasing={{0}: (1, {}), {1}: (2, {}), {2}: (3, {}), {3}: (4, {}), {4}... | custom-call | flops 100000000 | tf_op jit(solution)/shard_map/outer/pallas_call | solution.py:29
  38.5 0.1 collective-permute-start.5
  38.6 0.5 collective-permute-start.6
  39.1 1.8 %collective-permute-done.5.refs_0_ = f32[5,40,128]{2,1,0:T(8,128)S(1)} collective-permute-done((f32[5,40,128]{2,1,0:T(8,128)S(1)}, f32[5,40,128]{2,1,0:T(8,128)S(1)}, u32[]{:S(2)}, u32[]{:S(2)}) %collective-permute-start.5) | collective-permute-done | bytes 102432 | tf_op jit(solution)/shard_map/ppermute | solution.py:58
  40.9 2.9 %collective-permute-done.6.refs_1_ = f32[5,40,128]{2,1,0:T(8,128)S(1)} collective-permute-done((f32[5,40,128]{2,1,0:T(8,128)S(1)}, f32[5,40,128]{2,1,0:T(8,128)S(1)}, u32[]{:S(2)}, u32[]{:S(2)}) %collective-permute-start.6) | collective-permute-done | bytes 102432 | tf_op jit(solution)/shard_map/ppermute | solution.py:59
  43.8 0.2 coarse_x.1
  44.0 0.6 collective-permute-start.7
  44.6 4.3 %collective-permute-done.7.refs_0_ = f32[5,40,128]{2,1,0:T(8,128)S(1)} collective-permute-done((f32[5,40,128]{2,1,0:T(8,128)S(1)}, f32[5,40,128]{2,1,0:T(8,128)S(1)}, u32[]{:S(2)}, u32[]{:S(2)}) %collective-permute-start.7) | collective-permute-done | bytes 102432 | tf_op jit(solution)/shard_map/ppermute | solution.py:66
  48.9 0.9 %coarse_y.1 = (f32[2,1600,128]{2,1,0:T(8,128)S(1)}, f32[2,40,128]{2,1,0:T(8,128)S(1)}, f32[2,40,128]{2,1,0:T(8,128)S(1)}) custom-call(f32[5,40,128]{2,1,0:T(8,128)S(1)} %collective-permute-done.7.refs_0_, f32[2,1600,128]{2,1,0:T(8,128)S(1)} %get-tuple-element.47.refs_1_), custom_call_target="tpu_custom_call", output_to_operand_aliasing={{0}: (1, {})} | custom-call | flops 100000000 | tf_op jit(solution)/shard_map/coarse_y/pallas_call | solution.py:29
  49.8 0.1 collective-permute-start.8
  49.9 2.0 %collective-permute-start.9 = (f32[2,40,128]{2,1,0:T(8,128)S(1)}, f32[2,40,128]{2,1,0:T(8,128)S(1)}, u32[]{:S(2)}, u32[]{:S(2)}) collective-permute-start(f32[2,40,128]{2,1,0:T(8,128)S(1)} %get-tuple-element.49), channel_id=1, source_target_pairs={{1,2},{2,1},{5,6},{6,5},{9,10},{10,9},{13,14},{14,13},{17,18},{18,... | collective-permute-start | bytes 122888 | tf_op jit(solution)/shard_map/ppermute | solution.py:66
  51.9 2.0 %collective-permute-done.8.refs_0_ = f32[2,40,128]{2,1,0:T(8,128)S(1)} collective-permute-done((f32[2,40,128]{2,1,0:T(8,128)S(1)}, f32[2,40,128]{2,1,0:T(8,128)S(1)}, u32[]{:S(2)}, u32[]{:S(2)}) %collective-permute-start.8) | collective-permute-done | bytes 40992 | tf_op jit(solution)/shard_map/ppermute | solution.py:66
  53.9 1.9 %collective-permute-done.9.refs_1_ = f32[2,40,128]{2,1,0:T(8,128)S(1)} collective-permute-done((f32[2,40,128]{2,1,0:T(8,128)S(1)}, f32[2,40,128]{2,1,0:T(8,128)S(1)}, u32[]{:S(2)}, u32[]{:S(2)}) %collective-permute-start.9) | collective-permute-done | bytes 40992 | tf_op jit(solution)/shard_map/ppermute | solution.py:66
  55.8 7.3 %finish.1 = (f32[2,1600,128]{2,1,0:T(8,128)S(1)}, f32[64,64,256]{2,1,0:T(8,128)}) custom-call(f32[2,40,128]{2,1,0:T(8,128)S(1)} %collective-permute-done.8.refs_0_, f32[2,40,128]{2,1,0:T(8,128)S(1)} %collective-permute-done.9.refs_1_, f32[3,5184,128]{2,1,0:T(8,128)S(1)} %get-tuple-element.50.refs_2_, ...), custom_call_target="tpu_custom_call", output_to_operand_aliasing={{0}: (3, {})} | custom-call | flops 100000000 | tf_op jit(solution)/shard_map/finish/pallas_call | solution.py:29
  (2 shorter events, 0.0 us)
Async XLA Ops:
  2.1 9.0 %collective-permute-start = (f32[5,64,256]{2,1,0:T(8,128)S(1)}, f32[5,64,256]{2,1,0:T(8,128)S(1)}, u32[]{:S(2)}, u32[]{:S(2)}) collective-permute-start(f32[5,64,256]{2,1,0:T(8,128)S(1)} %pad_maximum_fusion), channel_id=1, source_target_pairs={{0,24},{8,0},{16,8},{24,16},{1,25},{9,1},{17,9},{25,17},{2,26},{10... | collective-permute-start | bytes 983048 | tf_op jit(solution)/shard_map/ppermute | solution.py:58
  3.1 9.1 %collective-permute-start.1 = (f32[5,64,256]{2,1,0:T(8,128)S(1)}, f32[5,64,256]{2,1,0:T(8,128)S(1)}, u32[]{:S(2)}, u32[]{:S(2)}) collective-permute-start(f32[5,64,256]{2,1,0:T(8,128)S(1)} %pad_maximum_fusion.1), channel_id=1, source_target_pairs={{0,8},{8,16},{16,24},{24,0},{1,9},{9,17},{17,25},{25,1},{2,10},{10... | collective-permute-start | bytes 983048 | tf_op jit(solution)/shard_map/ppermute | solution.py:59
  3.2 2.2 %copy-start = (f32[64,64,256]{2,1,0:T(8,128)S(1)}, f32[64,64,256]{2,1,0:T(8,128)}, u32[]{:S(2)}) copy-start(f32[64,64,256]{2,1,0:T(8,128)} %start.1) | copy-start | bytes 12582916
  5.3 2.2 %copy-start.1 = (f32[64,64,256]{2,1,0:T(8,128)S(1)}, f32[64,64,256]{2,1,0:T(8,128)}, u32[]{:S(2)}) copy-start(f32[64,64,256]{2,1,0:T(8,128)} %right.1) | copy-start | bytes 12582916
  13.0 4.7 %collective-permute-start.2 = (f32[3,64,128]{2,1,0:T(8,128)S(1)}, f32[3,64,128]{2,1,0:T(8,128)S(1)}, u32[]{:S(2)}, u32[]{:S(2)}) collective-permute-start(f32[3,64,128]{2,1,0:T(8,128)S(1)} %get-tuple-element.33), channel_id=1, source_target_pairs={{0,1},{1,0},{2,3},{3,2},{4,5},{5,4},{6,7},{7,6},{8,9},{9,8},{10,11... | collective-permute-start | bytes 294920 | tf_op jit(solution)/shard_map/ppermute | solution.py:66
  14.6 6.5 %collective-permute-start.3 = (f32[3,64,128]{2,1,0:T(8,128)S(1)}, f32[3,64,128]{2,1,0:T(8,128)S(1)}, u32[]{:S(2)}, u32[]{:S(2)}) collective-permute-start(f32[3,64,128]{2,1,0:T(8,128)S(1)} %get-tuple-element.34), channel_id=1, source_target_pairs={{1,2},{2,1},{5,6},{6,5},{9,10},{10,9},{13,14},{14,13},{17,18},{18,... | collective-permute-start | bytes 294920 | tf_op jit(solution)/shard_map/ppermute | solution.py:66
  23.2 11.1 %collective-permute-start.4 = (f32[11,72,128]{2,1,0:T(8,128)S(1)}, f32[11,72,128]{2,1,0:T(8,128)S(1)}, u32[]{:S(2)}, u32[]{:S(2)}) collective-permute-start(f32[11,72,128]{2,1,0:T(8,128)S(1)} %get-tuple-element.37), channel_id=1, source_target_pairs={{0,4},{4,0},{1,5},{5,1},{2,6},{6,2},{3,7},{7,3},{8,12},{12,8},{9,1... | collective-permute-start | bytes 1216520 | tf_op jit(solution)/shard_map/ppermute | solution.py:66
  38.5 2.4 %collective-permute-start.5 = (f32[5,40,128]{2,1,0:T(8,128)S(1)}, f32[5,40,128]{2,1,0:T(8,128)S(1)}, u32[]{:S(2)}, u32[]{:S(2)}) collective-permute-start(f32[5,40,128]{2,1,0:T(8,128)S(1)} %get-tuple-element.43), channel_id=1, source_target_pairs={{0,24},{8,0},{16,8},{24,16},{1,25},{9,1},{17,9},{25,17},{2,26},{10... | collective-permute-start | bytes 307208 | tf_op jit(solution)/shard_map/ppermute | solution.py:58
  38.6 5.2 %collective-permute-start.6 = (f32[5,40,128]{2,1,0:T(8,128)S(1)}, f32[5,40,128]{2,1,0:T(8,128)S(1)}, u32[]{:S(2)}, u32[]{:S(2)}) collective-permute-start(f32[5,40,128]{2,1,0:T(8,128)S(1)} %get-tuple-element.44), channel_id=1, source_target_pairs={{0,8},{8,16},{16,24},{24,0},{1,9},{9,17},{17,25},{25,1},{2,10},{10... | collective-permute-start | bytes 307208 | tf_op jit(solution)/shard_map/ppermute | solution.py:59
  44.0 4.9 %collective-permute-start.7 = (f32[5,40,128]{2,1,0:T(8,128)S(1)}, f32[5,40,128]{2,1,0:T(8,128)S(1)}, u32[]{:S(2)}, u32[]{:S(2)}) collective-permute-start(f32[5,40,128]{2,1,0:T(8,128)S(1)} %get-tuple-element.46), channel_id=1, source_target_pairs={{0,4},{4,0},{1,5},{5,1},{2,6},{6,2},{3,7},{7,3},{8,12},{12,8},{9,1... | collective-permute-start | bytes 307208 | tf_op jit(solution)/shard_map/ppermute | solution.py:66
  49.8 4.1 %collective-permute-start.8 = (f32[2,40,128]{2,1,0:T(8,128)S(1)}, f32[2,40,128]{2,1,0:T(8,128)S(1)}, u32[]{:S(2)}, u32[]{:S(2)}) collective-permute-start(f32[2,40,128]{2,1,0:T(8,128)S(1)} %get-tuple-element.48), channel_id=1, source_target_pairs={{0,1},{1,0},{2,3},{3,2},{4,5},{5,4},{6,7},{7,6},{8,9},{9,8},{10,11... | collective-permute-start | bytes 122888 | tf_op jit(solution)/shard_map/ppermute | solution.py:66
  49.9 5.9 %collective-permute-start.9 = (f32[2,40,128]{2,1,0:T(8,128)S(1)}, f32[2,40,128]{2,1,0:T(8,128)S(1)}, u32[]{:S(2)}, u32[]{:S(2)}) collective-permute-start(f32[2,40,128]{2,1,0:T(8,128)S(1)} %get-tuple-element.49), channel_id=1, source_target_pairs={{1,2},{2,1},{5,6},{6,5},{9,10},{10,9},{13,14},{14,13},{17,18},{18,... | collective-permute-start | bytes 122888 | tf_op jit(solution)/shard_map/ppermute | solution.py:66

commit v3 on v2

--- a/solution.py
+++ b/solution.py
@@ -25,11 +25,12 @@
     return jax.ShapeDtypeStruct(shape, jnp.float32)
 
 
-def call(body, name, ins, outs, scratch=(), alias=None, limit=None, out_specs=None, cost=1e8):
+def call(body, name, ins, outs, scratch=(), alias=None, limit=None, out_specs=None, cost=1e8,
+         in_specs=None):
     return pl.pallas_call(
         body,
         name=name,
-        in_specs=[VMEM] * len(ins),
+        in_specs=[VMEM] * len(ins) if in_specs is None else in_specs,
         out_specs=[VMEM] * len(outs) if out_specs is None else out_specs,
         out_shape=outs,
         scratch_shapes=list(scratch),
@@ -43,18 +44,26 @@
     return lax.broadcasted_iota(jnp.int32, shape, dim)
 
 
+RING = "gx/ring"
+
+
+def size_of(axis):
+    return lax.axis_size(axis.split("/")[0])
+
+
 def ends(axis):
-    i = lax.axis_index(axis)
-    return i == 0, i == lax.axis_size(axis) - 1
+    i = lax.axis_index(axis.split("/")[0])
+    return i == 0, i == size_of(axis) - 1
 
 
 def paired(axis):
-    return axis != "gx"
+    return axis != RING
 
 
 def exchange(msgs, axis):
-    n = lax.axis_size(axis)
+    n = size_of(axis)
     if not paired(axis):
+        axis = axis.split("/")[0]
         down = lax.ppermute(msgs[0], axis, [(i, (i - 1) % n) for i in range(n)])
         up = lax.ppermute(msgs[1], axis, [(i, (i + 1) % n) for i in range(n)])
         return [down, up]
@@ -68,7 +77,10 @@
 
 
 def emit(outs, index, axis, low, high):
-    if paired(axis):
+    if isinstance(outs, Kept):
+        outs.lows.append(low())
+        outs.highs.append(high())
+    elif paired(axis):
         even = lax.axis_index(axis) % 2 == 0
         low, high = low(), high()
         outs[0][index] = jnp.where(even, high, low)
@@ -99,49 +111,68 @@
 
 
 def count(axis):
-    return 1 if paired(axis) and lax.axis_size(axis) == 2 else 2
+    return 1 if paired(axis) and size_of(axis) == 2 else 2
 
 
 def turn(value, lanes):
     return pltpu.roll(value, lanes % LANES, 1)
 
 
-def pack(outs, se, re, row, at_row, group, planes, ye, partial):
+def xpack_body(*refs):
+    first_s, first_r, last_s, last_r, *outs = refs
+    for k in range(SLOT):
+        low, high, j = (first_s, last_s, k) if k < F else (first_r, last_r, k - F)
+        emit(outs, (k,), "gx", lambda: low[j], lambda: high[j])
+
+
+def pack(outs, at_row, group, planes, load, partial):
     lane = iota((8, LANES), 1)
-    nt = se.shape[0] - 1
     low, high = partial
+    done = None
+    wrapped = None
     for q in planes:
         at = (q - group * PER) * SLOT
-        here = pl.ds(q * ye + row, 8)
-        one = turn(jnp.where(lane < 64, se[0, here, :], re[nt - 1, here, :]), at + G)
-        two = turn(jnp.where(lane < 64, re[0, here, :], se[nt - 1, here, :]), at)
-        low = jnp.where((lane >= at + G) & (lane < at + SLOT), one, low)
-        low = jnp.where((lane >= at) & (lane < at + G), two, low)
-        back = (lane - (at - F)) % LANES
-        high = jnp.where(back < F, two, high)
-        high = jnp.where((back >= F) & (back < SLOT), one, high)
-    emit(outs, (group, pl.ds(at_row, 8)), "gz", lambda: low, lambda: high)
+        s_low, s_high, r_low, r_high = load(q)
+        one = turn(jnp.where(lane < 64, s_low, r_high), at + G)
+        two = turn(jnp.where(lane < 64, r_low, s_high), at)
+        start_at = lane >= at
+        start_g = lane >= at + G
+        if done is not None and done != q - 1:
+            raise ValueError("planes")
+        low = jnp.where(start_g, one, jnp.where(start_at, two, low))
+        if at == 0:
+            wrapped = two
+            high = jnp.where(start_at, one, high)
+        else:
+            high = jnp.where(start_at, one, jnp.where(lane >= at - F, two, high))
+        done = q
+    if wrapped is not None:
+        high = jnp.where(lane >= LANES - F, wrapped, high)
+    if planes:
+        emit(outs, (group, pl.ds(at_row, 8)), "gz", lambda: low, lambda: high)
 
 
 def build_body(start, right, se, re, *outs):
     nx, ny, nz = start.shape
     xe, ye = nx + 2 * O, ny + 2 * O
-
-    def plane(p, _):
-        for t in range(nz // LANES):
-            at = (p + O) * ye + O
-            se[t, pl.ds(at, ny), :] = start[p, :, t * LANES:(t + 1) * LANES]
-            re[t, pl.ds(at, ny), :] = right[p, :, t * LANES:(t + 1) * LANES]
-        return 0
-
-    lax.fori_loop(0, nx, plane, 0, unroll=4)
+    nt = nz // LANES
 
     def rows(r, _):
         at = pl.multiple_of(r * 8, 8)
         zero = jnp.zeros((8, LANES), jnp.float32)
+
+        def load(q):
+            found = {}
+            for t in range(nt):
+                for key, src, dst in (("s", start, se), ("r", right, re)):
+                    value = src[q - O, pl.ds(at, 8), t * LANES:(t + 1) * LANES]
+                    dst[t, pl.ds(q * ye + at + O, 8), :] = value
+                    found[key, t] = value
+            return found["s", 0], found["s", nt - 1], found["r", 0], found["r", nt - 1]
+
         for group in range(-(-xe // PER)):
             planes = range(max(O, group * PER), min(O + nx, (group + 1) * PER))
-            pack(outs, se, re, at + O, at, group, planes, ye, (zero, zero))
+            pack(outs, at, group, planes, load, (zero, zero))
         return 0
 
     lax.fori_loop(0, ny // 8, rows, 0)
@@ -161,17 +192,42 @@
             dst[t, pl.ds((O + nx + j) * ye + O, ny), :] = high
             dst[t, pl.ds((O - size + j) * ye + O, ny), :] = low
 
+    lane = iota((8, LANES), 1)
+
     def rows(r, _):
         at = pl.multiple_of(r * 8, 8)
+
+        def load(q):
+            here = pl.ds(q * ye + at + O, 8)
+            return se[0, here, :], se[nt - 1, here, :], re[0, here, :], re[nt - 1, here, :]
+
         for group in range(-(-xe // PER)):
             span = range(group * PER, min(xe, (group + 1) * PER))
-            planes = [q for q in span if O - F <= q < O or O + nx <= q < O + nx + F]
-            if planes:
-                high, low = written(outs, (group, pl.ds(at, 8)), "gz")
-                pack(outs, se, re, at + O, at, group, planes, ye, (low, high))
+            before = [q for q in span if O - F <= q < O]
+            after = [q for q in span if O + nx <= q < O + nx + F]
+            if not before and not after:
+                continue
+            core_high, core_low = written(outs, (group, pl.ds(at, 8)), "gz")
+            lows, highs = [], []
+            pack(Kept(lows, highs), at, group, before, load, (core_low, core_high))
+            if before:
+                top = (O - group * PER) * SLOT
+                low = jnp.where(lane < top, lows[0], core_low)
+                high = jnp.where((lane < top - F) | (lane >= LANES - F), highs[0], core_high)
+                core_low, core_high = low, high
+            if after:
+                lows, highs = [], []
+                pack(Kept(lows, highs), at, group, after, load, (core_low, core_high))
+                core_low, core_high = lows[0], jnp.where(lane >= LANES - F, core_high, highs[0])
+            emit(outs, (group, pl.ds(at, 8)), "gz", lambda: core_low, lambda: core_high)
         return 0
 
     lax.fori_loop(0, ny // 8, rows, 0)
+
+
+class Kept:
+    def __init__(self, lows, highs):
+        self.lows, self.highs = lows, highs
 
 
 def zhalo_body(nx, ny, nz, nin, *refs):
@@ -393,16 +449,34 @@
         return 0
 
     lax.fori_loop(0, cx + 1, restrict_y, 0, unroll=3 if cx % 3 == 2 else 1)
-    weight = transfer_weights(nz, cz, LANES, 0, 0.5, 0.25)
+    weight = transfer_weights(nz, cz, LANES, 0, 2.0, 1.0)
     lane_dot(ry, 0, coarse, (O - 1) * cye, (cx + 1) * cye, weight)
     for t in range(ct + 1):
         coarse[t, pl.ds((cx + 2 * O - 1) * cye, cye), :] = jnp.zeros((cye, LANES), jnp.float32)
-    faces(
-        outs, "gx",
-        lambda t, j: coarse[t, pl.ds((O - 1 + j) * cye, cye), :],
-        lambda t, j: coarse[t, pl.ds((cx + j) * cye, cye), :],
-        ct,
-    )
+    pack_coarse(outs, coarse, cx, cy)
+
+
+def pack_coarse(outs, coarse, cx, cy):
+    ct = coarse.shape[0] - 1
+    ye = cy + 2 * O
+    lane = iota((8, LANES), 1)
+
+    def rows(r, _):
+        base = pl.multiple_of(r * 8, 8)
+        for group in range(-(-(cx + 1) // CPER)):
+            low = high = None
+            for j in range(min(CPER, cx + 1 - group * CPER)):
+                at = j * CL
+                rows8 = pl.ds((O - 1 + group * CPER + j) * ye + base, 8)
+                head = jnp.where(lane < CL - 1, coarse[0, rows8, :], coarse[ct, rows8, :])
+                head = turn(head, at + 1)
+                tail = turn(coarse[ct - 1, rows8, :], at + CL)
+                low = head if low is None else jnp.where(lane >= at, head, low)
+                high = tail if high is None else jnp.where(lane >= at, tail, high)
+            emit(outs, (group, pl.ds(base, 8)), "gz", lambda: low, lambda: high)
+        return 0
+
+    lax.fori_loop(0, ye // 8, rows, 0)
 
 
 def faces(outs, axis, low, high, ct):
@@ -410,11 +484,11 @@
     for j in range(CL):
         for t in range(ct):
             emit(outs, (j * ct + t,), axis, lambda: low(t, j), lambda: high(t, j))
-        a = turn(low(ct, j), j + 1)
-        b = turn(high(ct, j), j + 1)
+        a = turn(low(ct, j), 8 * j + CL)
+        b = turn(high(ct, j), 8 * j + CL)
         lane = iota(a.shape, 1)
-        extra_low = a if j == 0 else jnp.where(lane == j, a, extra_low)
-        extra_high = b if j == 0 else jnp.where(lane == j, b, extra_high)
+        extra_low = a if j == 0 else jnp.where(lane >= 8 * j, a, extra_low)
+        extra_high = b if j == 0 else jnp.where(lane >= 8 * j, b, extra_high)
     emit(outs, (CL * ct,), axis, lambda: extra_low, lambda: extra_high)
 
 
@@ -426,12 +500,45 @@
             else:
                 high, low = arrived(refs, (CL * ct,), axis)
                 lane = iota(high.shape, 1)
-                high = jnp.where(lane == LANES - 1, turn(high, -1 - j), 0.0)
-                low = jnp.where(lane == LANES - 1, turn(low, -1 - j), 0.0)
+                used = (lane < CH) | (lane >= LANES - CL)
+                high = jnp.where(used, turn(high, -8 * j - CL), 0.0)
+                low = jnp.where(used, turn(low, -8 * j - CL), 0.0)
             q = size - 1 + j
             write(t, q, read(t, q) + high if j == 0 else high)
             q = j - CL
             write(t, q, read(t, q) + low if j == CL - 1 else low)
+
+
+def coarse_z_body(cx, cy, cz, nin, *refs):
+    halo = refs[:nin]
+    coarse, outs = refs[nin + 1], refs[nin + 2:]
+    ct = cz // LANES
+    xe, ye = cx + 2 * O, cy + 2 * O
+    lane = iota((8, LANES), 1)
+
+    def unpack(r, _):
+        base = pl.multiple_of(r * 8, 8)
+        for group in range(-(-(cx + 1) // CPER)):
+            high, low = arrived(halo, (group, pl.ds(base, 8)), "gz")
+            for j in range(min(CPER, cx + 1 - group * CPER)):
+                here = pl.ds((O - 1 + group * CPER + j) * ye + base, 8)
+                fromhigh = turn(high, -j * CL - 1)
+                fromlow = turn(low, -j * CL - CL)
+                edge = lane == LANES - 1
+                tail = coarse[ct - 1, here, :]
+                own = coarse[ct, here, :]
+                coarse[ct - 1, here, :] = tail + jnp.where(edge, fromhigh, 0.0)
+                wing = jnp.where(lane < CH, fromhigh, jnp.where(lane >= LANES - CL, fromlow, 0.0))
+                coarse[ct, here, :] = wing + jnp.where(edge, own, 0.0)
+        return 0
+
+    lax.fori_loop(0, ye // 8, unpack, 0)
+    faces(
+        outs, RING,
+        lambda t, j: coarse[t, pl.ds((O - 1 + j) * ye, ye), :],
+        lambda t, j: coarse[t, pl.ds((cx + j) * ye, ye), :],
+        ct,
+    )
 
 
 def coarse_x_body(cx, cy, cz, nin, *refs):
@@ -446,7 +553,7 @@
     def write(t, q, value):
         coarse[t, pl.ds((q + O) * ye, ye), :] = value
 
-    place_faces(halo, "gx", ct, cx, read, write)
+    place_faces(halo, RING, ct, cx, read, write)
     faces(
         outs, "gy",
         lambda t, j: coarse[t, pl.ds(O - 1 + j, xe, stride=ye), :],
@@ -455,115 +562,127 @@
     )
 
 
-def coarse_y_body(cx, cy, cz, nin, *refs):
-    halo = refs[:nin]
-    coarse, outs = refs[nin + 1], refs[nin + 2:]
-    ct = cz // LANES
-    xe, ye = cx + 2 * O, cy + 2 * O
-
-    def read(t, q):
-        return coarse[t, pl.ds(q + O, xe, stride=ye), :]
-
-    def write(t, q, value):
-        coarse[t, pl.ds(q + O, xe, stride=ye), :] = value
-
-    place_faces(halo, "gy", ct, cy, read, write)
-    lane = iota((8, LANES), 1)
+def coarse_sweeps(coarse, c, mask, cx, cy, first, tiles):
+    total, ye, _ = mask.shape
+    begin, last = ends("gx")
+    up = jnp.where(last, 0.0, 1.0)
+    down = jnp.where(begin, 0.0, 1.0)
 
     def rows(r, _):
-        base = pl.multiple_of(r * 8, 8)
-        for group in range(-(-xe // CPER)):
-            low = jnp.zeros((8, LANES), jnp.float32)
-            high = low
-            for j in range(min(CPER, xe - group * CPER)):
-                at = j * CL
-                rows8 = pl.ds((group * CPER + j) * ye + base, 8)
-                head = jnp.where(lane < CL - 1, coarse[0, rows8, :], coarse[ct, rows8, :])
-                here = (lane >= at) & (lane < at + CL)
-                low = jnp.where(here, turn(head, at + 1), low)
-                high = jnp.where(here, turn(coarse[ct - 1, rows8, :], at + CL), high)
-            emit(outs, (group, pl.ds(base, 8)), "gz", lambda: low, lambda: high)
-        return 0
-
-    lax.fori_loop(0, ye // 8, rows, 0)
-
-
-def finish_body(cx, cy, cz, nin, *refs):
-    halo = refs[:nin]
-    smooth, _, coarse, out = refs[nin:nin + 4]
-    ca, cb, mask, fine, stage, sems = refs[nin + 4:]
-    ct = cz // LANES
-    xe, ye = cx + 2 * O, cy + 2 * O
+        base = first[1](r)
+        m = [mask[t, pl.ds(base, 8), :] for t in range(total)]
+        for q in range(cx + 2 * O - 1):
+            here = pl.ds(q * ye + base, 8)
+            for t in range(total):
+                factor = m[t] * down if q < O else m[t] * up if q >= O + cx else m[t]
+                c[0][t, here, :] = factor * coarse[t, here, :]
+        return 0
+
+    lax.fori_loop(0, first[0], rows, 0)
+    for n, (low, high) in enumerate(((3, 2), (2, 1), (1, 0))):
+        sweep(c[n], c[n + 1], coarse, mask, cx, low, high, tiles[n])
+
+
+def prolong_add(c, fine, smooth, stage, cx, cy, cz, pieces, tiles):
+    ye = cy + 2 * O
     nx, ny, nz = 2 * cx, 2 * cy, 2 * cz
     nt = nz // LANES
-    lane = iota((8, LANES), 1)
-    first, last = ends("gx")
-    up = jnp.where(last, 0.0, 1.0)
-    down = jnp.where(first, 0.0, 1.0)
-    fill_mask(mask, cy)
-
-    def unpack(r, _):
-        base = pl.multiple_of(r * 8, 8)
-        m = [mask[t, pl.ds(base, 8), :] for t in range(ct + 1)]
-        for group in range(-(-xe // CPER)):
-            high, low = arrived(halo, (group, pl.ds(base, 8)), "gz")
-            for j in range(min(CPER, xe - group * CPER)):
-                q = group * CPER + j
-                here = pl.ds(q * ye + base, 8)
-                fromhigh = turn(high, -j * CL - 1)
-                fromlow = turn(low, -j * CL - CL)
-                edge = lane == LANES - 1
-                value = [coarse[t, here, :] for t in range(ct + 1)]
-                value[ct - 1] = value[ct - 1] + jnp.where(edge, fromhigh, 0.0)
-                wing = jnp.where(lane < CH, fromhigh, jnp.where(lane >= LANES - CL, fromlow, 0.0))
-                value[ct] = wing + jnp.where(edge, value[ct], 0.0)
-                for t in range(ct + 1):
-                    factor = m[t] * down if q < O else m[t] * up if q >= O + cx else m[t]
-                    scaled = 4.0 * value[t]
-                    coarse[t, here, :] = scaled
-                    ca[t, here, :] = factor * scaled
-        return 0
-
-    lax.fori_loop(0, ye // 8, unpack, 0)
-    sweep(ca, cb, coarse, mask, cx, 3, 2, every(ye))
-    sweep(cb, ca, coarse, mask, cx, 2, 1, every(ye))
-    sweep(ca, cb, coarse, mask, cx, 1, 0, every(ye))
-    lane_dot(cb, (O - 1) * ye, fine, 0, (cx + 1) * ye, transfer_weights(nz, cz, LANES, 1, 1.0, 0.5))
-
-    chunks = sems.shape[0]
-    per = cx // chunks
     fye = ny + 2 * O
+    weight = transfer_weights(nz, cz, LANES, 1, 1.0, 0.5)
+    starts = [q * ye + piece for q in range(cx + 1) for piece in pieces]
+    for at in range(0, len(starts), 33):
+        some = starts[at:at + 33]
+        wide = range(weight.shape[0] // LANES)
+        value = jnp.concatenate(
+            [
+                jnp.concatenate([c[t, pl.ds((O - 1) * ye + s, 8), :] for s in some], axis=0)
+                for t in wide
+            ],
+            axis=1,
+        )
+        got = split_dot(value, weight)
+        for n, s in enumerate(some):
+            for t in range(nt):
+                fine[t, pl.ds(s, 8), :] = got[8 * n:8 * n + 8, t * LANES:(t + 1) * LANES]
     flat = stage.reshape(nt, nx * ny, LANES)
-
-    def send(c, t):
-        at = c * 2 * per
-        cut = pl.ds(t * LANES, LANES)
-        return pltpu.make_async_copy(
-            stage.at[t, pl.ds(at, 2 * per)], out.at[pl.ds(at, 2 * per), :, cut], sems.at[c, t]
-        )
 
     def add(i, _):
         for t in range(nt):
-            for k in range(cy // 8):
-                at = (i + 1) * ye + O + 8 * k
+            for row in tiles:
+                at = (i + 1) * ye + O + row
                 here = fine[t, pl.ds(at, 8), :]
                 mid = 0.5 * (here + fine[t, pl.ds(at - 1, 8), :])
                 before = fine[t, pl.ds(at - ye, 8), :]
                 before_mid = 0.5 * (before + fine[t, pl.ds(at - ye - 1, 8), :])
                 parts = (0.5 * (before_mid + mid), 0.5 * (before + here), mid, here)
                 for n, part in enumerate(parts):
-                    src = (2 * i + n // 2 + O) * fye + O + 16 * k + n % 2
-                    dst = (2 * i + n // 2) * ny + 16 * k + n % 2
+                    src = (2 * i + n // 2 + O) * fye + O + 2 * row + n % 2
+                    dst = (2 * i + n // 2) * ny + 2 * row + n % 2
                     flat[t, pl.ds(dst, 8, stride=2), :] = smooth[t, pl.ds(src, 8, stride=2), :] + part
         return 0
+
+    return add
+
+
+def write_out(add, stage, out, sems, cx, spans):
+    chunks = sems.shape[0]
+    per = cx // chunks
+    nt = stage.shape[0]
+
+    def copies(c):
+        at = c * 2 * per
+        return [
+            pltpu.make_async_copy(
+                stage.at[t, pl.ds(at, 2 * per), pl.ds(row, many)],
+                out.at[pl.ds(at, 2 * per), pl.ds(row, many), pl.ds(t * LANES, LANES)],
+                sems.at[c, t * len(spans) + n],
+            )
+            for t in range(nt)
+            for n, (row, many) in enumerate(spans)
+        ]
 
     for c in range(chunks):
         lax.fori_loop(c * per, (c + 1) * per, add, 0)
-        for t in range(nt):
-            send(c, t).start()
+        for copy in copies(c):
+            copy.start()
     for c in range(chunks):
-        for t in range(nt):
-            send(c, t).wait()
+        for copy in copies(c):
+            copy.wait()
+
+
+def finish_inner_body(cx, cy, cz, smooth, coarse, c0, c1, c2, c3, out, mask, fine, stage, sems):
+    c = [c0, c1, c2, c3]
+    fill_mask(mask, cy)
+    tiles = []
+    for n in (1, 2, 3):
+        many = -(-(cy - 1 - 2 * n) // 8)
+        tiles.append((many, lambda r, n=n: jnp.minimum(O + n + 8 * r, O + cy - 1 - n - 8)))
+    coarse_sweeps(coarse, c, mask, cx, cy, every(cy + 2 * O), tiles)
+    add = prolong_add(c3, fine, smooth, stage, cx, cy, cz, range(0, cy, 8), range(4, cy - 4, 8))
+    write_out(add, stage, out, sems, cx, [(8, 2 * cy - 16)])
+
+
+def finish_outer_body(cx, cy, cz, nin, *refs):
+    halo = refs[:nin]
+    smooth, coarse = refs[nin], refs[nin + 7]
+    c = refs[nin + 8:nin + 12]
+    out = refs[nin + 12]
+    mask, fine, stage, sems = refs[nin + 13:]
+    ct = cz // LANES
+    xe, ye = cx + 2 * O, cy + 2 * O
+
+    def read(t, q):
+        return coarse[t, pl.ds(q + O, xe, stride=ye), :]
+
+    def write(t, q, value):
+        coarse[t, pl.ds(q + O, xe, stride=ye), :] = value
+
+    place_faces(halo, "gy", ct, cy, read, write)
+    fill_mask(mask, cy)
+    both = (2, lambda r: pl.multiple_of(r * cy, 8))
+    coarse_sweeps(coarse, c, mask, cx, cy, both, [both] * 3)
+    add = prolong_add(c[3], fine, smooth, stage, cx, cy, cz, (0, cy - 8, cy), (0, cy - 8))
+    write_out(add, stage, out, sems, cx, [(0, 8), (2 * cy - 8, 8)])
 
 
 def on_device(start, right):
@@ -576,9 +695,11 @@
     big = f32(nt + 1, xe * ye, LANES)
     mb = 1 << 20
 
-    to_prev = jnp.concatenate([start[:F], right[:G]], axis=0)
-    to_next = jnp.concatenate([start[nx - F:], right[nx - G:]], axis=0)
-    halo = exchange([to_prev, to_next], "gx")
+    msgs = call(
+        xpack_body, "xpack", [start[:F], right[:G], start[nx - F:], right[nx - G:]],
+        [f32(SLOT, ny, nz)] * count("gx"), limit=4 * mb, cost=9e9,
+    )
+    halo = exchange(msgs, "gx")
     face = [f32(-(-xe // PER), ny, LANES)] * count("gz")
     se, re, *msgs = call(build_body, "build", [start, right], [big, big] + face, limit=8 * mb)
 
@@ -605,11 +726,17 @@
     small = f32(ct + 1, cxe * cye, LANES)
     se, re, s1, s2, rx, coarse, *msgs = call(
         functools.partial(outer_body, nx, ny, nz, n), "outer", [*halo, se, re, s1, s2, rx],
-        [big, big, big, big, part, small] + [f32(CL * ct + 1, cye, LANES)] * count("gx"),
+        [big, big, big, big, part, small] + [f32(-(-(cx + 1) // CPER), cye, LANES)] * count("gz"),
         scratch=[pltpu.VMEM((nt, (cx + 1) * cye, LANES), jnp.float32), masks],
         alias={n + i: i for i in range(5)}, limit=8 * mb,
     )
-    halo = exchange(msgs, "gx")
+    halo = exchange(msgs, "gz")
+    n = len(halo)
+    coarse, *msgs = call(
+        functools.partial(coarse_z_body, cx, cy, cz, n), "coarse_z", [*halo, coarse],
+        [small] + [f32(CL * ct + 1, cye, LANES)] * count(RING), alias={n: 0}, limit=8 * mb,
+    )
+    halo = exchange(msgs, RING)
     n = len(halo)
     coarse, *msgs = call(
         functools.partial(coarse_x_body, cx, cy, cz, n), "coarse_x", [*halo, coarse],
@@ -617,24 +744,21 @@
     )
     halo = exchange(msgs, "gy")
     n = len(halo)
-    coarse, *msgs = call(
-        functools.partial(coarse_y_body, cx, cy, cz, n), "coarse_y", [*halo, coarse],
-        [small] + [f32(-(-cxe // CPER), cye, LANES)] * count("gz"), alias={n: 0}, limit=8 * mb,
-    )
-    halo = exchange(msgs, "gz")
-    n = len(halo)
-    _, out = call(
-        functools.partial(finish_body, cx, cy, cz, n), "finish", [*halo, s2, coarse],
-        [small, f32(nx, ny, nz)],
-        scratch=[
-            pltpu.VMEM((ct + 1, cxe * cye, LANES), jnp.float32),
-            pltpu.VMEM((ct + 1, cxe * cye, LANES), jnp.float32),
-            pltpu.VMEM((ct + 1, cye, LANES), jnp.float32),
-            pltpu.VMEM((nt, (cx + 1) * cye, LANES), jnp.float32),
-            pltpu.VMEM((nt, nx, ny, LANES), jnp.float32),
-            pltpu.SemaphoreType.DMA((8, nt)),
-        ],
-        alias={n + 1: 0}, limit=12 * mb, out_specs=[VMEM, ANY],
+    stage = [
+        pltpu.VMEM((ct + 1, cye, LANES), jnp.float32),
+        pltpu.VMEM((nt, (cx + 1) * cye, LANES), jnp.float32),
+        pltpu.VMEM((nt, nx, ny, LANES), jnp.float32),
+    ]
+    *c, out = call(
+        functools.partial(finish_inner_body, cx, cy, cz), "finish_inner", [s2, coarse],
+        [small] * 4 + [f32(nx, ny, nz)], scratch=stage + [pltpu.SemaphoreType.DMA((8, nt))],
+        limit=10 * mb, out_specs=[VMEM] * 4 + [ANY], cost=5e9,
+    )
+    *_, out = call(
+        functools.partial(finish_outer_body, cx, cy, cz, n), "finish_outer", [*halo, s2, coarse, *c, out],
+        [small] * 5 + [f32(nx, ny, nz)], scratch=stage + [pltpu.SemaphoreType.DMA((2, 2 * nt))],
+        alias={n + 1 + i: i for i in range(6)}, limit=10 * mb,
+        in_specs=[VMEM] * (n + 6) + [ANY], out_specs=[VMEM] * 5 + [ANY],
     )
     return out
 

time: 63.3 us -> 59.9 us (0.946)
  waiting for transfers between devices: 19.7 us -> 15.6 us
  Pallas kernels: 27.5 us -> 29.5 us
  local copies, waits for them, and re-layouts: 6.41 us -> 4.52 us
    ppermute x6 -> x8, waiting for transfers between devices: 12.8 us -> 8.56 us  [exchange(): found[phase] = lax.ppermute(msgs[phase], axis, routes)]
    ppermute x2 -> x1, waiting for transfers between devices: 3.97 us -> 6.02 us  [exchange(): up = lax.ppermute(msgs[1], axis, [(i, (i + 1) % n) for i in range(n)])]
    pallas_call x8 -> x10, Pallas kernels: 27.5 us -> 29.5 us  [call(): pl.pallas_call(body, name=name, in_specs=[VMEM] * len(ins) if in_specs is...]
    unnamed x4, local copies, waits for them, and re-layouts: 4.37 us -> 2.49 us
    ppermute x2 -> x1, waiting for transfers between devices: 2.88 us -> 1.02 us  [exchange(): down = lax.ppermute(msgs[0], axis, [(i, (i - 1) % n) for i in range(n)])]
    ppermute x2 -> x1, starting transfers between devices: 1.04 us -> 0.06 us  [exchange(): down = lax.ppermute(msgs[0], axis, [(i, (i - 1) % n) for i in range(n)])]
    ppermute x6 -> x8, starting transfers between devices: 7.75 us -> 8.58 us  [exchange(): found[phase] = lax.ppermute(msgs[phase], axis, routes)]
    ppermute x2 -> x1, starting transfers between devices: 0.56 us -> 1.23 us  [exchange(): up = lax.ppermute(msgs[1], axis, [(i, (i + 1) % n) for i in range(n)])]
  transfers between devices with their start and end apart: 10 -> 10, of which waited for: 9 -> 6; matrix products, arithmetic and copies ran while one was open for 0% -> 0% of each run, Pallas kernels for 19% -> 29%
where the time goes in v3:
time: 59.9 us; the launch traced here: 59.7 us
  Pallas kernels  29.5 us (49%)
  waiting for transfers between devices  15.6 us (26%)
  starting transfers between devices  9.87 us (16%)
  local copies, waits for them, and re-layouts  4.52 us (8%)
    pallas_call x10, Pallas kernels, call(): pl.pallas_call(body, name=name, in_specs=[VMEM] * len(ins) if in_specs is...  29.5 us
    ppermute x8, starting transfers between devices, exchange(): found[phase] = lax.ppermute(msgs[phase], axis, routes)  8.58 us
    ppermute x8, waiting for transfers between devices, exchange(): found[phase] = lax.ppermute(msgs[phase], axis, routes)  8.56 us
    ppermute x1, waiting for transfers between devices, exchange(): up = lax.ppermute(msgs[1], axis, [(i, (i + 1) % n) for i in range(n)])  6.02 us
    unnamed x4, local copies, waits for them, and re-layouts  2.49 us
    ppermute x1, starting transfers between devices, exchange(): up = lax.ppermute(msgs[1], axis, [(i, (i + 1) % n) for i in range(n)])  1.23 us
  transfers between devices with their start and end apart: 10, of which 6 were waited for; matrix products, arithmetic and copies ran while one was open for 0% of the time, Pallas kernels for 29%

profile of v3, /device:TPU:16, one launch (start us, length us, event | category | flops | bytes accessed | tf_op | source)
XLA Modules:
  0.0 59.7 jit_solution(14639370975285690761)
XLA Ops:
  0.0 1.0 %fusion = (f32[2,64,256]{2,1,0:T(8,128)S(1)}, f32[2,64,256]{2,1,0:T(8,128)S(1)}) fusion(f32[64,64,256]{2,1,0:T(8,128)} %right.1), kind=kLoop, calls=%fused_computation | loop fusion | bytes 524288 | tf_op jit(solution)/shard_map/slice | solution.py:699
  1.0 1.1 %fusion.1 = (f32[3,64,256]{2,1,0:T(8,128)S(1)}, f32[3,64,256]{2,1,0:T(8,128)S(1)}) fusion(f32[64,64,256]{2,1,0:T(8,128)} %start.1), kind=kLoop, calls=%fused_computation.1 | loop fusion | bytes 786432 | tf_op jit(solution)/shard_map/slice | solution.py:699
  2.0 0.0 copy-start
  2.1 0.0 copy-start.1
  2.1 0.1 xpack.1
  2.1 0.1 collective-permute-start
  2.2 0.8 %collective-permute-start.1 = (f32[5,64,256]{2,1,0:T(8,128)S(1)}, f32[5,64,256]{2,1,0:T(8,128)S(1)}, u32[]{:S(2)}, u32[]{:S(2)}) collective-permute-start(f32[5,64,256]{2,1,0:T(8,128)S(1)} %get-tuple-element.37), channel_id=1, source_target_pairs={{8,16},{16,8},{9,17},{17,9},{10,18},{18,10},{11,19},{19,11},{12,20... | collective-permute-start | bytes 983048 | tf_op jit(solution)/shard_map/ppermute | solution.py:75
  3.0 1.2 %copy-done = f32[64,64,256]{2,1,0:T(8,128)S(1)} copy-done((f32[64,64,256]{2,1,0:T(8,128)S(1)}, f32[64,64,256]{2,1,0:T(8,128)}, u32[]{:S(2)}) %copy-start) | copy-done | bytes 4194328
  4.2 1.3 %copy-done.1 = f32[64,64,256]{2,1,0:T(8,128)S(1)} copy-done((f32[64,64,256]{2,1,0:T(8,128)S(1)}, f32[64,64,256]{2,1,0:T(8,128)}, u32[]{:S(2)}) %copy-start.1) | copy-done | bytes 4194328
  5.5 1.9 %build.1 = (f32[3,5184,128]{2,1,0:T(8,128)S(1)}, f32[3,5184,128]{2,1,0:T(8,128)S(1)}, f32[3,64,128]{2,1,0:T(8,128)S(1)}, f32[3,64,128]{2,1,0:T(8,128)S(1)}) custom-call(f32[64,64,256]{2,1,0:T(8,128)S(1)} %copy-done, f32[64,64,256]{2,1,0:T(8,128)S(1)} %copy-done.1), custom_call_target="tpu_custom_call" | custom-call | flops 100000000 | tf_op jit(solution)/shard_map/build/pallas_call | solution.py:30
  7.4 0.0 collective-permute-done.refs_0_
  7.4 0.0 collective-permute-done.1.refs_1_
  7.5 0.7 %xhalo.1 = (f32[3,5184,128]{2,1,0:T(8,128)S(1)}, f32[3,5184,128]{2,1,0:T(8,128)S(1)}, f32[3,64,128]{2,1,0:T(8,128)S(1)}, f32[3,64,128]{2,1,0:T(8,128)S(1)}) custom-call(f32[5,64,256]{2,1,0:T(8,128)S(1)} %collective-permute-done.refs_0_, ...), custom_call_target="tpu_custom_call", output_to_operand_aliasing={{0}: (2, {}), {1}: (3, {}), {2}: (4, {}), {3}: (5, {})} | custom-call | flops 100000000 | tf_op jit(solution)/shard_map/xhalo/pallas_call | solution.py:30
  8.2 1.6 %collective-permute-start.2 = (f32[3,64,128]{2,1,0:T(8,128)S(1)}, f32[3,64,128]{2,1,0:T(8,128)S(1)}, u32[]{:S(2)}, u32[]{:S(2)}) collective-permute-start(f32[3,64,128]{2,1,0:T(8,128)S(1)} %get-tuple-element.42), channel_id=1, source_target_pairs={{0,1},{1,0},{2,3},{3,2},{4,5},{5,4},{6,7},{7,6},{8,9},{9,8},{10,11... | collective-permute-start | bytes 294920 | tf_op jit(solution)/shard_map/ppermute | solution.py:75
  9.8 1.9 %collective-permute-start.3 = (f32[3,64,128]{2,1,0:T(8,128)S(1)}, f32[3,64,128]{2,1,0:T(8,128)S(1)}, u32[]{:S(2)}, u32[]{:S(2)}) collective-permute-start(f32[3,64,128]{2,1,0:T(8,128)S(1)} %get-tuple-element.43), channel_id=1, source_target_pairs={{1,2},{2,1},{5,6},{6,5},{9,10},{10,9},{13,14},{14,13},{17,18},{18,... | collective-permute-start | bytes 294920 | tf_op jit(solution)/shard_map/ppermute | solution.py:75
  11.8 1.1 %collective-permute-done.2.refs_0_ = f32[3,64,128]{2,1,0:T(8,128)S(1)} collective-permute-done((f32[3,64,128]{2,1,0:T(8,128)S(1)}, f32[3,64,128]{2,1,0:T(8,128)S(1)}, u32[]{:S(2)}, u32[]{:S(2)}) %collective-permute-start.2) | collective-permute-done | bytes 98336 | tf_op jit(solution)/shard_map/ppermute | solution.py:75
  12.9 3.5 %collective-permute-done.3.refs_1_ = f32[3,64,128]{2,1,0:T(8,128)S(1)} collective-permute-done((f32[3,64,128]{2,1,0:T(8,128)S(1)}, f32[3,64,128]{2,1,0:T(8,128)S(1)}, u32[]{:S(2)}, u32[]{:S(2)}) %collective-permute-start.3) | collective-permute-done | bytes 98336 | tf_op jit(solution)/shard_map/ppermute | solution.py:75
  16.3 2.1 %zhalo.1 = (f32[3,5184,128]{2,1,0:T(8,128)S(1)}, f32[3,5184,128]{2,1,0:T(8,128)S(1)}, f32[11,72,128]{2,1,0:T(8,128)S(1)}) custom-call(f32[3,64,128]{2,1,0:T(8,128)S(1)} %collective-permute-done.2.refs_0_, f32[3,64,128]{2,1,0:T(8,128)S(1)} %collective-permute-done.3.refs_1_, ...), custom_call_target="tpu_custom_call", output_to_operand_aliasing={{0}: (2, {}), {1}: (3, {})} | custom-call | flops 100000000 | tf_op jit(solution)/shard_map/zhalo/pallas_call | solution.py:30
  18.5 1.6 %collective-permute-start.4 = (f32[11,72,128]{2,1,0:T(8,128)S(1)}, f32[11,72,128]{2,1,0:T(8,128)S(1)}, u32[]{:S(2)}, u32[]{:S(2)}) collective-permute-start(f32[11,72,128]{2,1,0:T(8,128)S(1)} %get-tuple-element.46), channel_id=1, source_target_pairs={{0,4},{4,0},{1,5},{5,1},{2,6},{6,2},{3,7},{7,3},{8,12},{12,8},{9,1... | collective-permute-start | bytes 1216520 | tf_op jit(solution)/shard_map/ppermute | solution.py:75
  20.1 10.0 %inner.1 = (f32[3,5184,128]{2,1,0:T(8,128)S(1)}, f32[3,5184,128]{2,1,0:T(8,128)S(1)}, f32[2,2120,128]{2,1,0:T(8,128)S(1)}) custom-call(f32[3,5184,128]{2,1,0:T(8,128)S(1)} %get-tuple-element.47.se.refs_1_, f32[3,5184,128]{2,1,0:T(8,128)S(1)} %get-tuple-element.48.re.refs_2_), custom_call_target="tpu_custom_call" | custom-call | flops 8999999488 | tf_op jit(solution)/shard_map/inner/pallas_call | solution.py:30
  30.0 0.0 collective-permute-done.4.refs_0_
  30.1 5.0 %outer.1 = (f32[3,5184,128]{2,1,0:T(8,128)S(1)}, f32[3,5184,128]{2,1,0:T(8,128)S(1)}, f32[3,5184,128]{2,1,0:T(8,128)S(1)}, f32[3,5184,128]{2,1,0:T(8,128)S(1)}, ...) custom-call(f32[11,72,128]{2,1,0:T(8,128)S(1)} %collective-permute-d, ...), custom_call_target="tpu_custom_call", output_to_operand_aliasing={{0}: (1, {}), {1}: (2, {}), {2}: (3, {}), {3}: (4, {}), {4}... | custom-call | flops 100000000 | tf_op jit(solution)/shard_map/outer/pallas_call | solution.py:30
  35.0 0.1 collective-permute-start.5
  35.1 1.9 %collective-permute-start.6 = (f32[2,40,128]{2,1,0:T(8,128)S(1)}, f32[2,40,128]{2,1,0:T(8,128)S(1)}, u32[]{:S(2)}, u32[]{:S(2)}) collective-permute-start(f32[2,40,128]{2,1,0:T(8,128)S(1)} %get-tuple-element.53), channel_id=1, source_target_pairs={{1,2},{2,1},{5,6},{6,5},{9,10},{10,9},{13,14},{14,13},{17,18},{18,... | collective-permute-start | bytes 122888 | tf_op jit(solution)/shard_map/ppermute | solution.py:75
  37.0 2.1 %collective-permute-done.5.refs_0_ = f32[2,40,128]{2,1,0:T(8,128)S(1)} collective-permute-done((f32[2,40,128]{2,1,0:T(8,128)S(1)}, f32[2,40,128]{2,1,0:T(8,128)S(1)}, u32[]{:S(2)}, u32[]{:S(2)}) %collective-permute-start.5) | collective-permute-done | bytes 40992 | tf_op jit(solution)/shard_map/ppermute | solution.py:75
  39.1 1.9 %collective-permute-done.6.refs_1_ = f32[2,40,128]{2,1,0:T(8,128)S(1)} collective-permute-done((f32[2,40,128]{2,1,0:T(8,128)S(1)}, f32[2,40,128]{2,1,0:T(8,128)S(1)}, u32[]{:S(2)}, u32[]{:S(2)}) %collective-permute-start.6) | collective-permute-done | bytes 40992 | tf_op jit(solution)/shard_map/ppermute | solution.py:75
  41.0 0.8 %coarse_z.1 = (f32[2,1600,128]{2,1,0:T(8,128)S(1)}, f32[5,40,128]{2,1,0:T(8,128)S(1)}, f32[5,40,128]{2,1,0:T(8,128)S(1)}) custom-call(f32[2,40,128]{2,1,0:T(8,128)S(1)} %collective-permute-done.5.refs_0_, f32[2,40,128]{2,1,0:T(8,128)S(1)} %collective-permute-done.6.refs_1_, ...), custom_call_target="tpu_custom_call", output_to_operand_aliasing={{0}: (2, {})} | custom-call | flops 100000000 | tf_op jit(solution)/shard_map/coarse_z/pallas_call | solution.py:30
  41.8 0.1 collective-permute-start.7
  41.9 1.2 %collective-permute-start.8 = (f32[5,40,128]{2,1,0:T(8,128)S(1)}, f32[5,40,128]{2,1,0:T(8,128)S(1)}, u32[]{:S(2)}, u32[]{:S(2)}) collective-permute-start(f32[5,40,128]{2,1,0:T(8,128)S(1)} %get-tuple-element.56), channel_id=1, source_target_pairs={{0,8},{8,16},{16,24},{24,0},{1,9},{9,17},{17,25},{25,1},{2,10},{10... | collective-permute-start | bytes 307208 | tf_op jit(solution)/shard_map/ppermute | solution.py:68
  43.1 1.0 %collective-permute-done.7.refs_0_ = f32[5,40,128]{2,1,0:T(8,128)S(1)} collective-permute-done((f32[5,40,128]{2,1,0:T(8,128)S(1)}, f32[5,40,128]{2,1,0:T(8,128)S(1)}, u32[]{:S(2)}, u32[]{:S(2)}) %collective-permute-start.7) | collective-permute-done | bytes 102432 | tf_op jit(solution)/shard_map/ppermute | solution.py:67
  44.1 6.0 %collective-permute-done.8.refs_1_ = f32[5,40,128]{2,1,0:T(8,128)S(1)} collective-permute-done((f32[5,40,128]{2,1,0:T(8,128)S(1)}, f32[5,40,128]{2,1,0:T(8,128)S(1)}, u32[]{:S(2)}, u32[]{:S(2)}) %collective-permute-start.8) | collective-permute-done | bytes 102432 | tf_op jit(solution)/shard_map/ppermute | solution.py:68
  50.2 0.2 coarse_x.1
  50.4 0.6 collective-permute-start.9
  50.9 5.3 %finish_inner.1 = (f32[2,1600,128]{2,1,0:T(8,128)S(1)}, f32[2,1600,128]{2,1,0:T(8,128)S(1)}, f32[2,1600,128]{2,1,0:T(8,128)S(1)}, f32[2,1600,128]{2,1,0:T(8,128)S(1)}, f32[64,64,256]{2,1,0:T(8,128)}) custom-call(f32[3,5184,128]{2,1,0:T(8,128)S(1)} %get-tuple-element.59.smooth.refs_1_, f32[2,1600,128]{2,1,0:T(8,128)S(1)} %get-tuple-element.60.coarse.refs_2_), custom_call_target="tpu_custom_call" | custom-call | flops 5000000000 | tf_op jit(solution)/shard_map/finish_inner/pallas_call | solution.py:30
  56.3 0.0 collective-permute-done.9.refs_0_
  56.3 3.4 %finish_outer.1 = (f32[2,1600,128]{2,1,0:T(8,128)S(1)}, f32[2,1600,128]{2,1,0:T(8,128)S(1)}, f32[2,1600,128]{2,1,0:T(8,128)S(1)}, f32[2,1600,128]{2,1,0:T(8,128)...) custom-call(f32[5,40,128]{2,1,0:T(8,128)S(1)} %collective-permute-do, ...), custom_call_target="tpu_custom_call", output_to_operand_aliasing={{0}: (2, {}), {1}: (3, {}), {2}: (4, {}), {3}: (5, {}), {4}... | custom-call | flops 100000000 | tf_op jit(solution)/shard_map/finish_outer/pallas_call | solution.py:30
Async XLA Ops:
  2.0 2.2 %copy-start = (f32[64,64,256]{2,1,0:T(8,128)S(1)}, f32[64,64,256]{2,1,0:T(8,128)}, u32[]{:S(2)}) copy-start(f32[64,64,256]{2,1,0:T(8,128)} %start.1) | copy-start | bytes 12582916
  2.1 3.5 %copy-start.1 = (f32[64,64,256]{2,1,0:T(8,128)S(1)}, f32[64,64,256]{2,1,0:T(8,128)}, u32[]{:S(2)}) copy-start(f32[64,64,256]{2,1,0:T(8,128)} %right.1) | copy-start | bytes 12582916
  2.1 5.3 %collective-permute-start = (f32[5,64,256]{2,1,0:T(8,128)S(1)}, f32[5,64,256]{2,1,0:T(8,128)S(1)}, u32[]{:S(2)}, u32[]{:S(2)}) collective-permute-start(f32[5,64,256]{2,1,0:T(8,128)S(1)} %get-tuple-element.36), channel_id=1, source_target_pairs={{0,8},{8,0},{16,24},{24,16},{1,9},{9,1},{17,25},{25,17},{2,10},{10... | collective-permute-start | bytes 983048 | tf_op jit(solution)/shard_map/ppermute | solution.py:75
  2.2 5.2 %collective-permute-start.1 = (f32[5,64,256]{2,1,0:T(8,128)S(1)}, f32[5,64,256]{2,1,0:T(8,128)S(1)}, u32[]{:S(2)}, u32[]{:S(2)}) collective-permute-start(f32[5,64,256]{2,1,0:T(8,128)S(1)} %get-tuple-element.37), channel_id=1, source_target_pairs={{8,16},{16,8},{9,17},{17,9},{10,18},{18,10},{11,19},{19,11},{12,20... | collective-permute-start | bytes 983048 | tf_op jit(solution)/shard_map/ppermute | solution.py:75
  8.2 4.7 %collective-permute-start.2 = (f32[3,64,128]{2,1,0:T(8,128)S(1)}, f32[3,64,128]{2,1,0:T(8,128)S(1)}, u32[]{:S(2)}, u32[]{:S(2)}) collective-permute-start(f32[3,64,128]{2,1,0:T(8,128)S(1)} %get-tuple-element.42), channel_id=1, source_target_pairs={{0,1},{1,0},{2,3},{3,2},{4,5},{5,4},{6,7},{7,6},{8,9},{9,8},{10,11... | collective-permute-start | bytes 294920 | tf_op jit(solution)/shard_map/ppermute | solution.py:75
  9.8 6.5 %collective-permute-start.3 = (f32[3,64,128]{2,1,0:T(8,128)S(1)}, f32[3,64,128]{2,1,0:T(8,128)S(1)}, u32[]{:S(2)}, u32[]{:S(2)}) collective-permute-start(f32[3,64,128]{2,1,0:T(8,128)S(1)} %get-tuple-element.43), channel_id=1, source_target_pairs={{1,2},{2,1},{5,6},{6,5},{9,10},{10,9},{13,14},{14,13},{17,18},{18,... | collective-permute-start | bytes 294920 | tf_op jit(solution)/shard_map/ppermute | solution.py:75
  18.5 11.6 %collective-permute-start.4 = (f32[11,72,128]{2,1,0:T(8,128)S(1)}, f32[11,72,128]{2,1,0:T(8,128)S(1)}, u32[]{:S(2)}, u32[]{:S(2)}) collective-permute-start(f32[11,72,128]{2,1,0:T(8,128)S(1)} %get-tuple-element.46), channel_id=1, source_target_pairs={{0,4},{4,0},{1,5},{5,1},{2,6},{6,2},{3,7},{7,3},{8,12},{12,8},{9,1... | collective-permute-start | bytes 1216520 | tf_op jit(solution)/shard_map/ppermute | solution.py:75
  35.0 4.1 %collective-permute-start.5 = (f32[2,40,128]{2,1,0:T(8,128)S(1)}, f32[2,40,128]{2,1,0:T(8,128)S(1)}, u32[]{:S(2)}, u32[]{:S(2)}) collective-permute-start(f32[2,40,128]{2,1,0:T(8,128)S(1)} %get-tuple-element.52), channel_id=1, source_target_pairs={{0,1},{1,0},{2,3},{3,2},{4,5},{5,4},{6,7},{7,6},{8,9},{9,8},{10,11... | collective-permute-start | bytes 122888 | tf_op jit(solution)/shard_map/ppermute | solution.py:75
  35.1 5.9 %collective-permute-start.6 = (f32[2,40,128]{2,1,0:T(8,128)S(1)}, f32[2,40,128]{2,1,0:T(8,128)S(1)}, u32[]{:S(2)}, u32[]{:S(2)}) collective-permute-start(f32[2,40,128]{2,1,0:T(8,128)S(1)} %get-tuple-element.53), channel_id=1, source_target_pairs={{1,2},{2,1},{5,6},{6,5},{9,10},{10,9},{13,14},{14,13},{17,18},{18,... | collective-permute-start | bytes 122888 | tf_op jit(solution)/shard_map/ppermute | solution.py:75
  41.8 2.3 %collective-permute-start.7 = (f32[5,40,128]{2,1,0:T(8,128)S(1)}, f32[5,40,128]{2,1,0:T(8,128)S(1)}, u32[]{:S(2)}, u32[]{:S(2)}) collective-permute-start(f32[5,40,128]{2,1,0:T(8,128)S(1)} %get-tuple-element.55), channel_id=1, source_target_pairs={{0,24},{8,0},{16,8},{24,16},{1,25},{9,1},{17,9},{25,17},{2,26},{10... | collective-permute-start | bytes 307208 | tf_op jit(solution)/shard_map/ppermute | solution.py:67
  41.9 8.3 %collective-permute-start.8 = (f32[5,40,128]{2,1,0:T(8,128)S(1)}, f32[5,40,128]{2,1,0:T(8,128)S(1)}, u32[]{:S(2)}, u32[]{:S(2)}) collective-permute-start(f32[5,40,128]{2,1,0:T(8,128)S(1)} %get-tuple-element.56), channel_id=1, source_target_pairs={{0,8},{8,16},{16,24},{24,0},{1,9},{9,17},{17,25},{25,1},{2,10},{10... | collective-permute-start | bytes 307208 | tf_op jit(solution)/shard_map/ppermute | solution.py:68
  50.4 5.9 %collective-permute-start.9 = (f32[5,40,128]{2,1,0:T(8,128)S(1)}, f32[5,40,128]{2,1,0:T(8,128)S(1)}, u32[]{:S(2)}, u32[]{:S(2)}) collective-permute-start(f32[5,40,128]{2,1,0:T(8,128)S(1)} %get-tuple-element.58), channel_id=1, source_target_pairs={{0,4},{4,0},{1,5},{5,1},{2,6},{6,2},{3,7},{7,3},{8,12},{12,8},{9,1... | collective-permute-start | bytes 307208 | tf_op jit(solution)/shard_map/ppermute | solution.py:75

commit v4 on v3

--- a/solution.py
+++ b/solution.py
@@ -175,31 +175,29 @@
             pack(outs, at, group, planes, load, (zero, zero))
         return 0
 
-    lax.fori_loop(0, ny // 8, rows, 0)
+    lax.fori_loop(0, ny // 8, rows, 0, unroll=2)
 
 
 def xhalo_body(nx, ny, nz, nin, *refs):
     halo = refs[:nin]
-    outs = refs[nin + 2 + count("gz"):]
-    se, re, outs = outs[0], outs[1], outs[2:]
-    xe, ye = nx + 2 * O, ny + 2 * O
-    nt = nz // LANES
-    for t in range(nt):
-        cut = slice(t * LANES, (t + 1) * LANES)
-        for k in range(SLOT):
-            high, low = arrived(halo, (k, slice(None), cut), "gx")
-            dst, size, j = (se, F, k) if k < F else (re, G, k - F)
-            dst[t, pl.ds((O + nx + j) * ye + O, ny), :] = high
-            dst[t, pl.ds((O - size + j) * ye + O, ny), :] = low
-
+    outs = refs[nin + count("gz"):]
+    xe = nx + 2 * O
+    first, final = slice(0, LANES), slice(nz - LANES, nz)
     lane = iota((8, LANES), 1)
 
     def rows(r, _):
         at = pl.multiple_of(r * 8, 8)
 
         def load(q):
-            here = pl.ds(q * ye + at + O, 8)
-            return se[0, here, :], se[nt - 1, here, :], re[0, here, :], re[nt - 1, here, :]
+            after = q >= O
+            s_layer = q - O - nx if after else q - O + F
+            r_layer = F + (min(q - O - nx, G - 1) if after else max(q - O + G, 0))
+
+            def get(layer, cut):
+                high, low = arrived(halo, (layer, pl.ds(at, 8), cut), "gx")
+                return high if after else low
+
+            return get(s_layer, first), get(s_layer, final), get(r_layer, first), get(r_layer, final)
 
         for group in range(-(-xe // PER)):
             span = range(group * PER, min(xe, (group + 1) * PER))
@@ -222,7 +220,7 @@
             emit(outs, (group, pl.ds(at, 8)), "gz", lambda: core_low, lambda: core_high)
         return 0
 
-    lax.fori_loop(0, ny // 8, rows, 0)
+    lax.fori_loop(0, ny // 8, rows, 0, unroll=2)
 
 
 class Kept:
@@ -230,9 +228,32 @@
         self.lows, self.highs = lows, highs
 
 
+def middle_body(nx, ny, nz, nin, *refs):
+    halo = refs[:nin]
+    se, re, outs = refs[nin + 2], refs[nin + 3], refs[nin + 4:]
+    xe, ye = nx + 2 * O, ny + 2 * O
+    nt = nz // LANES
+    for t in range(nt):
+        cut = slice(t * LANES, (t + 1) * LANES)
+        for k in range(SLOT):
+            high, low = arrived(halo, (k, slice(None), cut), "gx")
+            dst, size, j = (se, F, k) if k < F else (re, G, k - F)
+            dst[t, pl.ds((O + nx + j) * ye + O, ny), :] = high
+            dst[t, pl.ds((O - size + j) * ye + O, ny), :] = low
+    for k in range(SLOT):
+        src, size, j = (se, F, k) if k < F else (re, G, k - F)
+        for t in range(nt):
+            emit(
+                outs, (k * nt + t,), "gy",
+                lambda: src[t, pl.ds(O + j, xe, stride=ye), :],
+                lambda: src[t, pl.ds(O + ny - size + j, xe, stride=ye), :],
+            )
+
+
 def zhalo_body(nx, ny, nz, nin, *refs):
     halo = refs[:nin]
-    se, re, outs = refs[nin + 2], refs[nin + 3], refs[nin + 4:]
+    outs = refs[nin + 2 + count("gy"):]
+    se, re, outs = outs[0], outs[1], outs[2:]
     xe, ye = nx + 2 * O, ny + 2 * O
     nt = nz // LANES
     lane = iota((8, LANES), 1)
@@ -253,20 +274,16 @@
                 re[nt, here, :] = jnp.where(lane < 64, a, b)
         return 0
 
-    lax.fori_loop(0, ny // 8, unpack, 0)
+    lax.fori_loop(0, ny // 8, unpack, 0, unroll=2)
     lane = iota((xe, LANES), 1)
     extra_low = extra_high = jnp.zeros((xe, LANES), jnp.float32)
     for k in range(SLOT):
         src, size, j = (se, F, k) if k < F else (re, G, k - F)
-        for t in range(nt + 1):
-            low = src[t, pl.ds(O + j, xe, stride=ye), :]
-            high = src[t, pl.ds(O + ny - size + j, xe, stride=ye), :]
-            if t < nt:
-                emit(outs, (k * nt + t,), "gy", lambda: low, lambda: high)
-            else:
-                here = (lane >= 8 * k) & (lane < 8 * k + 2 * F)
-                extra_low = jnp.where(here, turn(low, 8 * k + F), extra_low)
-                extra_high = jnp.where(here, turn(high, 8 * k + F), extra_high)
+        low = src[nt, pl.ds(O + j, xe, stride=ye), :]
+        high = src[nt, pl.ds(O + ny - size + j, xe, stride=ye), :]
+        here = (lane >= 8 * k) & (lane < 8 * k + 2 * F)
+        extra_low = jnp.where(here, turn(low, 8 * k + F), extra_low)
+        extra_high = jnp.where(here, turn(high, 8 * k + F), extra_high)
     emit(outs, (SLOT * nt,), "gy", lambda: extra_low, lambda: extra_high)
 
 
@@ -344,7 +361,7 @@
         stencil(src, ye, base, range(-low, nx + high), total, use)
         return 0
 
-    lax.fori_loop(0, tiles[0], rows, 0)
+    lax.fori_loop(0, tiles[0], rows, 0, unroll=tiles[0] if tiles[0] <= 4 else 1)
 
 
 def residual_x(s2, re, rx, nx, ny, tiles):
@@ -370,7 +387,7 @@
         stencil(s2, ye, base, range(nx), rx.shape[0], use)
         return 0
 
-    lax.fori_loop(0, tiles[0], rows, 0)
+    lax.fori_loop(0, tiles[0], rows, 0, unroll=tiles[0] if tiles[0] <= 4 else 1)
 
 
 def every(ye):
@@ -428,10 +445,23 @@
     cx, cy, cz = nx // 2, ny // 2, nz // 2
     ct = cz // LANES
     cye = cy + 2 * O
+    restrict_yz(rx, ry, coarse, ny, cx, cz, [(0, CL), (cx + 1 - CL, CL)])
+    faces(
+        outs, RING,
+        lambda t, j: coarse[t, pl.ds((O - 1 + j) * cye, cye), :],
+        lambda t, j: coarse[t, pl.ds((cx + j) * cye, cye), :],
+        ct,
+    )
+
+
+def restrict_yz(rx, ry, coarse, ny, cx, cz, spans):
+    nt = rx.shape[0]
+    nz = nt * LANES
+    cy = ny // 2
+    cye = cy + 2 * O
     row = iota((8, LANES), 0)
     zero = jnp.zeros((8, LANES), jnp.float32)
-    for t in range(nt):
-        rx[t, pl.ds((cx + 1) * ny, 8), :] = zero
+    weight = transfer_weights(nz, cz, LANES, 0, 2.0, 1.0)
 
     def restrict_y(i, _):
         for t in range(nt):
@@ -448,12 +478,21 @@
                 ry[t, pl.ds(i * cye + O + 8 * k, 8), :] = (even + odd) + after
         return 0
 
-    lax.fori_loop(0, cx + 1, restrict_y, 0, unroll=3 if cx % 3 == 2 else 1)
-    weight = transfer_weights(nz, cz, LANES, 0, 2.0, 1.0)
-    lane_dot(ry, 0, coarse, (O - 1) * cye, (cx + 1) * cye, weight)
+    for t in range(nt):
+        rx[t, pl.ds((cx + 1) * ny, 8), :] = zero
+    for first, many in spans:
+        unroll = max(u for u in (5, 4, 3, 2, 1) if many % u == 0)
+        lax.fori_loop(first, first + many, restrict_y, 0, unroll=unroll)
+        lane_dot(ry, first * cye, coarse, (O - 1 + first) * cye, many * cye, weight)
+
+
+def rest_body(nx, ny, nz, rx, _, rx_out, coarse, ry):
+    cx = nx // 2
+    restrict_yz(rx_out, ry, coarse, ny, cx, nz // 2, [(CL, cx + 1 - 2 * CL)])
+    ct = coarse.shape[0] - 1
+    cye = ny // 2 + 2 * O
     for t in range(ct + 1):
         coarse[t, pl.ds((cx + 2 * O - 1) * cye, cye), :] = jnp.zeros((cye, LANES), jnp.float32)
-    pack_coarse(outs, coarse, cx, cy)
 
 
 def pack_coarse(outs, coarse, cx, cy):
@@ -463,11 +502,11 @@
 
     def rows(r, _):
         base = pl.multiple_of(r * 8, 8)
-        for group in range(-(-(cx + 1) // CPER)):
+        for group in range(-(-(cx + CL + CH) // CPER)):
             low = high = None
-            for j in range(min(CPER, cx + 1 - group * CPER)):
+            for j in range(min(CPER, cx + CL + CH - group * CPER)):
                 at = j * CL
-                rows8 = pl.ds((O - 1 + group * CPER + j) * ye + base, 8)
+                rows8 = pl.ds((group * CPER + j) * ye + base, 8)
                 head = jnp.where(lane < CL - 1, coarse[0, rows8, :], coarse[ct, rows8, :])
                 head = turn(head, at + 1)
                 tail = turn(coarse[ct - 1, rows8, :], at + CL)
@@ -518,10 +557,10 @@
 
     def unpack(r, _):
         base = pl.multiple_of(r * 8, 8)
-        for group in range(-(-(cx + 1) // CPER)):
+        for group in range(-(-(cx + CL + CH) // CPER)):
             high, low = arrived(halo, (group, pl.ds(base, 8)), "gz")
-            for j in range(min(CPER, cx + 1 - group * CPER)):
-                here = pl.ds((O - 1 + group * CPER + j) * ye + base, 8)
+            for j in range(min(CPER, cx + CL + CH - group * CPER)):
+                here = pl.ds((group * CPER + j) * ye + base, 8)
                 fromhigh = turn(high, -j * CL - 1)
                 fromlow = turn(low, -j * CL - CL)
                 edge = lane == LANES - 1
@@ -534,9 +573,9 @@
 
     lax.fori_loop(0, ye // 8, unpack, 0)
     faces(
-        outs, RING,
-        lambda t, j: coarse[t, pl.ds((O - 1 + j) * ye, ye), :],
-        lambda t, j: coarse[t, pl.ds((cx + j) * ye, ye), :],
+        outs, "gy",
+        lambda t, j: coarse[t, pl.ds(O - 1 + j, xe, stride=ye), :],
+        lambda t, j: coarse[t, pl.ds(cy + j, xe, stride=ye), :],
         ct,
     )
 
@@ -554,12 +593,7 @@
         coarse[t, pl.ds((q + O) * ye, ye), :] = value
 
     place_faces(halo, RING, ct, cx, read, write)
-    faces(
-        outs, "gy",
-        lambda t, j: coarse[t, pl.ds(O - 1 + j, xe, stride=ye), :],
-        lambda t, j: coarse[t, pl.ds(cy + j, xe, stride=ye), :],
-        ct,
-    )
+    pack_coarse(outs, coarse, cx, cy)
 
 
 def coarse_sweeps(coarse, c, mask, cx, cy, first, tiles):
@@ -681,7 +715,7 @@
     fill_mask(mask, cy)
     both = (2, lambda r: pl.multiple_of(r * cy, 8))
     coarse_sweeps(coarse, c, mask, cx, cy, both, [both] * 3)
-    add = prolong_add(c[3], fine, smooth, stage, cx, cy, cz, (0, cy - 8, cy), (0, cy - 8))
+    add = prolong_add(c[3], fine, smooth, stage, cx, cy, cz, (0, cy - 1), (0, cy - 8))
     write_out(add, stage, out, sems, cx, [(0, 8), (2 * cy - 8, 8)])
 
 
@@ -703,17 +737,21 @@
     face = [f32(-(-xe // PER), ny, LANES)] * count("gz")
     se, re, *msgs = call(build_body, "build", [start, right], [big, big] + face, limit=8 * mb)
 
-    n = len(halo)
-    alias = {n + i: i for i in range(2 + len(msgs))}
+    xhalo, n = halo, len(halo)
+    msgs = call(
+        functools.partial(xhalo_body, nx, ny, nz, n), "xhalo", [*xhalo, *msgs],
+        face, alias={n + i: i for i in range(len(msgs))}, limit=8 * mb,
+    )
+    halo = exchange(msgs, "gz")
+    yface = [f32(SLOT * nt + 1, xe, LANES)] * count("gy")
     se, re, *msgs = call(
-        functools.partial(xhalo_body, nx, ny, nz, n), "xhalo", [*halo, se, re, *msgs],
-        [big, big] + face, alias=alias, limit=8 * mb,
-    )
-    halo = exchange(msgs, "gz")
+        functools.partial(middle_body, nx, ny, nz, n), "middle", [*xhalo, se, re],
+        [big, big] + yface, alias={n: 0, n + 1: 1}, limit=8 * mb, cost=2e9,
+    )
     n = len(halo)
     se, re, *msgs = call(
-        functools.partial(zhalo_body, nx, ny, nz, n), "zhalo", [*halo, se, re],
-        [big, big] + [f32(SLOT * nt + 1, xe, LANES)] * count("gy"), alias={n: 0, n + 1: 1}, limit=8 * mb,
+        functools.partial(zhalo_body, nx, ny, nz, n), "zhalo", [*halo, se, re, *msgs],
+        [big, big] + yface, alias={n + i: i for i in range(2 + len(msgs))}, limit=8 * mb,
     )
     halo = exchange(msgs, "gy")
     part = f32(nt, (cx + 1) * ny + 8, LANES)
@@ -726,20 +764,24 @@
     small = f32(ct + 1, cxe * cye, LANES)
     se, re, s1, s2, rx, coarse, *msgs = call(
         functools.partial(outer_body, nx, ny, nz, n), "outer", [*halo, se, re, s1, s2, rx],
-        [big, big, big, big, part, small] + [f32(-(-(cx + 1) // CPER), cye, LANES)] * count("gz"),
+        [big, big, big, big, part, small] + [f32(CL * ct + 1, cye, LANES)] * count(RING),
         scratch=[pltpu.VMEM((nt, (cx + 1) * cye, LANES), jnp.float32), masks],
         alias={n + i: i for i in range(5)}, limit=8 * mb,
+    )
+    halo = exchange(msgs, RING)
+    rx, coarse = call(
+        functools.partial(rest_body, nx, ny, nz), "rest", [rx, coarse], [part, small],
+        scratch=[pltpu.VMEM((nt, (cx + 1) * cye, LANES), jnp.float32)], alias={0: 0, 1: 1}, limit=8 * mb, cost=2e9,
+    )
+    n = len(halo)
+    coarse, *msgs = call(
+        functools.partial(coarse_x_body, cx, cy, cz, n), "coarse_x", [*halo, coarse],
+        [small] + [f32(-(-(cx + CL + CH) // CPER), cye, LANES)] * count("gz"), alias={n: 0}, limit=8 * mb,
     )
     halo = exchange(msgs, "gz")
     n = len(halo)
     coarse, *msgs = call(
         functools.partial(coarse_z_body, cx, cy, cz, n), "coarse_z", [*halo, coarse],
-        [small] + [f32(CL * ct + 1, cye, LANES)] * count(RING), alias={n: 0}, limit=8 * mb,
-    )
-    halo = exchange(msgs, RING)
-    n = len(halo)
-    coarse, *msgs = call(
-        functools.partial(coarse_x_body, cx, cy, cz, n), "coarse_x", [*halo, coarse],
         [small] + [f32(CL * ct + 1, cxe, LANES)] * count("gy"), alias={n: 0}, limit=8 * mb,
     )
     halo = exchange(msgs, "gy")

time: 59.9 us -> 56.4 us (0.942)
  Pallas kernels: 29.5 us -> 26.7 us
  waiting for transfers between devices: 15.6 us -> 13.1 us
  starting transfers between devices: 9.87 us -> 11.7 us
    pallas_call x10 -> x12, Pallas kernels: 29.5 us -> 26.7 us  [call(): pl.pallas_call(body, name=name, in_specs=[VMEM] * len(ins) if in_specs is...]
    ppermute x1, starting transfers between devices: 1.23 us -> 3.09 us  [exchange(): up = lax.ppermute(msgs[1], axis, [(i, (i + 1) % n) for i in range(n)])]
    ppermute x1, waiting for transfers between devices: 6.02 us -> 4.68 us  [exchange(): up = lax.ppermute(msgs[1], axis, [(i, (i + 1) % n) for i in range(n)])]
    ppermute x1, waiting for transfers between devices: 1.02 us -> 0.01 us  [exchange(): down = lax.ppermute(msgs[0], axis, [(i, (i - 1) % n) for i in range(n)])]
  transfers between devices with their start and end apart: 10 -> 10, of which waited for: 6 -> 5; matrix products, arithmetic and copies ran while one was open for 0% -> 0% of each run, Pallas kernels for 29% -> 30%
where the time goes in v4:
time: 56.4 us; the launch traced here: 56.2 us
  Pallas kernels  26.7 us (47%)
  waiting for transfers between devices  13.1 us (23%)
  starting transfers between devices  11.7 us (21%)
  local copies, waits for them, and re-layouts  4.52 us (8%)
    pallas_call x12, Pallas kernels, call(): pl.pallas_call(body, name=name, in_specs=[VMEM] * len(ins) if in_specs is...  26.7 us
    ppermute x8, starting transfers between devices, exchange(): found[phase] = lax.ppermute(msgs[phase], axis, routes)  8.58 us
    ppermute x8, waiting for transfers between devices, exchange(): found[phase] = lax.ppermute(msgs[phase], axis, routes)  8.38 us
    ppermute x1, waiting for transfers between devices, exchange(): up = lax.ppermute(msgs[1], axis, [(i, (i + 1) % n) for i in range(n)])  4.68 us
    ppermute x1, starting transfers between devices, exchange(): up = lax.ppermute(msgs[1], axis, [(i, (i + 1) % n) for i in range(n)])  3.09 us
    unnamed x4, local copies, waits for them, and re-layouts  2.49 us
  transfers between devices with their start and end apart: 10, of which 5 were waited for; matrix products, arithmetic and copies ran while one was open for 0% of the time, Pallas kernels for 30%

profile of v4, /device:TPU:16, one launch (start us, length us, event | category | flops | bytes accessed | tf_op | source)
XLA Modules:
  0.0 56.2 jit_solution(11086949143833000150)
XLA Ops:
  0.0 1.0 %fusion = (f32[2,64,256]{2,1,0:T(8,128)S(1)}, f32[2,64,256]{2,1,0:T(8,128)S(1)}) fusion(f32[64,64,256]{2,1,0:T(8,128)} %right.1), kind=kLoop, calls=%fused_computation | loop fusion | bytes 524288 | tf_op jit(solution)/shard_map/slice | solution.py:733
  1.0 1.1 %fusion.1 = (f32[3,64,256]{2,1,0:T(8,128)S(1)}, f32[3,64,256]{2,1,0:T(8,128)S(1)}) fusion(f32[64,64,256]{2,1,0:T(8,128)} %start.1), kind=kLoop, calls=%fused_computation.1 | loop fusion | bytes 786432 | tf_op jit(solution)/shard_map/slice | solution.py:733
  2.0 0.0 copy-start
  2.1 0.0 copy-start.1
  2.1 0.1 xpack.1
  2.1 0.1 collective-permute-start
  2.2 0.8 %collective-permute-start.1 = (f32[5,64,256]{2,1,0:T(8,128)S(1)}, f32[5,64,256]{2,1,0:T(8,128)S(1)}, u32[]{:S(2)}, u32[]{:S(2)}) collective-permute-start(f32[5,64,256]{2,1,0:T(8,128)S(1)} %get-tuple-element.40), channel_id=1, source_target_pairs={{8,16},{16,8},{9,17},{17,9},{10,18},{18,10},{11,19},{19,11},{12,20... | collective-permute-start | bytes 983048 | tf_op jit(solution)/shard_map/ppermute | solution.py:75
  3.0 1.2 %copy-done = f32[64,64,256]{2,1,0:T(8,128)S(1)} copy-done((f32[64,64,256]{2,1,0:T(8,128)S(1)}, f32[64,64,256]{2,1,0:T(8,128)}, u32[]{:S(2)}) %copy-start) | copy-done | bytes 4194328
  4.2 1.3 %copy-done.1 = f32[64,64,256]{2,1,0:T(8,128)S(1)} copy-done((f32[64,64,256]{2,1,0:T(8,128)S(1)}, f32[64,64,256]{2,1,0:T(8,128)}, u32[]{:S(2)}) %copy-start.1) | copy-done | bytes 4194328
  5.5 1.5 %build.1 = (f32[3,5184,128]{2,1,0:T(8,128)S(1)}, f32[3,5184,128]{2,1,0:T(8,128)S(1)}, f32[3,64,128]{2,1,0:T(8,128)S(1)}, f32[3,64,128]{2,1,0:T(8,128)S(1)}) custom-call(f32[64,64,256]{2,1,0:T(8,128)S(1)} %copy-done, f32[64,64,256]{2,1,0:T(8,128)S(1)} %copy-done.1), custom_call_target="tpu_custom_call" | custom-call | flops 100000000 | tf_op jit(solution)/shard_map/build/pallas_call | solution.py:30
  7.0 0.0 collective-permute-done.refs_0_
  7.0 0.0 collective-permute-done.1.refs_1_
  7.0 0.4 xhalo.1
  7.5 1.6 %collective-permute-start.2 = (f32[3,64,128]{2,1,0:T(8,128)S(1)}, f32[3,64,128]{2,1,0:T(8,128)S(1)}, u32[]{:S(2)}, u32[]{:S(2)}) collective-permute-start(f32[3,64,128]{2,1,0:T(8,128)S(1)} %get-tuple-element.43), channel_id=1, source_target_pairs={{0,1},{1,0},{2,3},{3,2},{4,5},{5,4},{6,7},{7,6},{8,9},{9,8},{10,11... | collective-permute-start | bytes 294920 | tf_op jit(solution)/shard_map/ppermute | solution.py:75
  9.1 1.9 %collective-permute-start.3 = (f32[3,64,128]{2,1,0:T(8,128)S(1)}, f32[3,64,128]{2,1,0:T(8,128)S(1)}, u32[]{:S(2)}, u32[]{:S(2)}) collective-permute-start(f32[3,64,128]{2,1,0:T(8,128)S(1)} %get-tuple-element.44), channel_id=1, source_target_pairs={{1,2},{2,1},{5,6},{6,5},{9,10},{10,9},{13,14},{14,13},{17,18},{18,... | collective-permute-start | bytes 294920 | tf_op jit(solution)/shard_map/ppermute | solution.py:75
  11.0 0.2 middle.1
  11.2 0.9 %collective-permute-done.2.refs_0_ = f32[3,64,128]{2,1,0:T(8,128)S(1)} collective-permute-done((f32[3,64,128]{2,1,0:T(8,128)S(1)}, f32[3,64,128]{2,1,0:T(8,128)S(1)}, u32[]{:S(2)}, u32[]{:S(2)}) %collective-permute-start.2) | collective-permute-done | bytes 98336 | tf_op jit(solution)/shard_map/ppermute | solution.py:75
  12.2 3.5 %collective-permute-done.3.refs_1_ = f32[3,64,128]{2,1,0:T(8,128)S(1)} collective-permute-done((f32[3,64,128]{2,1,0:T(8,128)S(1)}, f32[3,64,128]{2,1,0:T(8,128)S(1)}, u32[]{:S(2)}, u32[]{:S(2)}) %collective-permute-start.3) | collective-permute-done | bytes 98336 | tf_op jit(solution)/shard_map/ppermute | solution.py:75
  15.6 1.7 %zhalo.1 = (f32[3,5184,128]{2,1,0:T(8,128)S(1)}, f32[3,5184,128]{2,1,0:T(8,128)S(1)}, f32[11,72,128]{2,1,0:T(8,128)S(1)}) custom-call(f32[3,64,128]{2,1,0:T(8,128)S(1)} %collective-permute-done.2.refs_0_, f32[3,64,128]{2,1,0:T(8,128)S(1)} %collective-permute-done.3.refs_1_, ...), custom_call_target="tpu_custom_call", output_to_operand_aliasing={{0}: (2, {}), {1}: (3, {}), {2}: (4, {})} | custom-call | flops 100000000 | tf_op jit(solution)/shard_map/zhalo/pallas_call | solution.py:30
  17.3 1.6 %collective-permute-start.4 = (f32[11,72,128]{2,1,0:T(8,128)S(1)}, f32[11,72,128]{2,1,0:T(8,128)S(1)}, u32[]{:S(2)}, u32[]{:S(2)}) collective-permute-start(f32[11,72,128]{2,1,0:T(8,128)S(1)} %get-tuple-element.50), channel_id=1, source_target_pairs={{0,4},{4,0},{1,5},{5,1},{2,6},{6,2},{3,7},{7,3},{8,12},{12,8},{9,1... | collective-permute-start | bytes 1216520 | tf_op jit(solution)/shard_map/ppermute | solution.py:75
  18.9 9.5 %inner.1 = (f32[3,5184,128]{2,1,0:T(8,128)S(1)}, f32[3,5184,128]{2,1,0:T(8,128)S(1)}, f32[2,2120,128]{2,1,0:T(8,128)S(1)}) custom-call(f32[3,5184,128]{2,1,0:T(8,128)S(1)} %get-tuple-element.51.se.refs_1_, f32[3,5184,128]{2,1,0:T(8,128)S(1)} %get-tuple-element.52.re.refs_2_), custom_call_target="tpu_custom_call" | custom-call | flops 8999999488 | tf_op jit(solution)/shard_map/inner/pallas_call | solution.py:30
  28.4 0.0 collective-permute-done.4.refs_0_
  28.4 3.0 %outer.1 = (f32[3,5184,128]{2,1,0:T(8,128)S(1)}, f32[3,5184,128]{2,1,0:T(8,128)S(1)}, f32[3,5184,128]{2,1,0:T(8,128)S(1)}, f32[3,5184,128]{2,1,0:T(8,128)S(1)}, ...) custom-call(f32[11,72,128]{2,1,0:T(8,128)S(1)} %collective-permute-d, ...), custom_call_target="tpu_custom_call", output_to_operand_aliasing={{0}: (1, {}), {1}: (2, {}), {2}: (3, {}), {3}: (4, {}), {4}... | custom-call | flops 100000000 | tf_op jit(solution)/shard_map/outer/pallas_call | solution.py:30
  31.4 0.1 collective-permute-start.5
  31.5 3.1 %collective-permute-start.6 = (f32[5,40,128]{2,1,0:T(8,128)S(1)}, f32[5,40,128]{2,1,0:T(8,128)S(1)}, u32[]{:S(2)}, u32[]{:S(2)}) collective-permute-start(f32[5,40,128]{2,1,0:T(8,128)S(1)} %get-tuple-element.57), channel_id=1, source_target_pairs={{0,8},{8,16},{16,24},{24,0},{1,9},{9,17},{17,25},{25,1},{2,10},{10... | collective-permute-start | bytes 307208 | tf_op jit(solution)/shard_map/ppermute | solution.py:68
  34.6 0.9 %rest.1 = (f32[2,2120,128]{2,1,0:T(8,128)S(1)}, f32[2,1600,128]{2,1,0:T(8,128)S(1)}) custom-call(f32[2,2120,128]{2,1,0:T(8,128)S(1)} %get-tuple-element.58.rx, f32[2,1600,128]{2,1,0:T(8,128)S(1)} %get-tuple-element.59._), custom_call_target="tpu_custom_call", output_to_operand_aliasing={{0}: (0, {}), {1}: (1, {})} | custom-call | flops 2000000000 | tf_op jit(solution)/shard_map/rest/pallas_call | solution.py:30
  35.5 0.0 collective-permute-done.5.refs_0_
  35.5 4.7 %collective-permute-done.6.refs_1_ = f32[5,40,128]{2,1,0:T(8,128)S(1)} collective-permute-done((f32[5,40,128]{2,1,0:T(8,128)S(1)}, f32[5,40,128]{2,1,0:T(8,128)S(1)}, u32[]{:S(2)}, u32[]{:S(2)}) %collective-permute-start.6) | collective-permute-done | bytes 102432 | tf_op jit(solution)/shard_map/ppermute | solution.py:68
  40.2 0.9 %coarse_x.1 = (f32[2,1600,128]{2,1,0:T(8,128)S(1)}, f32[2,40,128]{2,1,0:T(8,128)S(1)}, f32[2,40,128]{2,1,0:T(8,128)S(1)}) custom-call(f32[5,40,128]{2,1,0:T(8,128)S(1)} %collective-permute-done.5.refs_0_, f32[5,40,128]{2,1,0:T(8,128)S(1)} %collective-permute-done.6.refs_1_, ...), custom_call_target="tpu_custom_call", output_to_operand_aliasing={{0}: (2, {})} | custom-call | flops 100000000 | tf_op jit(solution)/shard_map/coarse_x/pallas_call | solution.py:30
  41.0 0.1 collective-permute-start.7
  41.1 1.9 %collective-permute-start.8 = (f32[2,40,128]{2,1,0:T(8,128)S(1)}, f32[2,40,128]{2,1,0:T(8,128)S(1)}, u32[]{:S(2)}, u32[]{:S(2)}) collective-permute-start(f32[2,40,128]{2,1,0:T(8,128)S(1)} %get-tuple-element.62), channel_id=1, source_target_pairs={{1,2},{2,1},{5,6},{6,5},{9,10},{10,9},{13,14},{14,13},{17,18},{18,... | collective-permute-start | bytes 122888 | tf_op jit(solution)/shard_map/ppermute | solution.py:75
  43.0 2.1 %collective-permute-done.7.refs_0_ = f32[2,40,128]{2,1,0:T(8,128)S(1)} collective-permute-done((f32[2,40,128]{2,1,0:T(8,128)S(1)}, f32[2,40,128]{2,1,0:T(8,128)S(1)}, u32[]{:S(2)}, u32[]{:S(2)}) %collective-permute-start.7) | collective-permute-done | bytes 40992 | tf_op jit(solution)/shard_map/ppermute | solution.py:75
  45.1 1.9 %collective-permute-done.8.refs_1_ = f32[2,40,128]{2,1,0:T(8,128)S(1)} collective-permute-done((f32[2,40,128]{2,1,0:T(8,128)S(1)}, f32[2,40,128]{2,1,0:T(8,128)S(1)}, u32[]{:S(2)}, u32[]{:S(2)}) %collective-permute-start.8) | collective-permute-done | bytes 40992 | tf_op jit(solution)/shard_map/ppermute | solution.py:75
  47.0 0.9 %coarse_z.1 = (f32[2,1600,128]{2,1,0:T(8,128)S(1)}, f32[5,40,128]{2,1,0:T(8,128)S(1)}) custom-call(f32[2,40,128]{2,1,0:T(8,128)S(1)} %collective-permute-done.7.refs_0_, f32[2,40,128]{2,1,0:T(8,128)S(1)} %collective-permute-done.8.refs_1_, f32[2,1600,128]{2,1,0:T(8,128)S(1)} %get-tuple-element.63.refs_2_), custom_call_target="tpu_custom_call", output_to_operand_aliasing={{0}: (2, {})} | custom-call | flops 100000000 | tf_op jit(solution)/shard_map/coarse_z/pallas_call | solution.py:30
  47.9 0.6 %collective-permute-start.9 = (f32[5,40,128]{2,1,0:T(8,128)S(1)}, f32[5,40,128]{2,1,0:T(8,128)S(1)}, u32[]{:S(2)}, u32[]{:S(2)}) collective-permute-start(f32[5,40,128]{2,1,0:T(8,128)S(1)} %get-tuple-element.64), channel_id=1, source_target_pairs={{0,4},{4,0},{1,5},{5,1},{2,6},{6,2},{3,7},{7,3},{8,12},{12,8},{9,1... | collective-permute-start | bytes 307208 | tf_op jit(solution)/shard_map/ppermute | solution.py:75
  48.5 4.7 %finish_inner.1 = (f32[2,1600,128]{2,1,0:T(8,128)S(1)}, f32[2,1600,128]{2,1,0:T(8,128)S(1)}, f32[2,1600,128]{2,1,0:T(8,128)S(1)}, f32[2,1600,128]{2,1,0:T(8,128)S(1)}, f32[64,64,256]{2,1,0:T(8,128)}) custom-call(f32[3,5184,128]{2,1,0:T(8,128)S(1)} %get-tuple-element.65.smooth.refs_1_, f32[2,1600,128]{2,1,0:T(8,128)S(1)} %get-tuple-element.66.coarse.refs_2_), custom_call_target="tpu_custom_call" | custom-call | flops 5000000000 | tf_op jit(solution)/shard_map/finish_inner/pallas_call | solution.py:30
  53.2 0.0 collective-permute-done.9.refs_0_
  53.2 3.0 %finish_outer.1 = (f32[2,1600,128]{2,1,0:T(8,128)S(1)}, f32[2,1600,128]{2,1,0:T(8,128)S(1)}, f32[2,1600,128]{2,1,0:T(8,128)S(1)}, f32[2,1600,128]{2,1,0:T(8,128)...) custom-call(f32[5,40,128]{2,1,0:T(8,128)S(1)} %collective-permute-do, ...), custom_call_target="tpu_custom_call", output_to_operand_aliasing={{0}: (2, {}), {1}: (3, {}), {2}: (4, {}), {3}: (5, {}), {4}... | custom-call | flops 100000000 | tf_op jit(solution)/shard_map/finish_outer/pallas_call | solution.py:30
Async XLA Ops:
  2.0 2.2 %copy-start = (f32[64,64,256]{2,1,0:T(8,128)S(1)}, f32[64,64,256]{2,1,0:T(8,128)}, u32[]{:S(2)}) copy-start(f32[64,64,256]{2,1,0:T(8,128)} %start.1) | copy-start | bytes 12582916
  2.1 3.5 %copy-start.1 = (f32[64,64,256]{2,1,0:T(8,128)S(1)}, f32[64,64,256]{2,1,0:T(8,128)}, u32[]{:S(2)}) copy-start(f32[64,64,256]{2,1,0:T(8,128)} %right.1) | copy-start | bytes 12582916
  2.1 4.9 %collective-permute-start = (f32[5,64,256]{2,1,0:T(8,128)S(1)}, f32[5,64,256]{2,1,0:T(8,128)S(1)}, u32[]{:S(2)}, u32[]{:S(2)}) collective-permute-start(f32[5,64,256]{2,1,0:T(8,128)S(1)} %get-tuple-element.39), channel_id=1, source_target_pairs={{0,8},{8,0},{16,24},{24,16},{1,9},{9,1},{17,25},{25,17},{2,10},{10... | collective-permute-start | bytes 983048 | tf_op jit(solution)/shard_map/ppermute | solution.py:75
  2.2 4.8 %collective-permute-start.1 = (f32[5,64,256]{2,1,0:T(8,128)S(1)}, f32[5,64,256]{2,1,0:T(8,128)S(1)}, u32[]{:S(2)}, u32[]{:S(2)}) collective-permute-start(f32[5,64,256]{2,1,0:T(8,128)S(1)} %get-tuple-element.40), channel_id=1, source_target_pairs={{8,16},{16,8},{9,17},{17,9},{10,18},{18,10},{11,19},{19,11},{12,20... | collective-permute-start | bytes 983048 | tf_op jit(solution)/shard_map/ppermute | solution.py:75
  7.5 4.7 %collective-permute-start.2 = (f32[3,64,128]{2,1,0:T(8,128)S(1)}, f32[3,64,128]{2,1,0:T(8,128)S(1)}, u32[]{:S(2)}, u32[]{:S(2)}) collective-permute-start(f32[3,64,128]{2,1,0:T(8,128)S(1)} %get-tuple-element.43), channel_id=1, source_target_pairs={{0,1},{1,0},{2,3},{3,2},{4,5},{5,4},{6,7},{7,6},{8,9},{9,8},{10,11... | collective-permute-start | bytes 294920 | tf_op jit(solution)/shard_map/ppermute | solution.py:75
  9.1 6.5 %collective-permute-start.3 = (f32[3,64,128]{2,1,0:T(8,128)S(1)}, f32[3,64,128]{2,1,0:T(8,128)S(1)}, u32[]{:S(2)}, u32[]{:S(2)}) collective-permute-start(f32[3,64,128]{2,1,0:T(8,128)S(1)} %get-tuple-element.44), channel_id=1, source_target_pairs={{1,2},{2,1},{5,6},{6,5},{9,10},{10,9},{13,14},{14,13},{17,18},{18,... | collective-permute-start | bytes 294920 | tf_op jit(solution)/shard_map/ppermute | solution.py:75
  17.3 11.1 %collective-permute-start.4 = (f32[11,72,128]{2,1,0:T(8,128)S(1)}, f32[11,72,128]{2,1,0:T(8,128)S(1)}, u32[]{:S(2)}, u32[]{:S(2)}) collective-permute-start(f32[11,72,128]{2,1,0:T(8,128)S(1)} %get-tuple-element.50), channel_id=1, source_target_pairs={{0,4},{4,0},{1,5},{5,1},{2,6},{6,2},{3,7},{7,3},{8,12},{12,8},{9,1... | collective-permute-start | bytes 1216520 | tf_op jit(solution)/shard_map/ppermute | solution.py:75
  31.4 4.1 %collective-permute-start.5 = (f32[5,40,128]{2,1,0:T(8,128)S(1)}, f32[5,40,128]{2,1,0:T(8,128)S(1)}, u32[]{:S(2)}, u32[]{:S(2)}) collective-permute-start(f32[5,40,128]{2,1,0:T(8,128)S(1)} %get-tuple-element.56), channel_id=1, source_target_pairs={{0,24},{8,0},{16,8},{24,16},{1,25},{9,1},{17,9},{25,17},{2,26},{10... | collective-permute-start | bytes 307208 | tf_op jit(solution)/shard_map/ppermute | solution.py:67
  31.5 8.7 %collective-permute-start.6 = (f32[5,40,128]{2,1,0:T(8,128)S(1)}, f32[5,40,128]{2,1,0:T(8,128)S(1)}, u32[]{:S(2)}, u32[]{:S(2)}) collective-permute-start(f32[5,40,128]{2,1,0:T(8,128)S(1)} %get-tuple-element.57), channel_id=1, source_target_pairs={{0,8},{8,16},{16,24},{24,0},{1,9},{9,17},{17,25},{25,1},{2,10},{10... | collective-permute-start | bytes 307208 | tf_op jit(solution)/shard_map/ppermute | solution.py:68
  41.0 4.1 %collective-permute-start.7 = (f32[2,40,128]{2,1,0:T(8,128)S(1)}, f32[2,40,128]{2,1,0:T(8,128)S(1)}, u32[]{:S(2)}, u32[]{:S(2)}) collective-permute-start(f32[2,40,128]{2,1,0:T(8,128)S(1)} %get-tuple-element.61), channel_id=1, source_target_pairs={{0,1},{1,0},{2,3},{3,2},{4,5},{5,4},{6,7},{7,6},{8,9},{9,8},{10,11... | collective-permute-start | bytes 122888 | tf_op jit(solution)/shard_map/ppermute | solution.py:75
  41.1 5.9 %collective-permute-start.8 = (f32[2,40,128]{2,1,0:T(8,128)S(1)}, f32[2,40,128]{2,1,0:T(8,128)S(1)}, u32[]{:S(2)}, u32[]{:S(2)}) collective-permute-start(f32[2,40,128]{2,1,0:T(8,128)S(1)} %get-tuple-element.62), channel_id=1, source_target_pairs={{1,2},{2,1},{5,6},{6,5},{9,10},{10,9},{13,14},{14,13},{17,18},{18,... | collective-permute-start | bytes 122888 | tf_op jit(solution)/shard_map/ppermute | solution.py:75
  47.9 5.3 %collective-permute-start.9 = (f32[5,40,128]{2,1,0:T(8,128)S(1)}, f32[5,40,128]{2,1,0:T(8,128)S(1)}, u32[]{:S(2)}, u32[]{:S(2)}) collective-permute-start(f32[5,40,128]{2,1,0:T(8,128)S(1)} %get-tuple-element.64), channel_id=1, source_target_pairs={{0,4},{4,0},{1,5},{5,1},{2,6},{6,2},{3,7},{7,3},{8,12},{12,8},{9,1... | collective-permute-start | bytes 307208 | tf_op jit(solution)/shard_map/ppermute | solution.py:75

commit v5 on v4

--- a/solution.py
+++ b/solution.py
@@ -114,15 +114,23 @@
     return 1 if paired(axis) and size_of(axis) == 2 else 2
 
 
+def loop(many, body, most=5):
+    if many <= most:
+        for r in range(many):
+            body(r, 0)
+    else:
+        unroll = max(u for u in range(1, most + 1) if many % u == 0)
+        lax.fori_loop(0, many, body, 0, unroll=unroll)
+
+
 def turn(value, lanes):
     return pltpu.roll(value, lanes % LANES, 1)
 
 
 def xpack_body(*refs):
-    first_s, first_r, last_s, last_r, *outs = refs
+    joined, *outs = refs
     for k in range(SLOT):
-        low, high, j = (first_s, last_s, k) if k < F else (first_r, last_r, k - F)
-        emit(outs, (k,), "gx", lambda: low[j], lambda: high[j])
+        emit(outs, (k,), "gx", lambda: joined[k], lambda: joined[SLOT + k])
 
 
 def pack(outs, at_row, group, planes, load, partial):
@@ -175,7 +183,7 @@
             pack(outs, at, group, planes, load, (zero, zero))
         return 0
 
-    lax.fori_loop(0, ny // 8, rows, 0, unroll=2)
+    loop(ny // 8, rows)
 
 
 def xhalo_body(nx, ny, nz, nin, *refs):
@@ -220,7 +228,7 @@
             emit(outs, (group, pl.ds(at, 8)), "gz", lambda: core_low, lambda: core_high)
         return 0
 
-    lax.fori_loop(0, ny // 8, rows, 0, unroll=2)
+    loop(ny // 8, rows)
 
 
 class Kept:
@@ -274,7 +282,7 @@
                 re[nt, here, :] = jnp.where(lane < 64, a, b)
         return 0
 
-    lax.fori_loop(0, ny // 8, unpack, 0, unroll=2)
+    loop(ny // 8, unpack)
     lane = iota((xe, LANES), 1)
     extra_low = extra_high = jnp.zeros((xe, LANES), jnp.float32)
     for k in range(SLOT):
@@ -361,7 +369,7 @@
         stencil(src, ye, base, range(-low, nx + high), total, use)
         return 0
 
-    lax.fori_loop(0, tiles[0], rows, 0, unroll=tiles[0] if tiles[0] <= 4 else 1)
+    loop(tiles[0], rows, 4)
 
 
 def residual_x(s2, re, rx, nx, ny, tiles):
@@ -387,7 +395,7 @@
         stencil(s2, ye, base, range(nx), rx.shape[0], use)
         return 0
 
-    lax.fori_loop(0, tiles[0], rows, 0, unroll=tiles[0] if tiles[0] <= 4 else 1)
+    loop(tiles[0], rows, 4)
 
 
 def every(ye):
@@ -515,7 +523,7 @@
             emit(outs, (group, pl.ds(base, 8)), "gz", lambda: low, lambda: high)
         return 0
 
-    lax.fori_loop(0, ye // 8, rows, 0)
+    loop(ye // 8, rows)
 
 
 def faces(outs, axis, low, high, ct):
@@ -571,7 +579,7 @@
                 coarse[ct, here, :] = wing + jnp.where(edge, own, 0.0)
         return 0
 
-    lax.fori_loop(0, ye // 8, unpack, 0)
+    loop(ye // 8, unpack)
     faces(
         outs, "gy",
         lambda t, j: coarse[t, pl.ds(O - 1 + j, xe, stride=ye), :],
@@ -612,7 +620,7 @@
                 c[0][t, here, :] = factor * coarse[t, here, :]
         return 0
 
-    lax.fori_loop(0, first[0], rows, 0)
+    loop(first[0], rows)
     for n, (low, high) in enumerate(((3, 2), (2, 1), (1, 0))):
         sweep(c[n], c[n + 1], coarse, mask, cx, low, high, tiles[n])
 
@@ -676,7 +684,8 @@
         ]
 
     for c in range(chunks):
-        lax.fori_loop(c * per, (c + 1) * per, add, 0)
+        unroll = max(u for u in (4, 2, 1) if per % u == 0)
+        lax.fori_loop(c * per, (c + 1) * per, add, 0, unroll=unroll)
         for copy in copies(c):
             copy.start()
     for c in range(chunks):
@@ -719,6 +728,21 @@
     write_out(add, stage, out, sems, cx, [(0, 8), (2 * cy - 8, 8)])
 
 
+def joined_faces(start, right):
+    nx = start.shape[0]
+    i = lax.broadcasted_iota(jnp.int32, (2 * SLOT, 1, 1), 0)
+    z = jnp.float32(0)
+
+    def put(v, first, many, at):
+        return lax.pad(v, z, [(at - first, (2 * SLOT - at) - (nx - first), 0), (0, 0, 0), (0, 0, 0)])
+
+    a = put(start, 0, F, 0)
+    b = put(right, 0, G, F)
+    c = put(start, nx - F, F, SLOT)
+    d = put(right, nx - G, G, SLOT + F)
+    return jnp.where(i < F, a, jnp.where(i < SLOT, b, jnp.where(i < SLOT + F, c, d)))
+
+
 def on_device(start, right):
     nx, ny, nz = start.shape
     nt = nz // LANES
@@ -730,7 +754,7 @@
     mb = 1 << 20
 
     msgs = call(
-        xpack_body, "xpack", [start[:F], right[:G], start[nx - F:], right[nx - G:]],
+        xpack_body, "xpack", [joined_faces(start, right)],
         [f32(SLOT, ny, nz)] * count("gx"), limit=4 * mb, cost=9e9,
     )
     halo = exchange(msgs, "gx")

time: 56.4 us -> 54.8 us (0.972)
  local copies, waits for them, and re-layouts: 4.52 us -> 2.49 us
  other arithmetic: 0 us -> 1.82 us
  Pallas kernels: 26.7 us -> 25 us
    slice x2 -> x0, local copies, waits for them, and re-layouts: 2.04 us -> none  [the longest x1 1.05 us: on_device(): start[nx - F:]]
    select_n x0 -> x1, other arithmetic: none -> 1.81 us  [joined_faces(): jnp.where(i < F, a, jnp.where(i < SLOT, b, jnp.where(i < SLOT + F, c, d)))]
    pallas_call x12, Pallas kernels: 26.7 us -> 25 us  [call(): pl.pallas_call(body, name=name, in_specs=[VMEM] * len(ins) if in_specs is...]
where the time goes in v5:
time: 54.8 us; the launch traced here: 54.6 us
  Pallas kernels  25 us (46%)
  waiting for transfers between devices  12.9 us (24%)
  starting transfers between devices  12.1 us (22%)
  local copies, waits for them, and re-layouts  2.49 us (5%)
  other arithmetic  1.82 us (3%)
    pallas_call x12, Pallas kernels, call(): pl.pallas_call(body, name=name, in_specs=[VMEM] * len(ins) if in_specs is...  25 us
    ppermute x8, starting transfers between devices, exchange(): found[phase] = lax.ppermute(msgs[phase], axis, routes)  8.76 us
    ppermute x8, waiting for transfers between devices, exchange(): found[phase] = lax.ppermute(msgs[phase], axis, routes)  8.2 us
    ppermute x1, waiting for transfers between devices, exchange(): up = lax.ppermute(msgs[1], axis, [(i, (i + 1) % n) for i in range(n)])  4.68 us
    ppermute x1, starting transfers between devices, exchange(): up = lax.ppermute(msgs[1], axis, [(i, (i + 1) % n) for i in range(n)])  3.29 us
    unnamed x4, local copies, waits for them, and re-layouts  2.49 us
    select_n x1, other arithmetic, joined_faces(): jnp.where(i < F, a, jnp.where(i < SLOT, b, jnp.where(i < SLOT + F, c, d)))  1.81 us
  transfers between devices with their start and end apart: 10, of which 5 were waited for; matrix products, arithmetic and copies ran while one was open for 0% of the time, Pallas kernels for 30%

profile of v5, /device:TPU:16, one launch (start us, length us, event | category | flops | bytes accessed | tf_op | source)
XLA Modules:
  0.0 54.6 jit_solution(13684719165891806656)
XLA Ops:
  0.0 1.8 %fusion.2.refs_0_ = f32[10,64,256]{2,1,0:T(8,128)S(1)} fusion(f32[64,64,256]{2,1,0:T(8,128)} %start.1, f32[64,64,256]{2,1,0:T(8,128)} %right.1, pred[10]{0:T(512)(128)(4,1)S(1)} %get-tuple-element.73, pred[10]{0:T(512)(128)(4,1)S(1)} %get-tuple-element.74, pred[10]{0:T(512)(128)(4,1)S(1)} %iota_compare_fusion.2), kind=kLoop, calls=%fused_computation.4 | loop fusion | flops 491520 | bytes 10354718 | tf_op jit(solution)/shard_map/jit(_where)/select_n | solution.py:743
  1.8 0.0 copy-start
  1.8 0.0 copy-start.1
  1.9 0.1 xpack.1
  1.9 0.1 collective-permute-start
  2.0 0.8 %collective-permute-start.1 = (f32[5,64,256]{2,1,0:T(8,128)S(1)}, f32[5,64,256]{2,1,0:T(8,128)S(1)}, u32[]{:S(2)}, u32[]{:S(2)}) collective-permute-start(f32[5,64,256]{2,1,0:T(8,128)S(1)} %get-tuple-element.40), channel_id=1, source_target_pairs={{8,16},{16,8},{9,17},{17,9},{10,18},{18,10},{11,19},{19,11},{12,20... | collective-permute-start | bytes 983048 | tf_op jit(solution)/shard_map/ppermute | solution.py:75
  2.8 1.2 %copy-done = f32[64,64,256]{2,1,0:T(8,128)S(1)} copy-done((f32[64,64,256]{2,1,0:T(8,128)S(1)}, f32[64,64,256]{2,1,0:T(8,128)}, u32[]{:S(2)}) %copy-start) | copy-done | bytes 4194328
  4.0 1.3 %copy-done.1 = f32[64,64,256]{2,1,0:T(8,128)S(1)} copy-done((f32[64,64,256]{2,1,0:T(8,128)S(1)}, f32[64,64,256]{2,1,0:T(8,128)}, u32[]{:S(2)}) %copy-start.1) | copy-done | bytes 4194328
  5.3 1.3 %build.1 = (f32[3,5184,128]{2,1,0:T(8,128)S(1)}, f32[3,5184,128]{2,1,0:T(8,128)S(1)}, f32[3,64,128]{2,1,0:T(8,128)S(1)}, f32[3,64,128]{2,1,0:T(8,128)S(1)}) custom-call(f32[64,64,256]{2,1,0:T(8,128)S(1)} %copy-done, f32[64,64,256]{2,1,0:T(8,128)S(1)} %copy-done.1), custom_call_target="tpu_custom_call" | custom-call | flops 100000000 | tf_op jit(solution)/shard_map/build/pallas_call | solution.py:30
  6.6 0.0 collective-permute-done.refs_0_
  6.6 0.0 collective-permute-done.1.refs_1_
  6.6 0.3 xhalo.1
  6.9 1.6 %collective-permute-start.2 = (f32[3,64,128]{2,1,0:T(8,128)S(1)}, f32[3,64,128]{2,1,0:T(8,128)S(1)}, u32[]{:S(2)}, u32[]{:S(2)}) collective-permute-start(f32[3,64,128]{2,1,0:T(8,128)S(1)} %get-tuple-element.43), channel_id=1, source_target_pairs={{0,1},{1,0},{2,3},{3,2},{4,5},{5,4},{6,7},{7,6},{8,9},{9,8},{10,11... | collective-permute-start | bytes 294920 | tf_op jit(solution)/shard_map/ppermute | solution.py:75
  8.5 1.9 %collective-permute-start.3 = (f32[3,64,128]{2,1,0:T(8,128)S(1)}, f32[3,64,128]{2,1,0:T(8,128)S(1)}, u32[]{:S(2)}, u32[]{:S(2)}) collective-permute-start(f32[3,64,128]{2,1,0:T(8,128)S(1)} %get-tuple-element.44), channel_id=1, source_target_pairs={{1,2},{2,1},{5,6},{6,5},{9,10},{10,9},{13,14},{14,13},{17,18},{18,... | collective-permute-start | bytes 294920 | tf_op jit(solution)/shard_map/ppermute | solution.py:75
  10.4 0.2 middle.1
  10.6 0.9 %collective-permute-done.2.refs_0_ = f32[3,64,128]{2,1,0:T(8,128)S(1)} collective-permute-done((f32[3,64,128]{2,1,0:T(8,128)S(1)}, f32[3,64,128]{2,1,0:T(8,128)S(1)}, u32[]{:S(2)}, u32[]{:S(2)}) %collective-permute-start.2) | collective-permute-done | bytes 98336 | tf_op jit(solution)/shard_map/ppermute | solution.py:75
  11.6 3.5 %collective-permute-done.3.refs_1_ = f32[3,64,128]{2,1,0:T(8,128)S(1)} collective-permute-done((f32[3,64,128]{2,1,0:T(8,128)S(1)}, f32[3,64,128]{2,1,0:T(8,128)S(1)}, u32[]{:S(2)}, u32[]{:S(2)}) %collective-permute-start.3) | collective-permute-done | bytes 98336 | tf_op jit(solution)/shard_map/ppermute | solution.py:75
  15.0 1.5 %zhalo.1 = (f32[3,5184,128]{2,1,0:T(8,128)S(1)}, f32[3,5184,128]{2,1,0:T(8,128)S(1)}, f32[11,72,128]{2,1,0:T(8,128)S(1)}) custom-call(f32[3,64,128]{2,1,0:T(8,128)S(1)} %collective-permute-done.2.refs_0_, f32[3,64,128]{2,1,0:T(8,128)S(1)} %collective-permute-done.3.refs_1_, ...), custom_call_target="tpu_custom_call", output_to_operand_aliasing={{0}: (2, {}), {1}: (3, {}), {2}: (4, {})} | custom-call | flops 100000000 | tf_op jit(solution)/shard_map/zhalo/pallas_call | solution.py:30
  16.5 1.6 %collective-permute-start.4 = (f32[11,72,128]{2,1,0:T(8,128)S(1)}, f32[11,72,128]{2,1,0:T(8,128)S(1)}, u32[]{:S(2)}, u32[]{:S(2)}) collective-permute-start(f32[11,72,128]{2,1,0:T(8,128)S(1)} %get-tuple-element.50), channel_id=1, source_target_pairs={{0,4},{4,0},{1,5},{5,1},{2,6},{6,2},{3,7},{7,3},{8,12},{12,8},{9,1... | collective-permute-start | bytes 1216520 | tf_op jit(solution)/shard_map/ppermute | solution.py:75
  18.1 9.5 %inner.1 = (f32[3,5184,128]{2,1,0:T(8,128)S(1)}, f32[3,5184,128]{2,1,0:T(8,128)S(1)}, f32[2,2120,128]{2,1,0:T(8,128)S(1)}) custom-call(f32[3,5184,128]{2,1,0:T(8,128)S(1)} %get-tuple-element.51.se.refs_1_, f32[3,5184,128]{2,1,0:T(8,128)S(1)} %get-tuple-element.52.re.refs_2_), custom_call_target="tpu_custom_call" | custom-call | flops 8999999488 | tf_op jit(solution)/shard_map/inner/pallas_call | solution.py:30
  27.6 0.0 collective-permute-done.4.refs_0_
  27.7 3.0 %outer.1 = (f32[3,5184,128]{2,1,0:T(8,128)S(1)}, f32[3,5184,128]{2,1,0:T(8,128)S(1)}, f32[3,5184,128]{2,1,0:T(8,128)S(1)}, f32[3,5184,128]{2,1,0:T(8,128)S(1)}, ...) custom-call(f32[11,72,128]{2,1,0:T(8,128)S(1)} %collective-permute-d, ...), custom_call_target="tpu_custom_call", output_to_operand_aliasing={{0}: (1, {}), {1}: (2, {}), {2}: (3, {}), {3}: (4, {}), {4}... | custom-call | flops 100000000 | tf_op jit(solution)/shard_map/outer/pallas_call | solution.py:30
  30.7 0.1 collective-permute-start.5
  30.7 3.3 %collective-permute-start.6 = (f32[5,40,128]{2,1,0:T(8,128)S(1)}, f32[5,40,128]{2,1,0:T(8,128)S(1)}, u32[]{:S(2)}, u32[]{:S(2)}) collective-permute-start(f32[5,40,128]{2,1,0:T(8,128)S(1)} %get-tuple-element.57), channel_id=1, source_target_pairs={{0,8},{8,16},{16,24},{24,0},{1,9},{9,17},{17,25},{25,1},{2,10},{10... | collective-permute-start | bytes 307208 | tf_op jit(solution)/shard_map/ppermute | solution.py:68
  34.0 0.9 %rest.1 = (f32[2,2120,128]{2,1,0:T(8,128)S(1)}, f32[2,1600,128]{2,1,0:T(8,128)S(1)}) custom-call(f32[2,2120,128]{2,1,0:T(8,128)S(1)} %get-tuple-element.58.rx, f32[2,1600,128]{2,1,0:T(8,128)S(1)} %get-tuple-element.59._), custom_call_target="tpu_custom_call", output_to_operand_aliasing={{0}: (0, {}), {1}: (1, {})} | custom-call | flops 2000000000 | tf_op jit(solution)/shard_map/rest/pallas_call | solution.py:30
  34.9 0.0 collective-permute-done.5.refs_0_
  34.9 4.7 %collective-permute-done.6.refs_1_ = f32[5,40,128]{2,1,0:T(8,128)S(1)} collective-permute-done((f32[5,40,128]{2,1,0:T(8,128)S(1)}, f32[5,40,128]{2,1,0:T(8,128)S(1)}, u32[]{:S(2)}, u32[]{:S(2)}) %collective-permute-start.6) | collective-permute-done | bytes 102432 | tf_op jit(solution)/shard_map/ppermute | solution.py:68
  39.6 0.5 coarse_x.1
  40.2 0.1 collective-permute-start.7
  40.2 2.1 %collective-permute-start.8 = (f32[2,40,128]{2,1,0:T(8,128)S(1)}, f32[2,40,128]{2,1,0:T(8,128)S(1)}, u32[]{:S(2)}, u32[]{:S(2)}) collective-permute-start(f32[2,40,128]{2,1,0:T(8,128)S(1)} %get-tuple-element.62), channel_id=1, source_target_pairs={{1,2},{2,1},{5,6},{6,5},{9,10},{10,9},{13,14},{14,13},{17,18},{18,... | collective-permute-start | bytes 122888 | tf_op jit(solution)/shard_map/ppermute | solution.py:75
  42.3 1.9 %collective-permute-done.7.refs_0_ = f32[2,40,128]{2,1,0:T(8,128)S(1)} collective-permute-done((f32[2,40,128]{2,1,0:T(8,128)S(1)}, f32[2,40,128]{2,1,0:T(8,128)S(1)}, u32[]{:S(2)}, u32[]{:S(2)}) %collective-permute-start.7) | collective-permute-done | bytes 40992 | tf_op jit(solution)/shard_map/ppermute | solution.py:75
  44.2 1.9 %collective-permute-done.8.refs_1_ = f32[2,40,128]{2,1,0:T(8,128)S(1)} collective-permute-done((f32[2,40,128]{2,1,0:T(8,128)S(1)}, f32[2,40,128]{2,1,0:T(8,128)S(1)}, u32[]{:S(2)}, u32[]{:S(2)}) %collective-permute-start.8) | collective-permute-done | bytes 40992 | tf_op jit(solution)/shard_map/ppermute | solution.py:75
  46.1 0.6 %coarse_z.1 = (f32[2,1600,128]{2,1,0:T(8,128)S(1)}, f32[5,40,128]{2,1,0:T(8,128)S(1)}) custom-call(f32[2,40,128]{2,1,0:T(8,128)S(1)} %collective-permute-done.7.refs_0_, f32[2,40,128]{2,1,0:T(8,128)S(1)} %collective-permute-done.8.refs_1_, f32[2,1600,128]{2,1,0:T(8,128)S(1)} %get-tuple-element.63.refs_2_), custom_call_target="tpu_custom_call", output_to_operand_aliasing={{0}: (2, {})} | custom-call | flops 100000000 | tf_op jit(solution)/shard_map/coarse_z/pallas_call | solution.py:30
  46.7 0.6 %collective-permute-start.9 = (f32[5,40,128]{2,1,0:T(8,128)S(1)}, f32[5,40,128]{2,1,0:T(8,128)S(1)}, u32[]{:S(2)}, u32[]{:S(2)}) collective-permute-start(f32[5,40,128]{2,1,0:T(8,128)S(1)} %get-tuple-element.64), channel_id=1, source_target_pairs={{0,4},{4,0},{1,5},{5,1},{2,6},{6,2},{3,7},{7,3},{8,12},{12,8},{9,1... | collective-permute-start | bytes 307208 | tf_op jit(solution)/shard_map/ppermute | solution.py:75
  47.3 4.4 %finish_inner.1 = (f32[2,1600,128]{2,1,0:T(8,128)S(1)}, f32[2,1600,128]{2,1,0:T(8,128)S(1)}, f32[2,1600,128]{2,1,0:T(8,128)S(1)}, f32[2,1600,128]{2,1,0:T(8,128)S(1)}, f32[64,64,256]{2,1,0:T(8,128)}) custom-call(f32[3,5184,128]{2,1,0:T(8,128)S(1)} %get-tuple-element.65.smooth.refs_1_, f32[2,1600,128]{2,1,0:T(8,128)S(1)} %get-tuple-element.66.coarse.refs_2_), custom_call_target="tpu_custom_call" | custom-call | flops 5000000000 | tf_op jit(solution)/shard_map/finish_inner/pallas_call | solution.py:30
  51.7 0.0 collective-permute-done.9.refs_0_
  51.7 2.7 %finish_outer.1 = (f32[2,1600,128]{2,1,0:T(8,128)S(1)}, f32[2,1600,128]{2,1,0:T(8,128)S(1)}, f32[2,1600,128]{2,1,0:T(8,128)S(1)}, f32[2,1600,128]{2,1,0:T(8,128)...) custom-call(f32[5,40,128]{2,1,0:T(8,128)S(1)} %collective-permute-do, ...), custom_call_target="tpu_custom_call", output_to_operand_aliasing={{0}: (2, {}), {1}: (3, {}), {2}: (4, {}), {3}: (5, {}), {4}... | custom-call | flops 100000000 | tf_op jit(solution)/shard_map/finish_outer/pallas_call | solution.py:30
  (2 shorter events, 0.0 us)
Async XLA Ops:
  1.8 2.2 %copy-start = (f32[64,64,256]{2,1,0:T(8,128)S(1)}, f32[64,64,256]{2,1,0:T(8,128)}, u32[]{:S(2)}) copy-start(f32[64,64,256]{2,1,0:T(8,128)} %start.1) | copy-start | bytes 12582916
  1.8 3.5 %copy-start.1 = (f32[64,64,256]{2,1,0:T(8,128)S(1)}, f32[64,64,256]{2,1,0:T(8,128)}, u32[]{:S(2)}) copy-start(f32[64,64,256]{2,1,0:T(8,128)} %right.1) | copy-start | bytes 12582916
  1.9 4.7 %collective-permute-start = (f32[5,64,256]{2,1,0:T(8,128)S(1)}, f32[5,64,256]{2,1,0:T(8,128)S(1)}, u32[]{:S(2)}, u32[]{:S(2)}) collective-permute-start(f32[5,64,256]{2,1,0:T(8,128)S(1)} %get-tuple-element.39), channel_id=1, source_target_pairs={{0,8},{8,0},{16,24},{24,16},{1,9},{9,1},{17,25},{25,17},{2,10},{10... | collective-permute-start | bytes 983048 | tf_op jit(solution)/shard_map/ppermute | solution.py:75
  2.0 4.6 %collective-permute-start.1 = (f32[5,64,256]{2,1,0:T(8,128)S(1)}, f32[5,64,256]{2,1,0:T(8,128)S(1)}, u32[]{:S(2)}, u32[]{:S(2)}) collective-permute-start(f32[5,64,256]{2,1,0:T(8,128)S(1)} %get-tuple-element.40), channel_id=1, source_target_pairs={{8,16},{16,8},{9,17},{17,9},{10,18},{18,10},{11,19},{19,11},{12,20... | collective-permute-start | bytes 983048 | tf_op jit(solution)/shard_map/ppermute | solution.py:75
  6.9 4.7 %collective-permute-start.2 = (f32[3,64,128]{2,1,0:T(8,128)S(1)}, f32[3,64,128]{2,1,0:T(8,128)S(1)}, u32[]{:S(2)}, u32[]{:S(2)}) collective-permute-start(f32[3,64,128]{2,1,0:T(8,128)S(1)} %get-tuple-element.43), channel_id=1, source_target_pairs={{0,1},{1,0},{2,3},{3,2},{4,5},{5,4},{6,7},{7,6},{8,9},{9,8},{10,11... | collective-permute-start | bytes 294920 | tf_op jit(solution)/shard_map/ppermute | solution.py:75
  8.5 6.5 %collective-permute-start.3 = (f32[3,64,128]{2,1,0:T(8,128)S(1)}, f32[3,64,128]{2,1,0:T(8,128)S(1)}, u32[]{:S(2)}, u32[]{:S(2)}) collective-permute-start(f32[3,64,128]{2,1,0:T(8,128)S(1)} %get-tuple-element.44), channel_id=1, source_target_pairs={{1,2},{2,1},{5,6},{6,5},{9,10},{10,9},{13,14},{14,13},{17,18},{18,... | collective-permute-start | bytes 294920 | tf_op jit(solution)/shard_map/ppermute | solution.py:75
  16.5 11.1 %collective-permute-start.4 = (f32[11,72,128]{2,1,0:T(8,128)S(1)}, f32[11,72,128]{2,1,0:T(8,128)S(1)}, u32[]{:S(2)}, u32[]{:S(2)}) collective-permute-start(f32[11,72,128]{2,1,0:T(8,128)S(1)} %get-tuple-element.50), channel_id=1, source_target_pairs={{0,4},{4,0},{1,5},{5,1},{2,6},{6,2},{3,7},{7,3},{8,12},{12,8},{9,1... | collective-permute-start | bytes 1216520 | tf_op jit(solution)/shard_map/ppermute | solution.py:75
  30.7 4.3 %collective-permute-start.5 = (f32[5,40,128]{2,1,0:T(8,128)S(1)}, f32[5,40,128]{2,1,0:T(8,128)S(1)}, u32[]{:S(2)}, u32[]{:S(2)}) collective-permute-start(f32[5,40,128]{2,1,0:T(8,128)S(1)} %get-tuple-element.56), channel_id=1, source_target_pairs={{0,24},{8,0},{16,8},{24,16},{1,25},{9,1},{17,9},{25,17},{2,26},{10... | collective-permute-start | bytes 307208 | tf_op jit(solution)/shard_map/ppermute | solution.py:67
  30.7 8.9 %collective-permute-start.6 = (f32[5,40,128]{2,1,0:T(8,128)S(1)}, f32[5,40,128]{2,1,0:T(8,128)S(1)}, u32[]{:S(2)}, u32[]{:S(2)}) collective-permute-start(f32[5,40,128]{2,1,0:T(8,128)S(1)} %get-tuple-element.57), channel_id=1, source_target_pairs={{0,8},{8,16},{16,24},{24,0},{1,9},{9,17},{17,25},{25,1},{2,10},{10... | collective-permute-start | bytes 307208 | tf_op jit(solution)/shard_map/ppermute | solution.py:68
  40.2 4.1 %collective-permute-start.7 = (f32[2,40,128]{2,1,0:T(8,128)S(1)}, f32[2,40,128]{2,1,0:T(8,128)S(1)}, u32[]{:S(2)}, u32[]{:S(2)}) collective-permute-start(f32[2,40,128]{2,1,0:T(8,128)S(1)} %get-tuple-element.61), channel_id=1, source_target_pairs={{0,1},{1,0},{2,3},{3,2},{4,5},{5,4},{6,7},{7,6},{8,9},{9,8},{10,11... | collective-permute-start | bytes 122888 | tf_op jit(solution)/shard_map/ppermute | solution.py:75
  40.2 5.9 %collective-permute-start.8 = (f32[2,40,128]{2,1,0:T(8,128)S(1)}, f32[2,40,128]{2,1,0:T(8,128)S(1)}, u32[]{:S(2)}, u32[]{:S(2)}) collective-permute-start(f32[2,40,128]{2,1,0:T(8,128)S(1)} %get-tuple-element.62), channel_id=1, source_target_pairs={{1,2},{2,1},{5,6},{6,5},{9,10},{10,9},{13,14},{14,13},{17,18},{18,... | collective-permute-start | bytes 122888 | tf_op jit(solution)/shard_map/ppermute | solution.py:75
  46.7 5.0 %collective-permute-start.9 = (f32[5,40,128]{2,1,0:T(8,128)S(1)}, f32[5,40,128]{2,1,0:T(8,128)S(1)}, u32[]{:S(2)}, u32[]{:S(2)}) collective-permute-start(f32[5,40,128]{2,1,0:T(8,128)S(1)} %get-tuple-element.64), channel_id=1, source_target_pairs={{0,4},{4,0},{1,5},{5,1},{2,6},{6,2},{3,7},{7,3},{8,12},{12,8},{9,1... | collective-permute-start | bytes 307208 | tf_op jit(solution)/shard_map/ppermute | solution.py:75

commit v6 on v5

--- a/solution.py
+++ b/solution.py
@@ -183,7 +183,7 @@
             pack(outs, at, group, planes, load, (zero, zero))
         return 0
 
-    loop(ny // 8, rows)
+    loop(ny // 8, rows, 8)
 
 
 def xhalo_body(nx, ny, nz, nin, *refs):
@@ -228,7 +228,7 @@
             emit(outs, (group, pl.ds(at, 8)), "gz", lambda: core_low, lambda: core_high)
         return 0
 
-    loop(ny // 8, rows)
+    loop(ny // 8, rows, 8)
 
 
 class Kept:
@@ -282,7 +282,7 @@
                 re[nt, here, :] = jnp.where(lane < 64, a, b)
         return 0
 
-    loop(ny // 8, unpack)
+    loop(ny // 8, unpack, 8)
     lane = iota((xe, LANES), 1)
     extra_low = extra_high = jnp.zeros((xe, LANES), jnp.float32)
     for k in range(SLOT):

time: 54.8 us -> 54.6 us (level)
  no operation moved by 1% of the time
where the time goes in v6:
time: 54.6 us; the launch traced here: 54.4 us
  Pallas kernels  24.7 us (45%)
  waiting for transfers between devices  13 us (24%)
  starting transfers between devices  12.1 us (22%)
  local copies, waits for them, and re-layouts  2.49 us (5%)
  other arithmetic  1.82 us (3%)
    pallas_call x12, Pallas kernels, call(): pl.pallas_call(body, name=name, in_specs=[VMEM] * len(ins) if in_specs is...  24.7 us
    ppermute x8, starting transfers between devices, exchange(): found[phase] = lax.ppermute(msgs[phase], axis, routes)  8.76 us
    ppermute x8, waiting for transfers between devices, exchange(): found[phase] = lax.ppermute(msgs[phase], axis, routes)  8.2 us
    ppermute x1, waiting for transfers between devices, exchange(): up = lax.ppermute(msgs[1], axis, [(i, (i + 1) % n) for i in range(n)])  4.78 us
    ppermute x1, starting transfers between devices, exchange(): up = lax.ppermute(msgs[1], axis, [(i, (i + 1) % n) for i in range(n)])  3.32 us
    unnamed x4, local copies, waits for them, and re-layouts  2.49 us
    select_n x1, other arithmetic, joined_faces(): jnp.where(i < F, a, jnp.where(i < SLOT, b, jnp.where(i < SLOT + F, c, d)))  1.81 us
  transfers between devices with their start and end apart: 10, of which 5 were waited for; matrix products, arithmetic and copies ran while one was open for 0% of the time, Pallas kernels for 30%

profile of v6, /device:TPU:16, one launch (start us, length us, event | category | flops | bytes accessed | tf_op | source)
XLA Modules:
  0.0 54.4 jit_solution(8987261644999383584)
XLA Ops:
  0.0 1.8 %fusion.2.refs_0_ = f32[10,64,256]{2,1,0:T(8,128)S(1)} fusion(f32[64,64,256]{2,1,0:T(8,128)} %start.1, f32[64,64,256]{2,1,0:T(8,128)} %right.1, pred[10]{0:T(512)(128)(4,1)S(1)} %get-tuple-element.73, pred[10]{0:T(512)(128)(4,1)S(1)} %get-tuple-element.74, pred[10]{0:T(512)(128)(4,1)S(1)} %iota_compare_fusion.2), kind=kLoop, calls=%fused_computation.4 | loop fusion | flops 491520 | bytes 10354718 | tf_op jit(solution)/shard_map/jit(_where)/select_n | solution.py:743
  1.8 0.0 copy-start
  1.8 0.0 copy-start.1
  1.9 0.1 xpack.1
  1.9 0.1 collective-permute-start
  2.0 0.8 %collective-permute-start.1 = (f32[5,64,256]{2,1,0:T(8,128)S(1)}, f32[5,64,256]{2,1,0:T(8,128)S(1)}, u32[]{:S(2)}, u32[]{:S(2)}) collective-permute-start(f32[5,64,256]{2,1,0:T(8,128)S(1)} %get-tuple-element.40), channel_id=1, source_target_pairs={{8,16},{16,8},{9,17},{17,9},{10,18},{18,10},{11,19},{19,11},{12,20... | collective-permute-start | bytes 983048 | tf_op jit(solution)/shard_map/ppermute | solution.py:75
  2.8 1.2 %copy-done = f32[64,64,256]{2,1,0:T(8,128)S(1)} copy-done((f32[64,64,256]{2,1,0:T(8,128)S(1)}, f32[64,64,256]{2,1,0:T(8,128)}, u32[]{:S(2)}) %copy-start) | copy-done | bytes 4194328
  4.0 1.3 %copy-done.1 = f32[64,64,256]{2,1,0:T(8,128)S(1)} copy-done((f32[64,64,256]{2,1,0:T(8,128)S(1)}, f32[64,64,256]{2,1,0:T(8,128)}, u32[]{:S(2)}) %copy-start.1) | copy-done | bytes 4194328
  5.3 1.2 %build.1 = (f32[3,5184,128]{2,1,0:T(8,128)S(1)}, f32[3,5184,128]{2,1,0:T(8,128)S(1)}, f32[3,64,128]{2,1,0:T(8,128)S(1)}, f32[3,64,128]{2,1,0:T(8,128)S(1)}) custom-call(f32[64,64,256]{2,1,0:T(8,128)S(1)} %copy-done, f32[64,64,256]{2,1,0:T(8,128)S(1)} %copy-done.1), custom_call_target="tpu_custom_call" | custom-call | flops 100000000 | tf_op jit(solution)/shard_map/build/pallas_call | solution.py:30
  6.5 0.0 collective-permute-done.refs_0_
  6.5 0.0 collective-permute-done.1.refs_1_
  6.5 0.2 xhalo.1
  6.7 1.6 %collective-permute-start.2 = (f32[3,64,128]{2,1,0:T(8,128)S(1)}, f32[3,64,128]{2,1,0:T(8,128)S(1)}, u32[]{:S(2)}, u32[]{:S(2)}) collective-permute-start(f32[3,64,128]{2,1,0:T(8,128)S(1)} %get-tuple-element.43), channel_id=1, source_target_pairs={{0,1},{1,0},{2,3},{3,2},{4,5},{5,4},{6,7},{7,6},{8,9},{9,8},{10,11... | collective-permute-start | bytes 294920 | tf_op jit(solution)/shard_map/ppermute | solution.py:75
  8.3 1.9 %collective-permute-start.3 = (f32[3,64,128]{2,1,0:T(8,128)S(1)}, f32[3,64,128]{2,1,0:T(8,128)S(1)}, u32[]{:S(2)}, u32[]{:S(2)}) collective-permute-start(f32[3,64,128]{2,1,0:T(8,128)S(1)} %get-tuple-element.44), channel_id=1, source_target_pairs={{1,2},{2,1},{5,6},{6,5},{9,10},{10,9},{13,14},{14,13},{17,18},{18,... | collective-permute-start | bytes 294920 | tf_op jit(solution)/shard_map/ppermute | solution.py:75
  10.2 0.2 middle.1
  10.4 0.9 %collective-permute-done.2.refs_0_ = f32[3,64,128]{2,1,0:T(8,128)S(1)} collective-permute-done((f32[3,64,128]{2,1,0:T(8,128)S(1)}, f32[3,64,128]{2,1,0:T(8,128)S(1)}, u32[]{:S(2)}, u32[]{:S(2)}) %collective-permute-start.2) | collective-permute-done | bytes 98336 | tf_op jit(solution)/shard_map/ppermute | solution.py:75
  11.4 3.5 %collective-permute-done.3.refs_1_ = f32[3,64,128]{2,1,0:T(8,128)S(1)} collective-permute-done((f32[3,64,128]{2,1,0:T(8,128)S(1)}, f32[3,64,128]{2,1,0:T(8,128)S(1)}, u32[]{:S(2)}, u32[]{:S(2)}) %collective-permute-start.3) | collective-permute-done | bytes 98336 | tf_op jit(solution)/shard_map/ppermute | solution.py:75
  14.8 1.4 %zhalo.1 = (f32[3,5184,128]{2,1,0:T(8,128)S(1)}, f32[3,5184,128]{2,1,0:T(8,128)S(1)}, f32[11,72,128]{2,1,0:T(8,128)S(1)}) custom-call(f32[3,64,128]{2,1,0:T(8,128)S(1)} %collective-permute-done.2.refs_0_, f32[3,64,128]{2,1,0:T(8,128)S(1)} %collective-permute-done.3.refs_1_, ...), custom_call_target="tpu_custom_call", output_to_operand_aliasing={{0}: (2, {}), {1}: (3, {}), {2}: (4, {})} | custom-call | flops 100000000 | tf_op jit(solution)/shard_map/zhalo/pallas_call | solution.py:30
  16.3 1.6 %collective-permute-start.4 = (f32[11,72,128]{2,1,0:T(8,128)S(1)}, f32[11,72,128]{2,1,0:T(8,128)S(1)}, u32[]{:S(2)}, u32[]{:S(2)}) collective-permute-start(f32[11,72,128]{2,1,0:T(8,128)S(1)} %get-tuple-element.50), channel_id=1, source_target_pairs={{0,4},{4,0},{1,5},{5,1},{2,6},{6,2},{3,7},{7,3},{8,12},{12,8},{9,1... | collective-permute-start | bytes 1216520 | tf_op jit(solution)/shard_map/ppermute | solution.py:75
  17.8 9.5 %inner.1 = (f32[3,5184,128]{2,1,0:T(8,128)S(1)}, f32[3,5184,128]{2,1,0:T(8,128)S(1)}, f32[2,2120,128]{2,1,0:T(8,128)S(1)}) custom-call(f32[3,5184,128]{2,1,0:T(8,128)S(1)} %get-tuple-element.51.se.refs_1_, f32[3,5184,128]{2,1,0:T(8,128)S(1)} %get-tuple-element.52.re.refs_2_), custom_call_target="tpu_custom_call" | custom-call | flops 8999999488 | tf_op jit(solution)/shard_map/inner/pallas_call | solution.py:30
  27.4 0.0 collective-permute-done.4.refs_0_
  27.4 3.0 %outer.1 = (f32[3,5184,128]{2,1,0:T(8,128)S(1)}, f32[3,5184,128]{2,1,0:T(8,128)S(1)}, f32[3,5184,128]{2,1,0:T(8,128)S(1)}, f32[3,5184,128]{2,1,0:T(8,128)S(1)}, ...) custom-call(f32[11,72,128]{2,1,0:T(8,128)S(1)} %collective-permute-d, ...), custom_call_target="tpu_custom_call", output_to_operand_aliasing={{0}: (1, {}), {1}: (2, {}), {2}: (3, {}), {3}: (4, {}), {4}... | custom-call | flops 100000000 | tf_op jit(solution)/shard_map/outer/pallas_call | solution.py:30
  30.4 0.1 collective-permute-start.5
  30.4 3.3 %collective-permute-start.6 = (f32[5,40,128]{2,1,0:T(8,128)S(1)}, f32[5,40,128]{2,1,0:T(8,128)S(1)}, u32[]{:S(2)}, u32[]{:S(2)}) collective-permute-start(f32[5,40,128]{2,1,0:T(8,128)S(1)} %get-tuple-element.57), channel_id=1, source_target_pairs={{0,8},{8,16},{16,24},{24,0},{1,9},{9,17},{17,25},{25,1},{2,10},{10... | collective-permute-start | bytes 307208 | tf_op jit(solution)/shard_map/ppermute | solution.py:68
  33.8 0.9 %rest.1 = (f32[2,2120,128]{2,1,0:T(8,128)S(1)}, f32[2,1600,128]{2,1,0:T(8,128)S(1)}) custom-call(f32[2,2120,128]{2,1,0:T(8,128)S(1)} %get-tuple-element.58.rx, f32[2,1600,128]{2,1,0:T(8,128)S(1)} %get-tuple-element.59._), custom_call_target="tpu_custom_call", output_to_operand_aliasing={{0}: (0, {}), {1}: (1, {})} | custom-call | flops 2000000000 | tf_op jit(solution)/shard_map/rest/pallas_call | solution.py:30
  34.7 0.0 collective-permute-done.5.refs_0_
  34.7 4.8 %collective-permute-done.6.refs_1_ = f32[5,40,128]{2,1,0:T(8,128)S(1)} collective-permute-done((f32[5,40,128]{2,1,0:T(8,128)S(1)}, f32[5,40,128]{2,1,0:T(8,128)S(1)}, u32[]{:S(2)}, u32[]{:S(2)}) %collective-permute-start.6) | collective-permute-done | bytes 102432 | tf_op jit(solution)/shard_map/ppermute | solution.py:68
  39.5 0.5 coarse_x.1
  40.0 0.1 collective-permute-start.7
  40.1 2.1 %collective-permute-start.8 = (f32[2,40,128]{2,1,0:T(8,128)S(1)}, f32[2,40,128]{2,1,0:T(8,128)S(1)}, u32[]{:S(2)}, u32[]{:S(2)}) collective-permute-start(f32[2,40,128]{2,1,0:T(8,128)S(1)} %get-tuple-element.62), channel_id=1, source_target_pairs={{1,2},{2,1},{5,6},{6,5},{9,10},{10,9},{13,14},{14,13},{17,18},{18,... | collective-permute-start | bytes 122888 | tf_op jit(solution)/shard_map/ppermute | solution.py:75
  42.2 1.9 %collective-permute-done.7.refs_0_ = f32[2,40,128]{2,1,0:T(8,128)S(1)} collective-permute-done((f32[2,40,128]{2,1,0:T(8,128)S(1)}, f32[2,40,128]{2,1,0:T(8,128)S(1)}, u32[]{:S(2)}, u32[]{:S(2)}) %collective-permute-start.7) | collective-permute-done | bytes 40992 | tf_op jit(solution)/shard_map/ppermute | solution.py:75
  44.1 1.9 %collective-permute-done.8.refs_1_ = f32[2,40,128]{2,1,0:T(8,128)S(1)} collective-permute-done((f32[2,40,128]{2,1,0:T(8,128)S(1)}, f32[2,40,128]{2,1,0:T(8,128)S(1)}, u32[]{:S(2)}, u32[]{:S(2)}) %collective-permute-start.8) | collective-permute-done | bytes 40992 | tf_op jit(solution)/shard_map/ppermute | solution.py:75
  46.0 0.6 %coarse_z.1 = (f32[2,1600,128]{2,1,0:T(8,128)S(1)}, f32[5,40,128]{2,1,0:T(8,128)S(1)}) custom-call(f32[2,40,128]{2,1,0:T(8,128)S(1)} %collective-permute-done.7.refs_0_, f32[2,40,128]{2,1,0:T(8,128)S(1)} %collective-permute-done.8.refs_1_, f32[2,1600,128]{2,1,0:T(8,128)S(1)} %get-tuple-element.63.refs_2_), custom_call_target="tpu_custom_call", output_to_operand_aliasing={{0}: (2, {})} | custom-call | flops 100000000 | tf_op jit(solution)/shard_map/coarse_z/pallas_call | solution.py:30
  46.6 0.6 %collective-permute-start.9 = (f32[5,40,128]{2,1,0:T(8,128)S(1)}, f32[5,40,128]{2,1,0:T(8,128)S(1)}, u32[]{:S(2)}, u32[]{:S(2)}) collective-permute-start(f32[5,40,128]{2,1,0:T(8,128)S(1)} %get-tuple-element.64), channel_id=1, source_target_pairs={{0,4},{4,0},{1,5},{5,1},{2,6},{6,2},{3,7},{7,3},{8,12},{12,8},{9,1... | collective-permute-start | bytes 307208 | tf_op jit(solution)/shard_map/ppermute | solution.py:75
  47.1 4.4 %finish_inner.1 = (f32[2,1600,128]{2,1,0:T(8,128)S(1)}, f32[2,1600,128]{2,1,0:T(8,128)S(1)}, f32[2,1600,128]{2,1,0:T(8,128)S(1)}, f32[2,1600,128]{2,1,0:T(8,128)S(1)}, f32[64,64,256]{2,1,0:T(8,128)}) custom-call(f32[3,5184,128]{2,1,0:T(8,128)S(1)} %get-tuple-element.65.smooth.refs_1_, f32[2,1600,128]{2,1,0:T(8,128)S(1)} %get-tuple-element.66.coarse.refs_2_), custom_call_target="tpu_custom_call" | custom-call | flops 5000000000 | tf_op jit(solution)/shard_map/finish_inner/pallas_call | solution.py:30
  51.5 0.0 collective-permute-done.9.refs_0_
  51.6 2.7 %finish_outer.1 = (f32[2,1600,128]{2,1,0:T(8,128)S(1)}, f32[2,1600,128]{2,1,0:T(8,128)S(1)}, f32[2,1600,128]{2,1,0:T(8,128)S(1)}, f32[2,1600,128]{2,1,0:T(8,128)...) custom-call(f32[5,40,128]{2,1,0:T(8,128)S(1)} %collective-permute-do, ...), custom_call_target="tpu_custom_call", output_to_operand_aliasing={{0}: (2, {}), {1}: (3, {}), {2}: (4, {}), {3}: (5, {}), {4}... | custom-call | flops 100000000 | tf_op jit(solution)/shard_map/finish_outer/pallas_call | solution.py:30
  (2 shorter events, 0.0 us)
Async XLA Ops:
  1.8 2.2 %copy-start = (f32[64,64,256]{2,1,0:T(8,128)S(1)}, f32[64,64,256]{2,1,0:T(8,128)}, u32[]{:S(2)}) copy-start(f32[64,64,256]{2,1,0:T(8,128)} %start.1) | copy-start | bytes 12582916
  1.8 3.5 %copy-start.1 = (f32[64,64,256]{2,1,0:T(8,128)S(1)}, f32[64,64,256]{2,1,0:T(8,128)}, u32[]{:S(2)}) copy-start(f32[64,64,256]{2,1,0:T(8,128)} %right.1) | copy-start | bytes 12582916
  1.9 4.5 %collective-permute-start = (f32[5,64,256]{2,1,0:T(8,128)S(1)}, f32[5,64,256]{2,1,0:T(8,128)S(1)}, u32[]{:S(2)}, u32[]{:S(2)}) collective-permute-start(f32[5,64,256]{2,1,0:T(8,128)S(1)} %get-tuple-element.39), channel_id=1, source_target_pairs={{0,8},{8,0},{16,24},{24,16},{1,9},{9,1},{17,25},{25,17},{2,10},{10... | collective-permute-start | bytes 983048 | tf_op jit(solution)/shard_map/ppermute | solution.py:75
  2.0 4.5 %collective-permute-start.1 = (f32[5,64,256]{2,1,0:T(8,128)S(1)}, f32[5,64,256]{2,1,0:T(8,128)S(1)}, u32[]{:S(2)}, u32[]{:S(2)}) collective-permute-start(f32[5,64,256]{2,1,0:T(8,128)S(1)} %get-tuple-element.40), channel_id=1, source_target_pairs={{8,16},{16,8},{9,17},{17,9},{10,18},{18,10},{11,19},{19,11},{12,20... | collective-permute-start | bytes 983048 | tf_op jit(solution)/shard_map/ppermute | solution.py:75
  6.7 4.7 %collective-permute-start.2 = (f32[3,64,128]{2,1,0:T(8,128)S(1)}, f32[3,64,128]{2,1,0:T(8,128)S(1)}, u32[]{:S(2)}, u32[]{:S(2)}) collective-permute-start(f32[3,64,128]{2,1,0:T(8,128)S(1)} %get-tuple-element.43), channel_id=1, source_target_pairs={{0,1},{1,0},{2,3},{3,2},{4,5},{5,4},{6,7},{7,6},{8,9},{9,8},{10,11... | collective-permute-start | bytes 294920 | tf_op jit(solution)/shard_map/ppermute | solution.py:75
  8.3 6.5 %collective-permute-start.3 = (f32[3,64,128]{2,1,0:T(8,128)S(1)}, f32[3,64,128]{2,1,0:T(8,128)S(1)}, u32[]{:S(2)}, u32[]{:S(2)}) collective-permute-start(f32[3,64,128]{2,1,0:T(8,128)S(1)} %get-tuple-element.44), channel_id=1, source_target_pairs={{1,2},{2,1},{5,6},{6,5},{9,10},{10,9},{13,14},{14,13},{17,18},{18,... | collective-permute-start | bytes 294920 | tf_op jit(solution)/shard_map/ppermute | solution.py:75
  16.3 11.1 %collective-permute-start.4 = (f32[11,72,128]{2,1,0:T(8,128)S(1)}, f32[11,72,128]{2,1,0:T(8,128)S(1)}, u32[]{:S(2)}, u32[]{:S(2)}) collective-permute-start(f32[11,72,128]{2,1,0:T(8,128)S(1)} %get-tuple-element.50), channel_id=1, source_target_pairs={{0,4},{4,0},{1,5},{5,1},{2,6},{6,2},{3,7},{7,3},{8,12},{12,8},{9,1... | collective-permute-start | bytes 1216520 | tf_op jit(solution)/shard_map/ppermute | solution.py:75
  30.4 4.3 %collective-permute-start.5 = (f32[5,40,128]{2,1,0:T(8,128)S(1)}, f32[5,40,128]{2,1,0:T(8,128)S(1)}, u32[]{:S(2)}, u32[]{:S(2)}) collective-permute-start(f32[5,40,128]{2,1,0:T(8,128)S(1)} %get-tuple-element.56), channel_id=1, source_target_pairs={{0,24},{8,0},{16,8},{24,16},{1,25},{9,1},{17,9},{25,17},{2,26},{10... | collective-permute-start | bytes 307208 | tf_op jit(solution)/shard_map/ppermute | solution.py:67
  30.4 9.0 %collective-permute-start.6 = (f32[5,40,128]{2,1,0:T(8,128)S(1)}, f32[5,40,128]{2,1,0:T(8,128)S(1)}, u32[]{:S(2)}, u32[]{:S(2)}) collective-permute-start(f32[5,40,128]{2,1,0:T(8,128)S(1)} %get-tuple-element.57), channel_id=1, source_target_pairs={{0,8},{8,16},{16,24},{24,0},{1,9},{9,17},{17,25},{25,1},{2,10},{10... | collective-permute-start | bytes 307208 | tf_op jit(solution)/shard_map/ppermute | solution.py:68
  40.0 4.1 %collective-permute-start.7 = (f32[2,40,128]{2,1,0:T(8,128)S(1)}, f32[2,40,128]{2,1,0:T(8,128)S(1)}, u32[]{:S(2)}, u32[]{:S(2)}) collective-permute-start(f32[2,40,128]{2,1,0:T(8,128)S(1)} %get-tuple-element.61), channel_id=1, source_target_pairs={{0,1},{1,0},{2,3},{3,2},{4,5},{5,4},{6,7},{7,6},{8,9},{9,8},{10,11... | collective-permute-start | bytes 122888 | tf_op jit(solution)/shard_map/ppermute | solution.py:75
  40.1 5.9 %collective-permute-start.8 = (f32[2,40,128]{2,1,0:T(8,128)S(1)}, f32[2,40,128]{2,1,0:T(8,128)S(1)}, u32[]{:S(2)}, u32[]{:S(2)}) collective-permute-start(f32[2,40,128]{2,1,0:T(8,128)S(1)} %get-tuple-element.62), channel_id=1, source_target_pairs={{1,2},{2,1},{5,6},{6,5},{9,10},{10,9},{13,14},{14,13},{17,18},{18,... | collective-permute-start | bytes 122888 | tf_op jit(solution)/shard_map/ppermute | solution.py:75
  46.6 5.0 %collective-permute-start.9 = (f32[5,40,128]{2,1,0:T(8,128)S(1)}, f32[5,40,128]{2,1,0:T(8,128)S(1)}, u32[]{:S(2)}, u32[]{:S(2)}) collective-permute-start(f32[5,40,128]{2,1,0:T(8,128)S(1)} %get-tuple-element.64), channel_id=1, source_target_pairs={{0,4},{4,0},{1,5},{5,1},{2,6},{6,2},{3,7},{7,3},{8,12},{12,8},{9,1... | collective-permute-start | bytes 307208 | tf_op jit(solution)/shard_map/ppermute | solution.py:75
